TPU v7x, 32 devices: a whole 2x2x4 slice. The times are simulated.
32 devices in a mesh: ctx: 4 (over x, core), seq: 2 (over y), tp: 4 (over z).
Axes of the slice: x: 2, y: 2, z: 4, core: 2. Of those that a mesh axis runs over, the one named last changes fastest.
Arguments:
- tokens: bfloat16 [2, 2048, 2048], P('seq', 'ctx'), may hold values from -8 to 8
- out_grad: bfloat16 [2, 2048, 2048], P('seq', 'ctx'), may hold values from -6 to 6
- group_order: int32 [2, 8], P('seq'), may hold values from 0 to 7, each once within a row
- w_query: bfloat16 [2048, 2048], P(None, 'tp'), may hold values from -5 to 5
- w_key: bfloat16 [2048, 2048], P(None, 'tp'), may hold values from -5 to 5
- w_value: bfloat16 [2048, 2048], P(None, 'tp'), may hold values from -0.125 to 0.125
- query_gain: float32 [16, 128], P('tp'), may hold values from 0.5 to 2
- key_gain: float32 [16, 128], P('tp'), may hold values from 0.5 to 2
- w_output: bfloat16 [2048, 2048], P('tp'), may hold values from -0.125 to 0.125
- attn_gain: float32 [2048], replicated, may hold values from 0.5 to 1.5
- w_gate: bfloat16 [2048, 8192], P(None, 'tp'), may hold values from -0.125 to 0.125
- w_up: bfloat16 [2048, 8192], P(None, 'tp'), may hold values from -0.125 to 0.125
- w_down: bfloat16 [8192, 2048], P('tp'), may hold values from -0.0625 to 0.0625
- mlp_gain: float32 [2048], replicated, may hold values from 0.5 to 1.5
Outputs:
- block_out: float32 [2, 2048, 2048], P('seq', 'ctx')
- input_grad: float32 [2, 2048, 2048], P('seq', 'ctx')
- grad_query: float32 [2048, 2048], P(('ctx', 'seq'), 'tp')
- grad_key: float32 [2048, 2048], P(('ctx', 'seq'), 'tp')
- grad_value: float32 [2048, 2048], P(('ctx', 'seq'), 'tp')
- grad_query_gain: float32 [16, 128], P('tp', ('ctx', 'seq'))
- grad_key_gain: float32 [16, 128], P('tp', ('ctx', 'seq'))
- grad_output: float32 [2048, 2048], P('tp', ('ctx', 'seq'))
- grad_attn_gain: float32 [2048], P(('ctx', 'seq'))
- grad_gate: float32 [2048, 8192], P(('ctx', 'seq'), 'tp')
- grad_up: float32 [2048, 8192], P(('ctx', 'seq'), 'tp')
- grad_down: float32 [8192, 2048], P('tp', ('ctx', 'seq'))
- grad_mlp_gain: float32 [2048], P(('ctx', 'seq'))
Inputs may be any that keep to these rules, and one draw needn't show every extreme that they name: Each row of group_order names every block of the sequence once.
All inputs are finite; a program needn't handle non-finite values.
Results may differ from a plain program's by a relative error of at most 0.04.
Values may be sent and summed in bfloat16 or wider, within the bound.
A program may use at most 320 MiB of HBM per device.

v0:
```python
import jax
import jax.numpy as jnp
from jax import lax
from jax.sharding import PartitionSpec as P

norm_eps = 1e-06
rope_base = 500000.0
masked_score = -1e30


def matmul(left, right):
    return jnp.dot(left, right, preferred_element_type=jnp.float32)


def rope_tables(positions, head_dim):
    half = head_dim // 2
    rates = rope_base ** (-(jnp.arange(half, dtype=jnp.float32) * 2.0 / head_dim))
    angle = positions.astype(jnp.float32)[:, None] * rates[None, :]
    return (jnp.cos(angle), jnp.sin(angle))


def rotate(heads_in, cosine, sine):
    half = heads_in.shape[-1] // 2
    first, second = (heads_in[..., :half], heads_in[..., half:])
    cosine, sine = (cosine[:, None, :], sine[:, None, :])
    return jnp.concatenate(
        [first * cosine - second * sine, second * cosine + first * sine], axis=-1
    )


def unrotate(grads_in, cosine, sine):
    half = grads_in.shape[-1] // 2
    first, second = (grads_in[..., :half], grads_in[..., half:])
    cosine, sine = (cosine[:, None, :], sine[:, None, :])
    return jnp.concatenate(
        [first * cosine + second * sine, second * cosine - first * sine], axis=-1
    )


def key_positions(order, first_row, count, group):
    row_ids = first_row + jnp.arange(count, dtype=jnp.int32)
    slots = row_ids // group
    picks = slots[:, None] == jnp.arange(order.shape[0], dtype=jnp.int32)[None, :]
    return jnp.sum(jnp.where(picks, order[None, :], 0), axis=1) * group + row_ids % group


def gather_pair(keys, values):
    return (
        lax.all_gather(keys, "ctx", axis=0, tiled=True),
        lax.all_gather(values, "ctx", axis=0, tiled=True),
    )


def per_device(
    tokens,
    out_grad,
    group_order,
    w_query,
    w_key,
    w_value,
    query_gain,
    key_gain,
    w_output,
    attn_gain,
    w_gate,
    w_up,
    w_down,
    mlp_gain,
):
    inputs_bf = tokens[0]
    order = group_order[0]
    row_count, width = inputs_bf.shape
    heads, head_dim = query_gain.shape
    local = heads * head_dim
    group = row_count // 2
    scale = head_dim ** (-0.5)
    query_pos = key_positions(order, lax.axis_index("ctx") * row_count, row_count, group)
    cosine, sine = rope_tables(query_pos, head_dim)
    inputs = inputs_bf.astype(jnp.float32)
    query = matmul(inputs_bf, w_query)
    keyraw = matmul(inputs_bf, w_key)
    values = matmul(inputs_bf, w_value).astype(jnp.bfloat16)
    query_sq, key_sq = lax.psum(
        (jnp.sum(query * query, axis=1), jnp.sum(keyraw * keyraw, axis=1)), "tp"
    )
    query_scale = lax.rsqrt(query_sq / width + norm_eps)
    key_scale = lax.rsqrt(key_sq / width + norm_eps)
    query_norm = query * query_scale[:, None]
    key_norm = keyraw * key_scale[:, None]
    qgain = query_gain.reshape(local)
    kgain = key_gain.reshape(local)
    query_rot = rotate(
        (query_norm * qgain).reshape(row_count, heads, head_dim), cosine, sine
    ).astype(jnp.bfloat16)
    key_rot = rotate((key_norm * kgain).reshape(row_count, heads, head_dim), cosine, sine).astype(
        jnp.bfloat16
    )
    key_flat = key_rot.reshape(row_count, local)
    start_state = (
        jnp.full((heads, row_count), masked_score, jnp.float32),
        jnp.zeros((heads, row_count), jnp.float32),
        jnp.zeros((heads, row_count, head_dim), jnp.float32),
    )
    keys_in = lax.all_gather(key_flat, "ctx", axis=0, tiled=True)
    values_in = lax.all_gather(values, "ctx", axis=0, tiled=True)
    count = keys_in.shape[0]
    attend_block = 512
    keys_in = keys_in.reshape(count // attend_block, attend_block, heads, head_dim)
    values_in = values_in.reshape(count // attend_block, attend_block, heads, head_dim)
    key_pos = key_positions(order, jnp.int32(0), count, group).reshape(
        count // attend_block, attend_block
    )

    def one_block(state, item):
        peak_old, total, accum = state
        key_block, value_block, pos_block = item
        scores = (
            jnp.einsum("qhd,khd->hqk", query_rot, key_block, preferred_element_type=jnp.float32)
            * scale
        )
        mask = (pos_block[None, :] <= query_pos[:, None])[None]
        peak = jnp.maximum(peak_old, jnp.max(jnp.where(mask, scores, masked_score), axis=2))
        share = jnp.where(mask, jnp.exp(scores - peak[:, :, None]), 0.0)
        fade = jnp.exp(peak_old - peak)
        total = total * fade + jnp.sum(share, axis=2)
        accum = accum * fade[:, :, None] + jnp.einsum(
            "hqk,khd->hqd",
            share.astype(jnp.bfloat16),
            value_block,
            preferred_element_type=jnp.float32,
        )
        return ((peak, total, accum), None)

    state, unused = lax.scan(one_block, start_state, (keys_in, values_in, key_pos))
    peak, total, accum = state
    log_total = peak + jnp.log(total)
    mixed = (accum / total[:, :, None]).astype(jnp.bfloat16)
    attn_flat = mixed.transpose(1, 0, 2).reshape(row_count, local)
    proj = lax.psum(matmul(attn_flat, w_output), "tp")
    attn_scale = lax.rsqrt(jnp.mean(proj * proj, axis=1) + norm_eps)
    attn_norm = proj * attn_scale[:, None]
    resid = inputs + attn_norm * attn_gain
    hidden = resid.astype(jnp.bfloat16)
    gate = matmul(hidden, w_gate)
    up = matmul(hidden, w_up)
    sigma = jax.nn.sigmoid(gate)
    active = gate * sigma
    inner = (active * up).astype(jnp.bfloat16)
    down = lax.psum(matmul(inner, w_down), "tp")
    mlp_scale = lax.rsqrt(jnp.mean(down * down, axis=1) + norm_eps)
    mlp_norm = down * mlp_scale[:, None]
    block_out = resid + mlp_norm * mlp_gain
    upstream = out_grad[0].astype(jnp.float32)
    d_mlp_gain = jnp.sum(upstream * mlp_norm, axis=0)
    d_mnorm = upstream * mlp_gain
    d_down = (
        mlp_scale[:, None]
        * (d_mnorm - mlp_norm * jnp.mean(d_mnorm * mlp_norm, axis=1, keepdims=True))
    ).astype(jnp.bfloat16)
    grad_down = matmul(inner.T, d_down)
    d_inner = matmul(d_down, w_down.T)
    d_gate = (d_inner * up * sigma * (1.0 + gate * (1.0 - sigma))).astype(jnp.bfloat16)
    d_up = (d_inner * active).astype(jnp.bfloat16)
    grad_gate = matmul(hidden.T, d_gate)
    grad_up = matmul(hidden.T, d_up)
    d_resid = upstream + lax.psum(matmul(d_gate, w_gate.T) + matmul(d_up, w_up.T), "tp")
    d_attn_gain = jnp.sum(d_resid * attn_norm, axis=0)
    d_anorm = d_resid * attn_gain
    d_proj = (
        attn_scale[:, None]
        * (d_anorm - attn_norm * jnp.mean(d_anorm * attn_norm, axis=1, keepdims=True))
    ).astype(jnp.bfloat16)
    grad_output = matmul(attn_flat.T, d_proj)
    d_attn = matmul(d_proj, w_output.T).astype(jnp.bfloat16)
    d_attn_heads = d_attn.reshape(row_count, heads, head_dim)
    delta = jnp.sum(
        d_attn_heads.transpose(1, 0, 2).astype(jnp.float32) * mixed.astype(jnp.float32), axis=2
    )
    whole_keys, whole_values = gather_pair(key_flat, values)
    count = whole_keys.shape[0]
    block = 512
    key_blocks = whole_keys.reshape(count // block, block, heads, head_dim)
    value_blocks = whole_values.reshape(count // block, block, heads, head_dim)
    pos_blocks = key_positions(order, 0, count, group).reshape(count // block, block)
    zero_grads = jnp.zeros((row_count, heads, head_dim), jnp.float32)

    def back_block(query_grad, item):
        key_block, value_block, pos_block = item
        scores = (
            jnp.einsum("qhd,khd->hqk", query_rot, key_block, preferred_element_type=jnp.float32)
            * scale
        )
        mask = (pos_block[None, :] <= query_pos[:, None])[None]
        share = jnp.where(mask, jnp.exp(scores - log_total[:, :, None]), 0.0)
        share_grad = jnp.einsum(
            "qhd,khd->hqk", d_attn_heads, value_block, preferred_element_type=jnp.float32
        )
        score_grad = (share * (share_grad - delta[:, :, None]) * scale).astype(jnp.bfloat16)
        query_grad = query_grad + jnp.einsum(
            "hqk,khd->qhd", score_grad, key_block, preferred_element_type=jnp.float32
        )
        key_grad = jnp.einsum(
            "hqk,qhd->khd", score_grad, query_rot, preferred_element_type=jnp.float32
        )
        value_grad = jnp.einsum(
            "hqk,qhd->khd",
            share.astype(jnp.bfloat16),
            d_attn_heads,
            preferred_element_type=jnp.float32,
        )
        return (
            query_grad,
            jnp.concatenate(
                [key_grad.reshape(block, local), value_grad.reshape(block, local)], axis=1
            ),
        )

    d_qrot, kv_terms = lax.scan(back_block, zero_grads, (key_blocks, value_blocks, pos_blocks))
    kv_grads = lax.psum_scatter(
        kv_terms.reshape(count, 2 * local), "ctx", scatter_dimension=0, tiled=True
    )
    d_krot = kv_grads[:, :local].reshape(row_count, heads, head_dim)
    d_value = kv_grads[:, local:].astype(jnp.bfloat16)
    d_qhead = unrotate(d_qrot, cosine, sine).reshape(row_count, local)
    d_khead = unrotate(d_krot, cosine, sine).reshape(row_count, local)
    d_query_gain = jnp.sum(d_qhead * query_norm, axis=0).reshape(heads, head_dim)
    d_key_gain = jnp.sum(d_khead * key_norm, axis=0).reshape(heads, head_dim)
    d_qnorm = d_qhead * qgain
    d_knorm = d_khead * kgain
    query_dot, key_dot = lax.psum(
        (jnp.sum(d_qnorm * query_norm, axis=1), jnp.sum(d_knorm * key_norm, axis=1)), "tp"
    )
    d_query = (query_scale[:, None] * (d_qnorm - query_norm * (query_dot / width)[:, None])).astype(
        jnp.bfloat16
    )
    d_key = (key_scale[:, None] * (d_knorm - key_norm * (key_dot / width)[:, None])).astype(
        jnp.bfloat16
    )
    grad_query = matmul(inputs_bf.T, d_query)
    grad_key = matmul(inputs_bf.T, d_key)
    grad_value = matmul(inputs_bf.T, d_value)
    input_grad = d_resid + lax.psum(
        matmul(d_query, w_query.T) + matmul(d_key, w_key.T) + matmul(d_value, w_value.T), "tp"
    )
    summed = (
        lax.psum_scatter(grad_query, ("ctx", "seq"), scatter_dimension=0, tiled=True),
        lax.psum_scatter(grad_key, ("ctx", "seq"), scatter_dimension=0, tiled=True),
        lax.psum_scatter(grad_value, ("ctx", "seq"), scatter_dimension=0, tiled=True),
        lax.psum_scatter(d_query_gain, ("ctx", "seq"), scatter_dimension=1, tiled=True),
        lax.psum_scatter(d_key_gain, ("ctx", "seq"), scatter_dimension=1, tiled=True),
        lax.psum_scatter(grad_output, ("ctx", "seq"), scatter_dimension=1, tiled=True),
        lax.psum_scatter(d_attn_gain, ("ctx", "seq"), scatter_dimension=0, tiled=True),
        lax.psum_scatter(grad_gate, ("ctx", "seq"), scatter_dimension=0, tiled=True),
        lax.psum_scatter(grad_up, ("ctx", "seq"), scatter_dimension=0, tiled=True),
        lax.psum_scatter(grad_down, ("ctx", "seq"), scatter_dimension=1, tiled=True),
        lax.psum_scatter(d_mlp_gain, ("ctx", "seq"), scatter_dimension=0, tiled=True),
    )
    return (
        block_out[None],
        input_grad[None],
        summed[0],
        summed[1],
        summed[2],
        summed[3],
        summed[4],
        summed[5],
        summed[6],
        summed[7],
        summed[8],
        summed[9],
        summed[10],
    )


def solution(mesh):
    return jax.shard_map(
        per_device,
        mesh=mesh,
        in_specs=(
            P("seq", "ctx", None),
            P("seq", "ctx", None),
            P("seq", None),
            P(None, "tp"),
            P(None, "tp"),
            P(None, "tp"),
            P("tp", None),
            P("tp", None),
            P("tp", None),
            P(),
            P(None, "tp"),
            P(None, "tp"),
            P("tp", None),
            P(),
        ),
        out_specs=(
            P("seq", "ctx", None),
            P("seq", "ctx", None),
            P(("ctx", "seq"), "tp"),
            P(("ctx", "seq"), "tp"),
            P(("ctx", "seq"), "tp"),
            P("tp", ("ctx", "seq")),
            P("tp", ("ctx", "seq")),
            P("tp", ("ctx", "seq")),
            P(("ctx", "seq")),
            P(("ctx", "seq"), "tp"),
            P(("ctx", "seq"), "tp"),
            P("tp", ("ctx", "seq")),
            P(("ctx", "seq")),
        ),
        check_vma=False,
    )
```

profile of v0, /device:TPU:0, one launch (start us, length us, event | category | flops | bytes accessed | tf_op | source)
XLA Modules:
  0.0 1605.6 jit_solution(7713981575235649113)
XLA Ops:
  18.8 13.4 all-reduce.4
  45.1 16.7 %all-gather.3.cloned.1.call-done = bf16[2048,512]{1,0:T(8,128)(2,1)} async-done(((bf16[512,512]{1,0:T(8,128)(2,1)}), bf16[2048,512]{1,0:T(8,128)(2,1)}) %all-gather.3.cloned.1.call-update) | async-done | bytes 2097168 | tf_op jit(solution)/shard_map/all_gather | solution.py:104
  69.1 27.6 %while.28 = (s32[]{:T(128)}, f32[4,512]{1,0:T(4,128)S(1)}, f32[4,512]{1,0:T(4,128)S(1)}, f32[4,512,128]{2,1,0:T(8,128)}, s32[4,512]{1,0:T(4,128)S(1)}, /*index=5...) while((s32[]{:T(128)}, f32[4,512]{1,0:T(4,128)S(1)}, ...), condition=%wide.region_9.10_spmd.clone, body=%wide.region_6.9_spmd.clone.sunk | while | flops 549464064 | bytes 25829572 | solution.py:134
  106.6 154.9 %all-reduce.10.cloned.1.call-done = f32[512,2048]{1,0:T(8,128)} async-done(((f32[512,2048]{1,0:T(8,128)}), f32[512,2048]{1,0:T(8,128)}) %all-reduce.10.cloned.1.call-update) | async-done | bytes 4194320 | tf_op jit(solution)/shard_map/psum | solution.py:139
  289.5 153.7 %all-reduce.12.cloned.1.call-done = f32[512,2048]{1,0:T(8,128)} async-done(((f32[512,2048]{1,0:T(8,128)}), f32[512,2048]{1,0:T(8,128)}) %all-reduce.12.cloned.1.call-update) | async-done | bytes 4194320 | tf_op jit(solution)/shard_map/psum | solution.py:149
  450.1 12.3 multiply_convert_fusion.1
  462.4 7.8 fusion.87
  470.2 9.5 convolution_add_fusion
  480.0 153.8 %all-reduce.14.cloned.1.call-done = f32[512,2048]{1,0:T(8,128)} async-done(((f32[512,2048]{1,0:T(8,128)}), f32[512,2048]{1,0:T(8,128)}) %all-reduce.14.cloned.1.call-update) | async-done | bytes 4194320 | tf_op jit(solution)/shard_map/psum | solution.py:166
  648.9 64.1 %while.29 = (s32[]{:T(128)}, f32[512,4,128]{0,2,1:T(8,128)}, f32[4,512,1024]{2,1,0:T(8,128)}, bf16[4,512,4,128]{3,1,2,0:T(8,128)(2,1)}, s32[4,512]{1,0:T(4,128)S...) while((s32[]{:T(128)}, f32[512,4,128]{0,2,1:T(8,128)}, ...), condition=%wide.region_19.20_spmd.clone, body=%wide.region_18.19_spmd.clone.sunk | while | flops 1355022336 | bytes 48529624 | solution.py:218
  713.2 70.5 %reduce-scatter.15.cloned.1.call-done = f32[512,1024]{1,0:T(8,128)} async-done(((f32[2048,1024]{1,0:T(8,128)}), f32[512,1024]{1,0:T(8,128)}) %reduce-scatter.15.cloned.1.call-update) | async-done | bytes 2097168 | tf_op jit(solution)/shard_map/reduce_scatter | solution.py:219
  795.0 11.9 all-reduce.3
  845.9 14.1 fusion.80
  860.1 13.1 fusion.92
  873.6 12.5 fusion.91
  888.0 25.2 %all-reduce.2 = (f32[2048]{0:T(1024)S(1)}, f32[2048]{0:T(1024)S(1)}) all-reduce(f32[2048]{0:T(1024)S(1)} %get-tuple-element.323, f32[2048]{0:T(1024)S(1)} %copy-done.28), channel_id=9, replica_groups=mesh['ctx'=4,'seq'=2,'tp'=4] {'ctx','seq'}, use_global_device_ids=true, to_apply=%region_35.36.clone | all-reduce | flops 4096 | bytes 32768
  917.2 103.9 %all-reduce.16.cloned.1.call-done = f32[512,2048]{1,0:T(8,128)} async-done(((f32[512,2048]{1,0:T(8,128)}), f32[512,2048]{1,0:T(8,128)}) %all-reduce.16.cloned.1.call-update) | async-done | bytes 4194320 | tf_op jit(solution)/shard_map/psum | solution.py:242
  1028.6 45.7 %reduce-scatter.19.cloned.1.call-done = f32[256,512]{0,1:T(8,128)} async-done(((f32[2048,512]{0,1:T(8,128)}), f32[256,512]{0,1:T(8,128)}) %reduce-scatter.19.cloned.1.call-update) | async-done | bytes 524304 | tf_op jit(solution)/shard_map/reduce_scatter | solution.py:247
  1076.4 52.4 %reduce-scatter.17.cloned.1.call-done = f32[256,512]{0,1:T(8,128)} async-done(((f32[2048,512]{0,1:T(8,128)}), f32[256,512]{0,1:T(8,128)}) %reduce-scatter.17.cloned.1.call-update) | async-done | bytes 524304 | tf_op jit(solution)/shard_map/reduce_scatter | solution.py:246
  1130.8 52.3 %reduce-scatter.21.cloned.1.call-done = f32[256,512]{0,1:T(8,128)} async-done(((f32[2048,512]{0,1:T(8,128)}), f32[256,512]{0,1:T(8,128)}) %reduce-scatter.21.cloned.1.call-update) | async-done | bytes 524304 | tf_op jit(solution)/shard_map/reduce_scatter | solution.py:248
  1185.2 53.0 %reduce-scatter.23.cloned.1.call-done = f32[512,256]{1,0:T(8,128)} async-done(((f32[512,2048]{1,0:T(8,128)}), f32[512,256]{1,0:T(8,128)}) %reduce-scatter.23.cloned.1.call-update) | async-done | bytes 524304 | tf_op jit(solution)/shard_map/reduce_scatter | solution.py:251
  1238.1 120.0 %reduce-scatter.29.cloned.1.call-done = f32[2048,256]{1,0:T(8,128)} async-done(((f32[2048,2048]{1,0:T(8,128)}), f32[2048,256]{1,0:T(8,128)}) %reduce-scatter.29.cloned.1.call-update) | async-done | bytes 2097168 | tf_op jit(solution)/shard_map/reduce_scatter | solution.py:255
  1358.1 120.2 %reduce-scatter.27.cloned.1.call-done = f32[256,2048]{1,0:T(8,128)} async-done(((f32[2048,2048]{1,0:T(8,128)}), f32[256,2048]{1,0:T(8,128)}) %reduce-scatter.27.cloned.1.call-update) | async-done | bytes 2097168 | tf_op jit(solution)/shard_map/reduce_scatter | solution.py:254
  1478.3 120.2 %reduce-scatter.25.cloned.1.call-done = f32[256,2048]{1,0:T(8,128)} async-done(((f32[2048,2048]{1,0:T(8,128)}), f32[256,2048]{1,0:T(8,128)}) %reduce-scatter.25.cloned.1.call-update) | async-done | bytes 2097168 | tf_op jit(solution)/shard_map/reduce_scatter | solution.py:253
  (303 shorter events, 252.1 us)
Async XLA Ops:
  7.2 30.7 %all-gather.5.cloned.1.call-start = ((), (), s32[]{:S(2)}) async-start(), calls=%async_computation.11 | async-start | bytes 2621440 | tf_op jit(solution)/shard_map/all_gather | solution.py:105
  11.7 50.2 %all-gather.3.cloned.1.call-start = ((), (), s32[]{:S(2)}) async-start(), calls=%async_computation.10 | async-start | bytes 2621440 | tf_op jit(solution)/shard_map/all_gather | solution.py:104
  16.4 15.9 copy-start.37
  16.4 16.6 %copy-start.33 = (f32[4,128]{1,0:T(4,128)S(1)}, f32[4,128]{1,0:T(4,128)}, u32[]{:S(2)}) copy-start(f32[4,128]{1,0:T(4,128)} %param.24) | copy-start | bytes 6148
  16.4 18.0 %copy-start.35 = (f32[4,128]{1,0:T(4,128)S(1)}, f32[4,128]{1,0:T(4,128)}, u32[]{:S(2)}) copy-start(f32[4,128]{1,0:T(4,128)} %param.25) | copy-start | bytes 6148
  37.3 224.2 %all-reduce.10.cloned.1.call-start = ((), (), s32[]{:S(2)}) async-start(), calls=%async_computation.12 | async-start | bytes 8388608 | tf_op jit(solution)/shard_map/psum | solution.py:139
  106.3 157.9 %copy-start.26 = (f32[2048]{0:T(1024)S(1)}, f32[2048]{0:T(1024)}, u32[]{:S(2)}) copy-start(f32[2048]{0:T(1024)} %param.27) | copy-start | bytes 24580
  106.3 336.8 %all-reduce.12.cloned.1.call-start = ((), (), s32[]{:S(2)}) async-start(), calls=%async_computation.13 | async-start | bytes 8388608 | tf_op jit(solution)/shard_map/psum | solution.py:149
  267.4 15.5 slice-start
  289.0 156.8 %copy-start.27 = (f32[2048]{0:T(1024)S(1)}, f32[2048]{0:T(1024)}, u32[]{:S(2)}) copy-start(f32[2048]{0:T(1024)} %param.31) | copy-start | bytes 24580
  289.1 344.8 %all-reduce.14.cloned.1.call-start = ((), (), s32[]{:S(2)}) async-start(), calls=%async_computation.14 | async-start | bytes 8388608 | tf_op jit(solution)/shard_map/psum | solution.py:166
  479.7 303.9 %reduce-scatter.15.cloned.1.call-start = ((), (), s32[]{:S(2)}) async-start(), calls=%async_computation.15 | async-start | bytes 10485760 | tf_op jit(solution)/shard_map/reduce_scatter | solution.py:219
  713.1 75.4 %copy-start.21 = (f32[512,64]{0,1:T(8,128)S(1)}, f32[512,64]{0,1:T(8,128)}, u32[]{:S(2)}) copy-start(f32[512,64]{0,1:T(8,128)} %copy-done.20) | copy-start | bytes 393220
  713.1 75.4 %copy-start.23 = (f32[512,64]{0,1:T(8,128)S(1)}, f32[512,64]{0,1:T(8,128)}, u32[]{:S(2)}) copy-start(f32[512,64]{0,1:T(8,128)} %copy-done.22) | copy-start | bytes 393220
  713.1 201.4 %reduce-scatter.33.cloned.1.call-start = ((), (), s32[]{:S(2)}) async-start(), calls=%async_computation.25 | async-start | bytes 73728
  792.2 123.6 %reduce-scatter.31.cloned.1.call-start = ((), (), s32[]{:S(2)}) async-start(), calls=%async_computation.24 | async-start | bytes 73728
  817.9 203.2 %all-reduce.16.cloned.1.call-start = ((), (), s32[]{:S(2)}) async-start(), calls=%async_computation.16 | async-start | bytes 8388608 | tf_op jit(solution)/shard_map/psum | solution.py:242
  825.6 248.7 %reduce-scatter.19.cloned.1.call-start = ((), (), s32[]{:S(2)}) async-start(), calls=%async_computation.18 | async-start | bytes 4718592 | tf_op jit(solution)/shard_map/reduce_scatter | solution.py:247
  830.5 298.3 %reduce-scatter.17.cloned.1.call-start = ((), (), s32[]{:S(2)}) async-start(), calls=%async_computation.17 | async-start | bytes 4718592 | tf_op jit(solution)/shard_map/reduce_scatter | solution.py:246
  835.4 347.8 %reduce-scatter.21.cloned.1.call-start = ((), (), s32[]{:S(2)}) async-start(), calls=%async_computation.19 | async-start | bytes 4718592 | tf_op jit(solution)/shard_map/reduce_scatter | solution.py:248
  840.7 397.4 %reduce-scatter.23.cloned.1.call-start = ((), (), s32[]{:S(2)}) async-start(), calls=%async_computation.20 | async-start | bytes 4718592 | tf_op jit(solution)/shard_map/reduce_scatter | solution.py:251
  845.6 512.5 %reduce-scatter.29.cloned.1.call-start = ((), (), s32[]{:S(2)}) async-start(), calls=%async_computation.23 | async-start | bytes 18874368 | tf_op jit(solution)/shard_map/reduce_scatter | solution.py:255
  860.0 618.3 %reduce-scatter.27.cloned.1.call-start = ((), (), s32[]{:S(2)}) async-start(), calls=%async_computation.22 | async-start | bytes 18874368 | tf_op jit(solution)/shard_map/reduce_scatter | solution.py:254
  873.2 725.3 %reduce-scatter.25.cloned.1.call-start = ((), (), s32[]{:S(2)}) async-start(), calls=%async_computation.21 | async-start | bytes 18874368 | tf_op jit(solution)/shard_map/reduce_scatter | solution.py:253
  (50 other events, 178.3 us)
Sparse Core Ops, SparseCore 0:
  11.8 25.2 all-gather.4
  39.2 22.5 all-gather.2
  106.5 154.9 all-reduce.9
  289.2 153.9 all-reduce.11
  479.8 153.9 all-reduce.13
  713.2 70.3 reduce-scatter.14
  792.4 33.5 reduce-scatter.32
  829.5 33.5 reduce-scatter.30
  866.0 154.9 all-reduce.15
  1024.2 50.0 reduce-scatter.18
  1077.7 51.0 reduce-scatter.16
  1132.0 51.0 reduce-scatter.20
  1187.1 51.0 reduce-scatter.22
  1242.1 115.9 reduce-scatter.28
  1362.1 116.1 reduce-scatter.26
  1482.3 116.1 reduce-scatter.24
where the time goes:
time: 1620 us; the launch traced here: 1610 us
  waiting for transfers between devices  1220 us (75%)
  matrix products  191 us (12%)
  local copies, waits for them, and re-layouts  73 us (5%)
  other arithmetic  54.7 us (3%)
  blocking collectives  50.6 us (3%)
    psum x1, waiting for transfers between devices, per_device(): proj = lax.psum(matmul(attn_flat, w_output), 'tp')  155 us
    psum x1, waiting for transfers between devices, per_device(): lax.psum(matmul(d_gate, w_gate.T) + matmul(d_up, w_up.T), 'tp')  154 us
    psum x1, waiting for transfers between devices, per_device(): down = lax.psum(matmul(inner, w_down), 'tp')  154 us
    dot_general x21, matrix products, matmul(): return jnp.dot(left, right, preferred_element_type=jnp.float32)  141 us
    reduce_scatter x1, waiting for transfers between devices, per_device(): lax.psum_scatter(grad_gate, ('ctx', 'seq'), scatter_dimension=0, tiled=True)  120 us
    reduce_scatter x1, waiting for transfers between devices, per_device(): lax.psum_scatter(grad_up, ('ctx', 'seq'), scatter_dimension=0, tiled=True)  120 us
    reduce_scatter x1, waiting for transfers between devices, per_device(): lax.psum_scatter(grad_down, ('ctx', 'seq'), scatter_dimension=1, tiled=True)  120 us
    psum x1, waiting for transfers between devices, per_device(): lax.psum(matmul(d_query, w_query.T) + matmul(d_key, w_key.T) + matmul(d_v...  104 us
  transfers between devices with their start and end apart: 16, of which 13 were waited for; matrix products, arithmetic and copies ran while one was open for 7% of the time, Pallas kernels for 0%

commit v1 on v0

--- a/solution.py
+++ b/solution.py
@@ -2,6 +2,125 @@
 import jax.numpy as jnp
 from jax import lax
 from jax.sharding import PartitionSpec as P
+from jax.experimental import pallas as pl
+from jax.experimental.pallas import tpu as pltpu
+
+MESH = pl.DeviceIdType.MESH
+
+def line_allreduce(x, n, blocks, chains, cid):
+    rows, width = x.shape
+    W = width // n
+    rc = rows // blocks
+    C = blocks // chains
+    M = C * n
+
+    def kernel(x_ref, out_ref, own, recv_l, recv_r, res, ssr, ssl, rsl, rsr):
+        i = lax.axis_index("tp")
+        has_l, has_r = i > 0, i < n - 1
+        bar = pltpu.get_barrier_semaphore()
+        @pl.when(has_l)
+        def _():
+            pl.semaphore_signal(bar, inc=1, device_id={"tp": i - 1}, device_id_type=MESH)
+        @pl.when(has_r)
+        def _():
+            pl.semaphore_signal(bar, inc=1, device_id={"tp": i + 1}, device_id_type=MESH)
+        for j in range(n):
+            own[j] = x_ref[:, j * W:(j + 1) * W]
+        pl.semaphore_wait(bar, has_l.astype(jnp.int32) + has_r.astype(jnp.int32))
+
+        def rows_of(g, p):
+            b = (p // n) * chains + g
+            return pl.ds(pl.multiple_of(b * rc, rc), rc)
+
+        def right(src, dst, g, p, j):
+            sl = rows_of(g, p)
+            return pltpu.make_async_remote_copy(src.at[j, sl], dst.at[j, sl], ssr.at[g, p], rsl.at[g, p],
+                                                device_id={"tp": i + 1}, device_id_type=MESH)
+        def left(src, dst, g, q, j):
+            sl = rows_of(g, q)
+            return pltpu.make_async_remote_copy(src.at[j, sl], dst.at[j, sl], ssl.at[g, q], rsr.at[g, q],
+                                                device_id={"tp": i - 1}, device_id_type=MESH)
+        def wait_l(g, p, j):
+            sl = rows_of(g, p)
+            pltpu.make_async_remote_copy(own.at[j, sl], recv_l.at[j, sl], ssr.at[g, p], rsl.at[g, p],
+                                         device_id={"tp": i - 1}, device_id_type=MESH).wait_recv()
+        def wait_r(g, q, j):
+            sl = rows_of(g, q)
+            pltpu.make_async_remote_copy(own.at[j, sl], recv_r.at[j, sl], ssl.at[g, q], rsr.at[g, q],
+                                         device_id={"tp": i + 1}, device_id_type=MESH).wait_recv()
+
+        def step(t, _):
+            for g in range(chains):
+                p = t - i
+                q = t - (n - 1 - i)
+                pm = lax.rem(p + n * M, n)
+                jr = n - 1 - pm
+                jl = lax.rem(q + n * M, n)
+                pv = (p >= 0) & (p < M)
+                qv = (q >= 0) & (q < M)
+                @pl.when(pv & has_l)
+                def _():
+                    wait_l(g, p, jr)
+                @pl.when(qv & has_r)
+                def _():
+                    wait_r(g, q, jl)
+                @pl.when(pv & (jr > i))
+                def _():
+                    sl = rows_of(g, p)
+                    @pl.when(has_l)
+                    def _():
+                        own[jr, sl] = (own[jr, sl].astype(jnp.float32) + recv_l[jr, sl].astype(jnp.float32)).astype(jnp.bfloat16)
+                    right(own, recv_l, g, p, jr).start()
+                @pl.when(qv & (jl < i))
+                def _():
+                    sl = rows_of(g, q)
+                    @pl.when(has_r)
+                    def _():
+                        own[jl, sl] = (own[jl, sl].astype(jnp.float32) + recv_r[jl, sl].astype(jnp.float32)).astype(jnp.bfloat16)
+                    left(own, recv_r, g, q, jl).start()
+                @pl.when(pv & (jr == i))
+                def _():
+                    sl = rows_of(g, p)
+                    @pl.when(has_l & has_r)
+                    def _():
+                        res[i, sl] = (own[i, sl].astype(jnp.float32) + recv_l[i, sl].astype(jnp.float32) + recv_r[i, sl].astype(jnp.float32)).astype(jnp.bfloat16)
+                    @pl.when(jnp.logical_not(has_l))
+                    def _():
+                        res[i, sl] = (own[i, sl].astype(jnp.float32) + recv_r[i, sl].astype(jnp.float32)).astype(jnp.bfloat16)
+                    @pl.when(jnp.logical_not(has_r))
+                    def _():
+                        res[i, sl] = (own[i, sl].astype(jnp.float32) + recv_l[i, sl].astype(jnp.float32)).astype(jnp.bfloat16)
+                @pl.when(pv & (jr <= i) & has_r)
+                def _():
+                    right(res, res, g, p, jr).start()
+                @pl.when(qv & (jl >= i) & has_l)
+                def _():
+                    left(res, res, g, q, jl).start()
+            return 0
+        lax.fori_loop(0, M + n - 1, step, 0)
+
+        def drain(p, _):
+            for g in range(chains):
+                @pl.when(has_r)
+                def _():
+                    right(own, recv_l, g, p, 0).wait_send()
+                @pl.when(has_l)
+                def _():
+                    left(own, recv_r, g, p, 0).wait_send()
+            return 0
+        lax.fori_loop(0, M, drain, 0)
+        for j in range(n):
+            out_ref[:, j * W:(j + 1) * W] = res[j]
+
+    return pl.pallas_call(
+        kernel,
+        out_shape=jax.ShapeDtypeStruct((rows, width), jnp.bfloat16),
+        in_specs=[pl.BlockSpec(memory_space=pltpu.VMEM)],
+        out_specs=pl.BlockSpec(memory_space=pltpu.VMEM),
+        scratch_shapes=[pltpu.VMEM((n, rows, W), jnp.bfloat16)] * 4 + [pltpu.SemaphoreType.DMA((chains, M))] * 4,
+        compiler_params=pltpu.CompilerParams(collective_id=cid, has_side_effects=True, vmem_limit_bytes=40 * 2**20),
+        name=f"line_ar_{blocks}_{chains}",
+    )(x)
 
 norm_eps = 1e-06
 rope_base = 500000.0
@@ -49,6 +168,12 @@
         lax.all_gather(keys, "ctx", axis=0, tiled=True),
         lax.all_gather(values, "ctx", axis=0, tiled=True),
     )
+
+
+def tp_sum(partial, cid):
+    n = lax.axis_size("tp")
+    summed = line_allreduce(partial.astype(jnp.bfloat16), n, 16, 8, cid)
+    return summed.astype(jnp.float32)
 
 
 def per_device(
@@ -136,7 +261,7 @@
     log_total = peak + jnp.log(total)
     mixed = (accum / total[:, :, None]).astype(jnp.bfloat16)
     attn_flat = mixed.transpose(1, 0, 2).reshape(row_count, local)
-    proj = lax.psum(matmul(attn_flat, w_output), "tp")
+    proj = tp_sum(matmul(attn_flat, w_output), 1)
     attn_scale = lax.rsqrt(jnp.mean(proj * proj, axis=1) + norm_eps)
     attn_norm = proj * attn_scale[:, None]
     resid = inputs + attn_norm * attn_gain
@@ -146,7 +271,7 @@
     sigma = jax.nn.sigmoid(gate)
     active = gate * sigma
     inner = (active * up).astype(jnp.bfloat16)
-    down = lax.psum(matmul(inner, w_down), "tp")
+    down = tp_sum(matmul(inner, w_down), 2)
     mlp_scale = lax.rsqrt(jnp.mean(down * down, axis=1) + norm_eps)
     mlp_norm = down * mlp_scale[:, None]
     block_out = resid + mlp_norm * mlp_gain
@@ -163,7 +288,7 @@
     d_up = (d_inner * active).astype(jnp.bfloat16)
     grad_gate = matmul(hidden.T, d_gate)
     grad_up = matmul(hidden.T, d_up)
-    d_resid = upstream + lax.psum(matmul(d_gate, w_gate.T) + matmul(d_up, w_up.T), "tp")
+    d_resid = upstream + tp_sum(matmul(d_gate, w_gate.T) + matmul(d_up, w_up.T), 3)
     d_attn_gain = jnp.sum(d_resid * attn_norm, axis=0)
     d_anorm = d_resid * attn_gain
     d_proj = (
@@ -217,8 +342,9 @@
 
     d_qrot, kv_terms = lax.scan(back_block, zero_grads, (key_blocks, value_blocks, pos_blocks))
     kv_grads = lax.psum_scatter(
-        kv_terms.reshape(count, 2 * local), "ctx", scatter_dimension=0, tiled=True
-    )
+        kv_terms.reshape(count, 2 * local).astype(jnp.bfloat16), "ctx", scatter_dimension=0, tiled=True
+    )
+    kv_grads = kv_grads.astype(jnp.float32)
     d_krot = kv_grads[:, :local].reshape(row_count, heads, head_dim)
     d_value = kv_grads[:, local:].astype(jnp.bfloat16)
     d_qhead = unrotate(d_qrot, cosine, sine).reshape(row_count, local)
@@ -239,20 +365,20 @@
     grad_query = matmul(inputs_bf.T, d_query)
     grad_key = matmul(inputs_bf.T, d_key)
     grad_value = matmul(inputs_bf.T, d_value)
-    input_grad = d_resid + lax.psum(
-        matmul(d_query, w_query.T) + matmul(d_key, w_key.T) + matmul(d_value, w_value.T), "tp"
+    input_grad = d_resid + tp_sum(
+        matmul(d_query, w_query.T) + matmul(d_key, w_key.T) + matmul(d_value, w_value.T), 4
     )
     summed = (
-        lax.psum_scatter(grad_query, ("ctx", "seq"), scatter_dimension=0, tiled=True),
-        lax.psum_scatter(grad_key, ("ctx", "seq"), scatter_dimension=0, tiled=True),
-        lax.psum_scatter(grad_value, ("ctx", "seq"), scatter_dimension=0, tiled=True),
+        lax.psum_scatter(grad_query.astype(jnp.bfloat16), ("ctx", "seq"), scatter_dimension=0, tiled=True).astype(jnp.float32),
+        lax.psum_scatter(grad_key.astype(jnp.bfloat16), ("ctx", "seq"), scatter_dimension=0, tiled=True).astype(jnp.float32),
+        lax.psum_scatter(grad_value.astype(jnp.bfloat16), ("ctx", "seq"), scatter_dimension=0, tiled=True).astype(jnp.float32),
         lax.psum_scatter(d_query_gain, ("ctx", "seq"), scatter_dimension=1, tiled=True),
         lax.psum_scatter(d_key_gain, ("ctx", "seq"), scatter_dimension=1, tiled=True),
-        lax.psum_scatter(grad_output, ("ctx", "seq"), scatter_dimension=1, tiled=True),
+        lax.psum_scatter(grad_output.astype(jnp.bfloat16), ("ctx", "seq"), scatter_dimension=1, tiled=True).astype(jnp.float32),
         lax.psum_scatter(d_attn_gain, ("ctx", "seq"), scatter_dimension=0, tiled=True),
-        lax.psum_scatter(grad_gate, ("ctx", "seq"), scatter_dimension=0, tiled=True),
-        lax.psum_scatter(grad_up, ("ctx", "seq"), scatter_dimension=0, tiled=True),
-        lax.psum_scatter(grad_down, ("ctx", "seq"), scatter_dimension=1, tiled=True),
+        lax.psum_scatter(grad_gate.astype(jnp.bfloat16), ("ctx", "seq"), scatter_dimension=0, tiled=True).astype(jnp.float32),
+        lax.psum_scatter(grad_up.astype(jnp.bfloat16), ("ctx", "seq"), scatter_dimension=0, tiled=True).astype(jnp.float32),
+        lax.psum_scatter(grad_down.astype(jnp.bfloat16), ("ctx", "seq"), scatter_dimension=1, tiled=True).astype(jnp.float32),
         lax.psum_scatter(d_mlp_gain, ("ctx", "seq"), scatter_dimension=0, tiled=True),
     )
     return (

time: 1620 us -> 980 us (0.60)
  waiting for transfers between devices: 1220 us -> 365 us
  Pallas kernels: 0 us -> 232 us
    psum x4 -> x0, waiting for transfers between devices: 566 us -> none  [the longest x1 155 us: per_device(): proj = lax.psum(matmul(attn_flat, w_output), 'tp')]
    reduce_scatter x8, waiting for transfers between devices: 634 us -> 331 us  [the longest x1 72.8 us: per_device(): lax.psum_scatter(grad_down.astype(jnp.bfloat16), ('ctx', 'seq'), scatter_...]
    pallas_call x0 -> x4, Pallas kernels: none -> 232 us  [line_allreduce(): pl.pallas_call(kernel, out_shape=jax.ShapeDtypeStruct((rows, width), jnp....]
    dot_general x21, matrix products: 141 us -> 116 us  [matmul(): return jnp.dot(left, right, preferred_element_type=jnp.float32)]
    all_gather x1, waiting for transfers between devices: 0.02 us -> 17.4 us  [per_device(): values_in = lax.all_gather(values, 'ctx', axis=0, tiled=True)]
  transfers between devices with their start and end apart: 16 -> 12, of which waited for: 13 -> 8; matrix products, arithmetic and copies ran while one was open for 7% -> 10% of each run, Pallas kernels for 0% -> 6%
where the time goes in v1:
time: 980 us; the launch traced here: 970 us
  waiting for transfers between devices  365 us (37%)
  Pallas kernels  232 us (24%)
  matrix products  187 us (19%)
  local copies, waits for them, and re-layouts  64 us (7%)
  other arithmetic  55.1 us (6%)
  blocking collectives  49.4 us (5%)
  between operations  16 us (2%)
    pallas_call x4, Pallas kernels, line_allreduce(): pl.pallas_call(kernel, out_shape=jax.ShapeDtypeStruct((rows, width), jnp....  232 us
    dot_general x21, matrix products, matmul(): return jnp.dot(left, right, preferred_element_type=jnp.float32)  116 us
    reduce_scatter x1, waiting for transfers between devices, per_device(): lax.psum_scatter(grad_down.astype(jnp.bfloat16), ('ctx', 'seq'), scatter_...  72.8 us
    reduce_scatter x1, waiting for transfers between devices, per_device(): lax.psum_scatter(grad_gate.astype(jnp.bfloat16), ('ctx', 'seq'), scatter_...  72.3 us
    reduce_scatter x1, waiting for transfers between devices, per_device(): lax.psum_scatter(grad_up.astype(jnp.bfloat16), ('ctx', 'seq'), scatter_di...  72.1 us
    reduce_scatter x1, waiting for transfers between devices, per_device(): lax.psum_scatter(grad_value.astype(jnp.bfloat16), ('ctx', 'seq'), scatter...  42.5 us
    reduce_scatter x1, waiting for transfers between devices, per_device(): lax.psum_scatter(kv_terms.reshape(count, 2 * local).astype(jnp.bfloat16),...  38.4 us
    reduce_scatter x1, waiting for transfers between devices, per_device(): lax.psum_scatter(grad_query.astype(jnp.bfloat16), ('ctx', 'seq'), scatter...  33.4 us
  transfers between devices with their start and end apart: 12, of which 8 were waited for; matrix products, arithmetic and copies ran while one was open for 10% of the time, Pallas kernels for 6%

profile of v1, /device:TPU:0, one launch (start us, length us, event | category | flops | bytes accessed | tf_op | source)
XLA Modules:
  0.0 969.7 jit_solution(15569346414164433813)
XLA Ops:
  14.4 13.5 %all-reduce.4 = (f32[512]{0:T(512)S(1)}, f32[512]{0:T(512)S(1)}) all-reduce(f32[512]{0:T(512)S(1)} %get-tuple-element.401, f32[512]{0:T(512)S(1)} %get-tuple-element.403), channel_id=1, replica_groups=mesh['ctx'=4,'seq'=2,'tp'=4] {'tp'}, use_global_device_ids=true, to_apply=%region_1.2 | all-reduce | flops 1024 | bytes 8192 | tf_op jit(solution)/shard_map/psum | solution.py:208
  39.0 16.0 %all-gather.3.cloned.1.call-done = bf16[2048,512]{1,0:T(8,128)(2,1)} async-done(((bf16[512,512]{1,0:T(8,128)(2,1)}), bf16[2048,512]{1,0:T(8,128)(2,1)}) %all-gather.3.cloned.1.call-update) | async-done | bytes 2097168 | tf_op jit(solution)/shard_map/all_gather | solution.py:229
  62.3 17.4 %all-gather.5.cloned.1.call-done = bf16[2048,512]{1,0:T(8,128)(2,1)} async-done(((bf16[512,512]{1,0:T(8,128)(2,1)}), bf16[2048,512]{1,0:T(8,128)(2,1)}) %all-gather.5.cloned.1.call-update) | async-done | bytes 2097168 | tf_op jit(solution)/shard_map/all_gather | solution.py:230
  87.0 45.3 %while.28 = (s32[]{:T(128)}, f32[4,512]{1,0:T(4,128)S(1)}, f32[4,512]{1,0:T(4,128)S(1)}, f32[4,512,128]{2,1,0:T(8,128)}, s32[4,512]{1,0:T(4,128)S(1)}, /*index=5...) while((s32[]{:T(128)}, f32[4,512]{1,0:T(4,128)S(1)}, ...), condition=%wide.region_9.10_spmd.clone, body=%wide.region_6.9_spmd.clone.sunk | while | flops 549464064 | bytes 34219160 | solution.py:259
  139.4 59.6 %line_ar_16_8.4 = bf16[512,2048]{1,0:T(8,128)(2,1)S(1)} custom-call(bf16[512,2048]{1,0:T(8,128)(2,1)S(1)} %convolution_convert_fusion.8.x_ref), custom_call_target="tpu_custom_call" | custom-call | tf_op jit(solution)/shard_map/line_ar_16_8/pallas_call | solution.py:115
  206.8 10.7 %multiply_convert_fusion.2 = (bf16[512,2048]{1,0:T(8,128)(2,1)S(1)}, f32[512,2048]{1,0:T(8,128)}) fusion(f32[512,2048]{1,0:T(8,128)} %fusion.105, bf16[512,2048]{1,0:T(8,128)(2,1)S(1)} %fusion.69, bf16[2048,2048]{1,0:T(8,128)(2,1)} %param.29), kind=kOutput, calls=%fused_computation.94 | convolution fusion | flops 4301258752 | bytes 20971520 | tf_op jit(solution)/shard_map/dot_general | solution.py:131
  223.7 57.5 %line_ar_16_8.5 = bf16[512,2048]{1,0:T(8,128)(2,1)S(1)} custom-call(bf16[512,2048]{1,0:T(8,128)(2,1)S(1)} %convolution_convert_fusion.7.x_ref), custom_call_target="tpu_custom_call" | custom-call | tf_op jit(solution)/shard_map/line_ar_16_8/pallas_call | solution.py:115
  283.1 12.0 %multiply_convert_fusion = (bf16[512,2048]{1,0:T(8,128)(2,1)}, bf16[512,2048]{1,0:T(8,128)(2,1)}) fusion(f32[512,2048]{1,0:T(8,128)} %fusion.105, f32[512,2048]{1,0:T(8,128)} %get-tuple-element.406, bf16[2048,2048]{1,0:T(8,128)(2,1)} %param.30, bf16[512,2048]{1,0:T(8,128)(2,1)S(1)} %line_ar_16_8.5, bf16[1,512,2048]{2,1,0:T(8,128)(2,1)S(1)} %copy-done.9, ...), kind=kOutput, calls=%fused_computation.92 | convolution fusion | flops 4316987392 | bytes 25178112 | tf_op jit(solution)/shard_map/dot_general | solution.py:131
  295.1 7.6 fusion.106
  302.7 8.6 add_convert_fusion.1.x_ref
  311.3 56.9 %line_ar_16_8.6 = bf16[512,2048]{1,0:T(8,128)(2,1)S(1)} custom-call(bf16[512,2048]{1,0:T(8,128)(2,1)S(1)} %add_convert_fusion.1.x_ref), custom_call_target="tpu_custom_call" | custom-call | tf_op jit(solution)/shard_map/line_ar_16_8/pallas_call | solution.py:115
  377.4 61.8 %while.29 = (s32[]{:T(128)}, f32[512,4,128]{0,2,1:T(8,128)}, bf16[4,512,1024]{2,1,0:T(8,128)(2,1)}, bf16[4,512,4,128]{3,1,2,0:T(8,128)(2,1)}, s32[4,512]{1,0:T(4...) while((s32[]{:T(128)}, f32[512,4,128]{0,2,1:T(8,128)}, ...), condition=%wide.region_16.17_spmd.clone, body=%wide.region_15.16_spmd.clone.sunk | while | flops 1356595200 | bytes 49580308 | solution.py:343
  444.6 38.4 %reduce-scatter.15.cloned.1.call-done = bf16[512,1024]{1,0:T(8,128)(2,1)} async-done(((bf16[2048,1024]{1,0:T(8,128)(2,1)}), bf16[512,1024]{1,0:T(8,128)(2,1)}) %reduce-scatter.15.cloned.1.call-update) | async-done | bytes 1048592 | tf_op jit(solution)/shard_map/reduce_scatter | solution.py:344
  494.7 11.7 %all-reduce.3 = (f32[512]{0:T(512)S(1)}, f32[512]{0:T(512)S(1)}) all-reduce(f32[512]{0:T(512)S(1)} %get-tuple-element.330, f32[512]{0:T(512)S(1)} %get-tuple-element.328), channel_id=1, replica_groups=mesh['ctx'=4,'seq'=2,'tp'=4] {'tp'}, use_global_device_ids=true, to_apply=%region_18.19 | all-reduce | flops 1024 | bytes 8192 | tf_op jit(solution)/shard_map/psum | solution.py:356
  525.4 11.1 %convolution_convert_fusion = bf16[2048,2048]{1,0:T(8,128)(2,1)} fusion(bf16[512,2048]{1,0:T(8,128)(2,1)} %copy-done.52, bf16[512,2048]{1,0:T(8,128)(2,1)} %copy-done.1, bf16[1,512,2048]{2,1,0:T(8,128)(2,1)} %param.19, f32[512]{0:T(512)S(1)} %broadcast_multiply_fusion.4, f32[2048]{0:T(1024)S(1)} %copy-done.40, f32[512]{0:T(512)S(1)} %add_rsqrt_fusion), kind=kOutput, calls=%fused_computation.57 | convolution fusion | flops 4307550208 | bytes 14692352 | tf_op jit(solution)/shard_map/dot_general | solution.py:131
  536.8 10.0 %convolution_convert_fusion.2 = bf16[2048,2048]{1,0:T(8,128)(2,1)} fusion(bf16[512,2048]{1,0:T(8,128)(2,1)} %copy-done.24, bf16[512,2048]{1,0:T(8,128)(2,1)} %get-tuple-element.384), kind=kOutput, calls=%fused_computation.59 | convolution fusion | flops 4299161600 | bytes 12582912 | tf_op jit(solution)/shard_map/dot_general | solution.py:131
  546.9 10.1 %convolution_convert_fusion.1 = bf16[2048,2048]{1,0:T(8,128)(2,1)} fusion(bf16[512,2048]{1,0:T(8,128)(2,1)} %copy-done.24, bf16[512,2048]{1,0:T(8,128)(2,1)} %get-tuple-element.383), kind=kOutput, calls=%fused_computation.58 | convolution fusion | flops 4299161600 | bytes 12582912 | tf_op jit(solution)/shard_map/dot_general | solution.py:131
  558.9 24.2 %all-reduce.2 = (f32[2048]{0:T(1024)S(1)}, f32[2048]{0:T(1024)S(1)}) all-reduce(f32[2048]{0:T(1024)S(1)} %get-tuple-element.323, f32[2048]{0:T(1024)S(1)} %get-tuple-element.325), channel_id=9, replica_groups=mesh['ctx'=4,'seq'=2,'tp'=4] {'ctx','seq'}, use_global_device_ids=true, to_apply=%region_31.32.clone | all-reduce | flops 4096 | bytes 32768
  591.2 58.3 %line_ar_16_8.7 = bf16[512,2048]{1,0:T(8,128)(2,1)S(1)} custom-call(bf16[512,2048]{1,0:T(8,128)(2,1)S(1)} %add_convert_fusion.x_ref), custom_call_target="tpu_custom_call" | custom-call | tf_op jit(solution)/shard_map/line_ar_16_8/pallas_call | solution.py:115
  657.4 33.4 %reduce-scatter.17.cloned.1.call-done = bf16[256,512]{0,1:T(8,128)(2,1)} async-done(((bf16[2048,512]{0,1:T(8,128)(2,1)}), bf16[256,512]{0,1:T(8,128)(2,1)}) %reduce-scatter.17.cloned.1.call-update) | async-done | bytes 262160 | tf_op jit(solution)/shard_map/reduce_scatter | solution.py:372
  692.6 42.5 %reduce-scatter.21.cloned.1.call-done = bf16[256,512]{0,1:T(8,128)(2,1)} async-done(((bf16[2048,512]{0,1:T(8,128)(2,1)}), bf16[256,512]{0,1:T(8,128)(2,1)}) %reduce-scatter.21.cloned.1.call-update) | async-done | bytes 262160 | tf_op jit(solution)/shard_map/reduce_scatter | solution.py:374
  737.0 72.8 %reduce-scatter.29.cloned.1.call-done = bf16[2048,256]{1,0:T(8,128)(2,1)} async-done(((bf16[2048,2048]{1,0:T(8,128)(2,1)}), bf16[2048,256]{1,0:T(8,128)(2,1)}) %reduce-scatter.29.cloned.1.call-update) | async-done | bytes 1048592 | tf_op jit(solution)/shard_map/reduce_scatter | solution.py:381
  812.5 72.3 %reduce-scatter.25.cloned.1.call-done = bf16[256,2048]{1,0:T(8,128)(2,1)} async-done(((bf16[2048,2048]{1,0:T(8,128)(2,1)}), bf16[256,2048]{1,0:T(8,128)(2,1)}) %reduce-scatter.25.cloned.1.call-update) | async-done | bytes 1048592 | tf_op jit(solution)/shard_map/reduce_scatter | solution.py:379
  887.6 72.1 %reduce-scatter.27.cloned.1.call-done = bf16[256,2048]{1,0:T(8,128)(2,1)} async-done(((bf16[2048,2048]{1,0:T(8,128)(2,1)}), bf16[256,2048]{1,0:T(8,128)(2,1)}) %reduce-scatter.27.cloned.1.call-update) | async-done | bytes 1048592 | tf_op jit(solution)/shard_map/reduce_scatter | solution.py:380
  (333 shorter events, 236.6 us)
Async XLA Ops:
  7.2 47.8 %all-gather.3.cloned.1.call-start = ((), (), s32[]{:S(2)}) async-start(), calls=%async_computation.10 | async-start | bytes 2621440 | tf_op jit(solution)/shard_map/all_gather | solution.py:229
  34.1 45.7 %all-gather.5.cloned.1.call-start = ((), (), s32[]{:S(2)}) async-start(), calls=%async_computation.11 | async-start | bytes 2621440 | tf_op jit(solution)/shard_map/all_gather | solution.py:230
  38.4 444.6 %reduce-scatter.15.cloned.1.call-start = ((), (), s32[]{:S(2)}) async-start(), calls=%async_computation.12 | async-start | bytes 5242880 | tf_op jit(solution)/shard_map/reduce_scatter | solution.py:344
  136.2 62.7 %copy-start.35 = (bf16[4,512,128]{1,2,0:T(8,128)(2,1)}, bf16[4,512,128]{1,2,0:T(8,128)(2,1)S(1)}, u32[]{:S(2)}) copy-start(bf16[4,512,128]{1,2,0:T(8,128)(2,1)S(1)} %divide_convert_fusion) | copy-start | bytes 1572868
  136.2 64.5 %slice-start.2 = ((s8[8388608]{0:T(1024)(128)(4,1)}), s8[4194304]{0:T(1024)(128)(4,1)S(1)}, s32[]{:S(2)}) async-start(s8[8388608]{0:T(1024)(128)(4,1)} %bitcast.260), calls=%async_computation.24 | async-start | bytes 8388608
  139.3 60.1 %copy-start.18 = (bf16[1,512,2048]{2,1,0:T(8,128)(2,1)S(1)}, bf16[1,512,2048]{2,1,0:T(8,128)(2,1)}, u32[]{:S(2)}) copy-start(bf16[1,512,2048]{2,1,0:T(8,128)(2,1)} %param.18) | copy-start | bytes 6291460
  139.3 60.1 %copy-start.39 = (f32[2048]{0:T(1024)S(1)}, f32[2048]{0:T(1024)}, u32[]{:S(2)}) copy-start(f32[2048]{0:T(1024)} %param.27) | copy-start | bytes 24580
  139.4 61.4 %slice-start.3 = ((s8[8388608]{0:T(1024)(128)(4,1)}), s8[4194304]{0:T(1024)(128)(4,1)S(1)}, s32[]{:S(2)}) async-start(s8[8388608]{0:T(1024)(128)(4,1)} %bitcast.260), calls=%async_computation.25 | async-start | bytes 8388608
  223.7 58.1 %copy-start.9 = (bf16[1,512,2048]{2,1,0:T(8,128)(2,1)S(1)}, bf16[1,512,2048]{2,1,0:T(8,128)(2,1)}, u32[]{:S(2)}) copy-start(bf16[1,512,2048]{2,1,0:T(8,128)(2,1)} %param.19) | copy-start | bytes 6291460
  223.7 58.0 %copy-start.40 = (f32[2048]{0:T(1024)S(1)}, f32[2048]{0:T(1024)}, u32[]{:S(2)}) copy-start(f32[2048]{0:T(1024)} %param.31) | copy-start | bytes 24580
  281.2 88.6 %copy-start.1 = (bf16[512,2048]{1,0:T(8,128)(2,1)}, bf16[512,2048]{1,0:T(8,128)(2,1)S(1)}, u32[]{:S(2)}) copy-start(bf16[512,2048]{1,0:T(8,128)(2,1)S(1)} %line_ar_16_8.5) | copy-start | bytes 6291460
  439.2 145.2 %reduce-scatter.23.cloned.1.call-start = ((), (), s32[]{:S(2)}) async-start(), calls=%async_computation.16 | async-start | bytes 2359296 | tf_op jit(solution)/shard_map/reduce_scatter | solution.py:377
  444.4 43.4 %copy-start.29 = (f32[512,64]{0,1:T(8,128)S(1)}, f32[512,64]{0,1:T(8,128)}, u32[]{:S(2)}) copy-start(f32[512,64]{0,1:T(8,128)} %copy-done.28) | copy-start | bytes 393220
  444.4 43.4 %copy-start.31 = (f32[512,64]{0,1:T(8,128)S(1)}, f32[512,64]{0,1:T(8,128)}, u32[]{:S(2)}) copy-start(f32[512,64]{0,1:T(8,128)} %copy-done.30) | copy-start | bytes 393220
  444.4 208.4 %reduce-scatter.33.cloned.1.call-start = ((), (), s32[]{:S(2)}) async-start(), calls=%async_computation.21 | async-start | bytes 73728
  506.4 147.7 %reduce-scatter.31.cloned.1.call-start = ((), (), s32[]{:S(2)}) async-start(), calls=%async_computation.20 | async-start | bytes 73728
  510.1 145.4 %reduce-scatter.19.cloned.1.call-start = ((), (), s32[]{:S(2)}) async-start(), calls=%async_computation.14 | async-start | bytes 2359296 | tf_op jit(solution)/shard_map/reduce_scatter | solution.py:373
  514.5 176.2 %reduce-scatter.17.cloned.1.call-start = ((), (), s32[]{:S(2)}) async-start(), calls=%async_computation.13 | async-start | bytes 2359296 | tf_op jit(solution)/shard_map/reduce_scatter | solution.py:372
  521.1 214.0 %reduce-scatter.21.cloned.1.call-start = ((), (), s32[]{:S(2)}) async-start(), calls=%async_computation.15 | async-start | bytes 2359296 | tf_op jit(solution)/shard_map/reduce_scatter | solution.py:374
  525.4 284.4 %reduce-scatter.29.cloned.1.call-start = ((), (), s32[]{:S(2)}) async-start(), calls=%async_computation.19 | async-start | bytes 9437184 | tf_op jit(solution)/shard_map/reduce_scatter | solution.py:381
  536.6 348.2 %reduce-scatter.25.cloned.1.call-start = ((), (), s32[]{:S(2)}) async-start(), calls=%async_computation.17 | async-start | bytes 9437184 | tf_op jit(solution)/shard_map/reduce_scatter | solution.py:379
  546.9 412.8 %reduce-scatter.27.cloned.1.call-start = ((), (), s32[]{:S(2)}) async-start(), calls=%async_computation.18 | async-start | bytes 9437184 | tf_op jit(solution)/shard_map/reduce_scatter | solution.py:380
  591.1 58.4 %copy-start.3 = (bf16[512,2048]{1,0:T(8,128)(2,1)S(1)}, bf16[512,2048]{1,0:T(8,128)(2,1)}, u32[]{:S(2)}) copy-start(bf16[512,2048]{1,0:T(8,128)(2,1)} %copy-done.2) | copy-start | bytes 6291460
  591.2 58.4 %copy-start.10 = (bf16[1,512,2048]{2,1,0:T(8,128)(2,1)S(1)}, bf16[1,512,2048]{2,1,0:T(8,128)(2,1)}, u32[]{:S(2)}) copy-start(bf16[1,512,2048]{2,1,0:T(8,128)(2,1)} %param.19) | copy-start | bytes 6291460
  (63 other events, 360.6 us)
Sparse Core Ops, SparseCore 0:
  34.2 20.7 all-gather.2
  57.2 22.5 all-gather.4
  439.3 43.6 reduce-scatter.14
  486.2 41.1 reduce-scatter.22
  530.2 33.5 reduce-scatter.32
  567.2 33.5 reduce-scatter.30
  604.6 41.1 reduce-scatter.18
  649.6 41.0 reduce-scatter.16
  694.0 41.0 reduce-scatter.20
  738.5 71.2 reduce-scatter.28
  813.3 71.4 reduce-scatter.24
  888.1 71.5 reduce-scatter.26

commit v2 on v0

--- a/solution.py
+++ b/solution.py
@@ -2,6 +2,550 @@
 import jax.numpy as jnp
 from jax import lax
 from jax.sharding import PartitionSpec as P
+from jax.experimental import pallas as pl
+from jax.experimental.pallas import tpu as pltpu
+
+MESH = pl.DeviceIdType.MESH
+bf16 = jnp.bfloat16
+f32 = jnp.float32
+lanes = 128
+row_blocks = 16
+row_chains = 8
+
+
+def remote(src, dst, send, recv, where):
+    return pltpu.make_async_remote_copy(
+        src, dst, send, recv, device_id=where, device_id_type=MESH
+    )
+
+
+class LineSum:
+    def __init__(self, n, rows, width):
+        self.n, self.rows, self.width = n, rows, width
+        self.part = width // n
+        self.rc = rows // row_blocks
+        self.total = row_blocks // row_chains * n
+        self.steps = self.total + n - 1
+
+    def scratch(self):
+        shape = (self.n, self.rows, self.part)
+        return [pltpu.VMEM(shape, bf16)] * 4 + [
+            pltpu.SemaphoreType.DMA((row_chains, self.total))
+        ] * 4
+
+    def bind(self, refs):
+        self.own, self.from_l, self.from_r, self.res = refs[:4]
+        self.send_r, self.send_l, self.recv_l, self.recv_r = refs[4:]
+        self.i = lax.axis_index("tp")
+        self.has_l, self.has_r = self.i > 0, self.i < self.n - 1
+
+    def greet(self, bar):
+        @pl.when(self.has_l)
+        def _():
+            pl.semaphore_signal(bar, inc=1, device_id={"tp": self.i - 1}, device_id_type=MESH)
+
+        @pl.when(self.has_r)
+        def _():
+            pl.semaphore_signal(bar, inc=1, device_id={"tp": self.i + 1}, device_id_type=MESH)
+
+        return self.has_l.astype(jnp.int32) + self.has_r.astype(jnp.int32)
+
+    def load(self, x_ref):
+        for j in range(self.n):
+            self.own[j] = x_ref[:, j * self.part : (j + 1) * self.part]
+
+    def rows_of(self, g, p):
+        block = (p // self.n) * row_chains + g
+        return pl.ds(pl.multiple_of(block * self.rc, self.rc), self.rc)
+
+    def right(self, src, dst, g, p, j):
+        sl = self.rows_of(g, p)
+        return remote(
+            src.at[j, sl], dst.at[j, sl], self.send_r.at[g, p], self.recv_l.at[g, p],
+            {"tp": self.i + 1},
+        )
+
+    def left(self, src, dst, g, q, j):
+        sl = self.rows_of(g, q)
+        return remote(
+            src.at[j, sl], dst.at[j, sl], self.send_l.at[g, q], self.recv_r.at[g, q],
+            {"tp": self.i - 1},
+        )
+
+    def wait_l(self, g, p, j):
+        sl = self.rows_of(g, p)
+        remote(
+            self.own.at[j, sl], self.from_l.at[j, sl], self.send_r.at[g, p], self.recv_l.at[g, p],
+            {"tp": self.i - 1},
+        ).wait_recv()
+
+    def wait_r(self, g, q, j):
+        sl = self.rows_of(g, q)
+        remote(
+            self.own.at[j, sl], self.from_r.at[j, sl], self.send_l.at[g, q], self.recv_r.at[g, q],
+            {"tp": self.i + 1},
+        ).wait_recv()
+
+    def step(self, t):
+        n, i, has_l, has_r = self.n, self.i, self.has_l, self.has_r
+        own, from_l, from_r, res = self.own, self.from_l, self.from_r, self.res
+        for g in range(row_chains):
+            p = t - i
+            q = t - (n - 1 - i)
+            jr = n - 1 - lax.rem(p + n * self.total, n)
+            jl = lax.rem(q + n * self.total, n)
+            pv = (p >= 0) & (p < self.total)
+            qv = (q >= 0) & (q < self.total)
+
+            @pl.when(pv & has_l)
+            def _():
+                self.wait_l(g, p, jr)
+
+            @pl.when(qv & has_r)
+            def _():
+                self.wait_r(g, q, jl)
+
+            @pl.when(pv & (jr > i))
+            def _():
+                sl = self.rows_of(g, p)
+
+                @pl.when(has_l)
+                def _():
+                    own[jr, sl] = (own[jr, sl].astype(f32) + from_l[jr, sl].astype(f32)).astype(bf16)
+
+                self.right(own, from_l, g, p, jr).start()
+
+            @pl.when(qv & (jl < i))
+            def _():
+                sl = self.rows_of(g, q)
+
+                @pl.when(has_r)
+                def _():
+                    own[jl, sl] = (own[jl, sl].astype(f32) + from_r[jl, sl].astype(f32)).astype(bf16)
+
+                self.left(own, from_r, g, q, jl).start()
+
+            @pl.when(pv & (jr == i))
+            def _():
+                sl = self.rows_of(g, p)
+
+                @pl.when(has_l & has_r)
+                def _():
+                    res[i, sl] = (
+                        own[i, sl].astype(f32) + from_l[i, sl].astype(f32) + from_r[i, sl].astype(f32)
+                    ).astype(bf16)
+
+                @pl.when(jnp.logical_not(has_l))
+                def _():
+                    res[i, sl] = (own[i, sl].astype(f32) + from_r[i, sl].astype(f32)).astype(bf16)
+
+                @pl.when(jnp.logical_not(has_r))
+                def _():
+                    res[i, sl] = (own[i, sl].astype(f32) + from_l[i, sl].astype(f32)).astype(bf16)
+
+            @pl.when(pv & (jr <= i) & has_r)
+            def _():
+                self.right(res, res, g, p, jr).start()
+
+            @pl.when(qv & (jl >= i) & has_l)
+            def _():
+                self.left(res, res, g, q, jl).start()
+
+    def drain(self):
+        def one(p, carry):
+            for g in range(row_chains):
+
+                @pl.when(self.has_r)
+                def _():
+                    self.right(self.own, self.from_l, g, p, 0).wait_send()
+
+                @pl.when(self.has_l)
+                def _():
+                    self.left(self.own, self.from_r, g, p, 0).wait_send()
+
+            return carry
+
+        lax.fori_loop(0, self.total, one, 0)
+
+    def store(self, out_ref):
+        for j in range(self.n):
+            out_ref[:, j * self.part : (j + 1) * self.part] = self.res[j]
+
+
+class GradScatter:
+    def __init__(self, n_ctx, n_seq, width, jobs):
+        self.nx, self.ny = n_ctx // 2, n_seq
+        self.rows = width // (n_ctx * n_seq)
+        self.jobs = jobs
+        start = 0
+        self.spans = []
+        for job in jobs:
+            self.spans.append((start, start + job["count"]))
+            start += job["count"]
+        self.total = start
+        self.steps = start + 5
+
+    def scratch(self):
+        nx, ny, r, t = self.nx, self.ny, self.rows, self.total
+        tile = (r, lanes)
+        sem = pltpu.SemaphoreType.DMA
+        return [
+            pltpu.VMEM((2, nx, ny, 2) + tile, bf16),
+            pltpu.VMEM((2, nx, ny, 2) + tile, f32),
+            pltpu.VMEM((t, nx, ny, 2) + tile, bf16),
+            pltpu.VMEM((3, nx, ny) + tile, bf16),
+            pltpu.VMEM((3, ny, nx) + tile, bf16),
+            pltpu.VMEM((t, nx - 1, ny) + tile, bf16),
+            pltpu.VMEM((t, ny - 1, nx) + tile, bf16),
+            pltpu.VMEM((3, ny) + tile, bf16),
+            pltpu.VMEM((3, nx) + tile, bf16),
+            pltpu.VMEM((t, ny - 1) + tile, bf16),
+            pltpu.VMEM((t, nx - 1) + tile, bf16),
+            sem((2,)), sem((t,)),
+            sem((3, nx - 1)), sem((t, nx - 1)), sem((3, ny - 1)), sem((t, ny - 1)),
+            sem((3, ny - 1)), sem((t, ny - 1)), sem((3, nx - 1)), sem((t, nx - 1)),
+        ]
+
+    def bind(self, refs, at_refs, b_refs, out_refs):
+        (self.send0, self.keep, self.recv0, self.pa, self.pb, self.r1a, self.r1b, self.qa, self.qb,
+         self.r2a, self.r2b, self.s0, self.d0, self.s1a, self.d1a, self.s1b, self.d1b,
+         self.s2a, self.d2a, self.s2b, self.d2b) = refs
+        self.at_refs, self.b_refs, self.out_refs = at_refs, b_refs, out_refs
+        ctx = lax.axis_index("ctx")
+        self.mx, self.core, self.my = ctx // 2, lax.rem(ctx, 2), lax.axis_index("seq")
+
+    def at_x(self, d):
+        return {"ctx": lax.rem(self.mx + d, self.nx) * 2 + self.core}
+
+    def at_y(self, d):
+        return {"seq": lax.rem(self.my + d, self.ny)}
+
+    def at_mate(self):
+        return {"ctx": self.mx * 2 + 1 - self.core}
+
+    def greet(self, bar):
+        places = [self.at_mate()]
+        places += [self.at_x(d) for d in range(1, self.nx)]
+        places += [self.at_y(d) for d in range(1, self.ny)]
+        for place in places:
+            pl.semaphore_signal(bar, inc=1, device_id=place, device_id_type=MESH)
+        return len(places)
+
+    def c0(self, c, slot):
+        return remote(self.send0.at[slot], self.recv0.at[c], self.s0.at[slot], self.d0.at[c], self.at_mate())
+
+    def c1a(self, c, slot, d):
+        return remote(
+            self.pa.at[slot, lax.rem(self.mx + d, self.nx)], self.r1a.at[c, d - 1],
+            self.s1a.at[slot, d - 1], self.d1a.at[c, d - 1], self.at_x(d),
+        )
+
+    def c1b(self, c, slot, d):
+        return remote(
+            self.pb.at[slot, lax.rem(self.my + d, self.ny)], self.r1b.at[c, d - 1],
+            self.s1b.at[slot, d - 1], self.d1b.at[c, d - 1], self.at_y(d),
+        )
+
+    def c2a(self, c, slot, d):
+        return remote(
+            self.qa.at[slot, lax.rem(self.my + d, self.ny)], self.r2a.at[c, d - 1],
+            self.s2a.at[slot, d - 1], self.d2a.at[c, d - 1], self.at_y(d),
+        )
+
+    def c2b(self, c, slot, d):
+        return remote(
+            self.qb.at[slot, lax.rem(self.mx + d, self.nx)], self.r2b.at[c, d - 1],
+            self.s2b.at[slot, d - 1], self.d2b.at[c, d - 1], self.at_x(d),
+        )
+
+    def make(self, c):
+        slot = lax.rem(c, 2)
+        nx, ny, r = self.nx, self.ny, self.rows
+
+        @pl.when(c >= 2)
+        def _():
+            self.c0(c, slot).wait_send()
+
+        def products(at_ref, b_ref, col, parity, write):
+            def tile(e, carry):
+                x, y = e // ny, lax.rem(e, ny)
+                row = pl.multiple_of(((x * 2 + parity) * ny + y) * r, r)
+                acc = jnp.dot(
+                    at_ref[pl.ds(row, r), :], b_ref[:, pl.ds(col, 2 * lanes)],
+                    preferred_element_type=f32,
+                )
+                write(x, y, acc)
+                return carry
+
+            lax.fori_loop(0, nx * ny, tile, 0)
+
+        def to_send(x, y, acc):
+            self.send0[slot, x, y, 0] = acc[:, :lanes].astype(bf16)
+            self.send0[slot, x, y, 1] = acc[:, lanes:].astype(bf16)
+
+        def to_keep(x, y, acc):
+            self.keep[slot, x, y, 0] = acc[:, :lanes]
+            self.keep[slot, x, y, 1] = acc[:, lanes:]
+
+        for job, (lo, hi) in zip(self.jobs, self.spans):
+
+            @pl.when((c >= lo) & (c < hi))
+            def _():
+                at_ref, b_ref = self.at_refs[job["a"]], self.b_refs[job["b"]]
+                col = pl.multiple_of((c - lo + job["first"]) * (2 * lanes), 2 * lanes)
+                products(at_ref, b_ref, col, 1 - self.core, to_send)
+                self.c0(c, slot).start()
+                products(at_ref, b_ref, col, self.core, to_keep)
+
+    def pair(self, c):
+        slot = lax.rem(c, 3)
+        nx, ny = self.nx, self.ny
+
+        @pl.when(c >= 3)
+        def _():
+            for d in range(1, nx):
+                self.c1a(c, slot, d).wait_send()
+            for d in range(1, ny):
+                self.c1b(c, slot, d).wait_send()
+
+        self.c0(c, lax.rem(c, 2)).wait_recv()
+        for x in range(nx):
+            for y in range(ny):
+                self.pa[slot, x, y] = (
+                    self.keep[lax.rem(c, 2), x, y, 0] + self.recv0[c, x, y, 0].astype(f32)
+                ).astype(bf16)
+        for d in range(1, nx):
+            self.c1a(c, slot, d).start()
+        for x in range(nx):
+            for y in range(ny):
+                self.pb[slot, y, x] = (
+                    self.keep[lax.rem(c, 2), x, y, 1] + self.recv0[c, x, y, 1].astype(f32)
+                ).astype(bf16)
+        for d in range(1, ny):
+            self.c1b(c, slot, d).start()
+
+    def cross(self, c):
+        slot = lax.rem(c, 3)
+        nx, ny = self.nx, self.ny
+
+        @pl.when(c >= 3)
+        def _():
+            for d in range(1, ny):
+                self.c2a(c, slot, d).wait_send()
+            for d in range(1, nx):
+                self.c2b(c, slot, d).wait_send()
+
+        for d in range(1, nx):
+            self.c1a(c, slot, d).wait_recv()
+        for y in range(ny):
+            acc = self.pa[slot, self.mx, y].astype(f32)
+            for d in range(1, nx):
+                acc = acc + self.r1a[c, d - 1, y].astype(f32)
+            self.qa[slot, y] = acc.astype(bf16)
+        for d in range(1, ny):
+            self.c2a(c, slot, d).start()
+        for d in range(1, ny):
+            self.c1b(c, slot, d).wait_recv()
+        for x in range(nx):
+            acc = self.pb[slot, self.my, x].astype(f32)
+            for d in range(1, ny):
+                acc = acc + self.r1b[c, d - 1, x].astype(f32)
+            self.qb[slot, x] = acc.astype(bf16)
+        for d in range(1, nx):
+            self.c2b(c, slot, d).start()
+
+    def finish(self, c):
+        slot = lax.rem(c, 3)
+        nx, ny = self.nx, self.ny
+        for d in range(1, ny):
+            self.c2a(c, slot, d).wait_recv()
+        for d in range(1, nx):
+            self.c2b(c, slot, d).wait_recv()
+        for job, (lo, hi) in zip(self.jobs, self.spans):
+
+            @pl.when((c >= lo) & (c < hi))
+            def _():
+                out_ref = self.out_refs[job["out"]]
+                col = pl.multiple_of((c - lo + job["place"]) * (2 * lanes), 2 * lanes)
+                acc = self.qa[slot, self.my].astype(f32)
+                for d in range(1, ny):
+                    acc = acc + self.r2a[c, d - 1].astype(f32)
+                out_ref[:, pl.ds(col, lanes)] = acc
+                acc = self.qb[slot, self.mx].astype(f32)
+                for d in range(1, nx):
+                    acc = acc + self.r2b[c, d - 1].astype(f32)
+                out_ref[:, pl.ds(col + lanes, lanes)] = acc
+
+    def early(self, it):
+        @pl.when((it >= 5) & (it < self.total + 5))
+        def _():
+            self.finish(it - 5)
+
+        @pl.when((it >= 3) & (it < self.total + 3))
+        def _():
+            self.cross(it - 3)
+
+        @pl.when((it >= 1) & (it < self.total + 1))
+        def _():
+            self.pair(it - 1)
+
+    def late(self, it):
+        @pl.when(it < self.total)
+        def _():
+            self.make(it)
+
+    def drain(self):
+        for c in range(max(self.total - 2, 0), self.total):
+            self.c0(c, c % 2).wait_send()
+        for c in range(max(self.total - 3, 0), self.total):
+            slot = c % 3
+            for d in range(1, self.nx):
+                self.c1a(c, slot, d).wait_send()
+                self.c2b(c, slot, d).wait_send()
+            for d in range(1, self.ny):
+                self.c1b(c, slot, d).wait_send()
+                self.c2a(c, slot, d).wait_send()
+
+
+class GainSum:
+    def __init__(self, n_ctx, n_seq):
+        self.ny, self.n = n_seq, n_ctx * n_seq
+
+    def scratch(self):
+        sem = pltpu.SemaphoreType.DMA
+        return [pltpu.VMEM((self.n - 1, 8, lanes), f32), sem((self.n - 1,)), sem((self.n - 1,))]
+
+    def bind(self, refs, in_ref, out_ref):
+        self.got, self.sent, self.done = refs
+        self.in_ref, self.out_ref = in_ref, out_ref
+        self.me = lax.axis_index("ctx") * self.ny + lax.axis_index("seq")
+
+    def place(self, d):
+        to = lax.rem(self.me + d, self.n)
+        return to, {"ctx": to // self.ny, "seq": lax.rem(to, self.ny)}
+
+    def copy(self, d):
+        to, where = self.place(d)
+        return remote(self.in_ref.at[to], self.got.at[d - 1], self.sent.at[d - 1], self.done.at[d - 1], where)
+
+    def greet(self, bar):
+        for d in range(1, self.n):
+            pl.semaphore_signal(bar, inc=1, device_id=self.place(d)[1], device_id_type=MESH)
+        return self.n - 1
+
+    def start(self):
+        for d in range(1, self.n):
+            self.copy(d).start()
+
+    def finish(self):
+        acc = self.in_ref[self.me]
+        for d in range(1, self.n):
+            self.copy(d).wait_recv()
+            acc = acc + self.got[d - 1]
+        self.out_ref[...] = acc
+        for d in range(1, self.n):
+            self.copy(d).wait_send()
+
+
+def vmem_spec():
+    return pl.BlockSpec(memory_space=pltpu.VMEM)
+
+
+def comm_call(body, args, outs, scratch, cid, name):
+    return pl.pallas_call(
+        body,
+        out_shape=outs,
+        in_specs=[vmem_spec()] * len(args),
+        out_specs=[vmem_spec()] * len(outs),
+        scratch_shapes=scratch,
+        compiler_params=pltpu.CompilerParams(
+            collective_id=cid, has_side_effects=True, vmem_limit_bytes=62 * 2**20
+        ),
+        name=name,
+    )(*args)
+
+
+def tp_sum(partial, cid):
+    rows, width = partial.shape
+    line = LineSum(lax.axis_size("tp"), rows, width)
+
+    def body(x_ref, out_ref, *refs):
+        line.bind(refs)
+        bar = pltpu.get_barrier_semaphore()
+        peers = line.greet(bar)
+        line.load(x_ref)
+        pl.semaphore_wait(bar, peers)
+
+        def one(t, carry):
+            line.step(t)
+            return carry
+
+        lax.fori_loop(0, line.steps, one, 0)
+        line.drain()
+        line.store(out_ref)
+
+    out = jax.ShapeDtypeStruct((rows, width), bf16)
+    (summed,) = comm_call(body, [partial.astype(bf16)], [out], line.scratch(), cid, "tp_sum")
+    return summed.astype(f32)
+
+
+def sum_and_scatter(partial, ats, bs, jobs, out_widths, cid, gains=None):
+    rows, width = partial.shape
+    n_ctx, n_seq = lax.axis_size("ctx"), lax.axis_size("seq")
+    line = LineSum(lax.axis_size("tp"), rows, width)
+    grads = GradScatter(n_ctx, n_seq, width, jobs)
+    small = GainSum(n_ctx, n_seq)
+    small_in = [] if gains is None else [gains]
+    na, nb, no, ns = len(ats), len(bs), len(out_widths), len(small_in)
+    n_line, n_grads = len(line.scratch()), len(grads.scratch())
+
+    def body(x_ref, *refs):
+        at_refs, b_refs = refs[:na], refs[na : na + nb]
+        refs = refs[na + nb :]
+        small_refs, refs = refs[:ns], refs[ns:]
+        out_ref, grad_refs, refs = refs[0], refs[1 : 1 + no], refs[1 + no :]
+        small_out, scratch = refs[:ns], refs[ns:]
+        line.bind(scratch[:n_line])
+        grads.bind(scratch[n_line : n_line + n_grads], at_refs, b_refs, grad_refs)
+        bar = pltpu.get_barrier_semaphore()
+        peers = line.greet(bar)
+        if ns:
+            small.bind(scratch[n_line + n_grads :], small_refs[0], small_out[0])
+            peers = peers + small.greet(bar)
+        else:
+            peers = peers + grads.greet(bar)
+        line.load(x_ref)
+        pl.semaphore_wait(bar, peers)
+        if ns:
+            small.start()
+
+        def one(it, carry):
+            grads.early(it)
+
+            @pl.when(it < line.steps)
+            def _():
+                line.step(it)
+
+            grads.late(it)
+            return carry
+
+        lax.fori_loop(0, max(line.steps, grads.steps), one, 0)
+        if ns:
+            small.finish()
+        line.drain()
+        grads.drain()
+        line.store(out_ref)
+
+    outs = [jax.ShapeDtypeStruct((rows, width), bf16)] + [
+        jax.ShapeDtypeStruct((grads.rows, w), f32) for w in out_widths
+    ]
+    outs += [jax.ShapeDtypeStruct((8, lanes), f32)] * ns
+    res = comm_call(
+        body, [partial.astype(bf16)] + list(ats) + list(bs) + small_in, outs,
+        line.scratch() + grads.scratch() + (small.scratch() if ns else []), cid, "sum_and_scatter",
+    )
+    return res[0].astype(f32), res[1:]
+
 
 norm_eps = 1e-06
 rope_base = 500000.0
@@ -136,7 +680,7 @@
     log_total = peak + jnp.log(total)
     mixed = (accum / total[:, :, None]).astype(jnp.bfloat16)
     attn_flat = mixed.transpose(1, 0, 2).reshape(row_count, local)
-    proj = lax.psum(matmul(attn_flat, w_output), "tp")
+    proj = tp_sum(matmul(attn_flat, w_output), 1)
     attn_scale = lax.rsqrt(jnp.mean(proj * proj, axis=1) + norm_eps)
     attn_norm = proj * attn_scale[:, None]
     resid = inputs + attn_norm * attn_gain
@@ -146,7 +690,7 @@
     sigma = jax.nn.sigmoid(gate)
     active = gate * sigma
     inner = (active * up).astype(jnp.bfloat16)
-    down = lax.psum(matmul(inner, w_down), "tp")
+    down = tp_sum(matmul(inner, w_down), 2)
     mlp_scale = lax.rsqrt(jnp.mean(down * down, axis=1) + norm_eps)
     mlp_norm = down * mlp_scale[:, None]
     block_out = resid + mlp_norm * mlp_gain
@@ -157,20 +701,30 @@
         mlp_scale[:, None]
         * (d_mnorm - mlp_norm * jnp.mean(d_mnorm * mlp_norm, axis=1, keepdims=True))
     ).astype(jnp.bfloat16)
-    grad_down = matmul(inner.T, d_down)
     d_inner = matmul(d_down, w_down.T)
     d_gate = (d_inner * up * sigma * (1.0 + gate * (1.0 - sigma))).astype(jnp.bfloat16)
     d_up = (d_inner * active).astype(jnp.bfloat16)
-    grad_gate = matmul(hidden.T, d_gate)
-    grad_up = matmul(hidden.T, d_up)
-    d_resid = upstream + lax.psum(matmul(d_gate, w_gate.T) + matmul(d_up, w_up.T), "tp")
+    hidden_t = hidden.T
+    wide = inner.shape[1] // (2 * lanes)
+    half = wide // 2
+    back, (grad_down, grad_gate_a) = sum_and_scatter(
+        matmul(d_gate, w_gate.T) + matmul(d_up, w_up.T),
+        [d_down.T, hidden_t],
+        [inner, d_gate],
+        [
+            dict(a=0, b=0, first=0, count=wide, out=0, place=0),
+            dict(a=1, b=1, first=0, count=half, out=1, place=0),
+        ],
+        [inner.shape[1], half * 2 * lanes],
+        3,
+    )
+    d_resid = upstream + back
     d_attn_gain = jnp.sum(d_resid * attn_norm, axis=0)
     d_anorm = d_resid * attn_gain
     d_proj = (
         attn_scale[:, None]
         * (d_anorm - attn_norm * jnp.mean(d_anorm * attn_norm, axis=1, keepdims=True))
     ).astype(jnp.bfloat16)
-    grad_output = matmul(attn_flat.T, d_proj)
     d_attn = matmul(d_proj, w_output.T).astype(jnp.bfloat16)
     d_attn_heads = d_attn.reshape(row_count, heads, head_dim)
     delta = jnp.sum(
@@ -217,8 +771,9 @@
 
     d_qrot, kv_terms = lax.scan(back_block, zero_grads, (key_blocks, value_blocks, pos_blocks))
     kv_grads = lax.psum_scatter(
-        kv_terms.reshape(count, 2 * local), "ctx", scatter_dimension=0, tiled=True
-    )
+        kv_terms.reshape(count, 2 * local).astype(jnp.bfloat16), "ctx", scatter_dimension=0, tiled=True
+    )
+    kv_grads = kv_grads.astype(jnp.float32)
     d_krot = kv_grads[:, :local].reshape(row_count, heads, head_dim)
     d_value = kv_grads[:, local:].astype(jnp.bfloat16)
     d_qhead = unrotate(d_qrot, cosine, sine).reshape(row_count, local)
@@ -236,24 +791,52 @@
     d_key = (key_scale[:, None] * (d_knorm - key_norm * (key_dot / width)[:, None])).astype(
         jnp.bfloat16
     )
-    grad_query = matmul(inputs_bf.T, d_query)
-    grad_key = matmul(inputs_bf.T, d_key)
-    grad_value = matmul(inputs_bf.T, d_value)
-    input_grad = d_resid + lax.psum(
-        matmul(d_query, w_query.T) + matmul(d_key, w_key.T) + matmul(d_value, w_value.T), "tp"
-    )
+    thin = local // (2 * lanes)
+    owners = lax.axis_size("ctx") * lax.axis_size("seq")
+    pieces = [
+        d_attn_gain.reshape(owners, -1),
+        d_mlp_gain.reshape(owners, -1),
+        d_query_gain.reshape(heads, owners, -1).transpose(1, 0, 2).reshape(owners, -1),
+        d_key_gain.reshape(heads, owners, -1).transpose(1, 0, 2).reshape(owners, -1),
+    ]
+    cuts = [piece.shape[1] for piece in pieces]
+    packed = jnp.concatenate(pieces, axis=1)
+    packed = jnp.pad(packed, ((0, 0), (0, 8 * lanes - packed.shape[1]))).reshape(owners, 8, lanes)
+    back, (grad_gate_b, grad_up, grad_qkv, grad_output, small) = sum_and_scatter(
+        matmul(d_query, w_query.T) + matmul(d_key, w_key.T) + matmul(d_value, w_value.T),
+        [hidden_t, inputs_bf.T, d_proj.T],
+        [d_gate, d_up, d_query, d_key, d_value, attn_flat],
+        [
+            dict(a=0, b=0, first=half, count=wide - half, out=0, place=0),
+            dict(a=0, b=1, first=0, count=wide, out=1, place=0),
+            dict(a=2, b=5, first=0, count=thin, out=3, place=0),
+            dict(a=1, b=2, first=0, count=thin, out=2, place=0),
+            dict(a=1, b=3, first=0, count=thin, out=2, place=thin),
+            dict(a=1, b=4, first=0, count=thin, out=2, place=2 * thin),
+        ],
+        [(wide - half) * 2 * lanes, inner.shape[1], 3 * local, local],
+        4,
+        packed,
+    )
+    small = small.reshape(-1)
+    g_attn, g_mlp, g_query, g_key = jnp.split(
+        small[: sum(cuts)], [cuts[0], cuts[0] + cuts[1], cuts[0] + cuts[1] + cuts[2]]
+    )
+    input_grad = d_resid + back
+    grad_query, grad_key, grad_value = jnp.split(grad_qkv, 3, axis=1)
+    grad_gate = jnp.concatenate([grad_gate_a, grad_gate_b], axis=1)
     summed = (
-        lax.psum_scatter(grad_query, ("ctx", "seq"), scatter_dimension=0, tiled=True),
-        lax.psum_scatter(grad_key, ("ctx", "seq"), scatter_dimension=0, tiled=True),
-        lax.psum_scatter(grad_value, ("ctx", "seq"), scatter_dimension=0, tiled=True),
-        lax.psum_scatter(d_query_gain, ("ctx", "seq"), scatter_dimension=1, tiled=True),
-        lax.psum_scatter(d_key_gain, ("ctx", "seq"), scatter_dimension=1, tiled=True),
-        lax.psum_scatter(grad_output, ("ctx", "seq"), scatter_dimension=1, tiled=True),
-        lax.psum_scatter(d_attn_gain, ("ctx", "seq"), scatter_dimension=0, tiled=True),
-        lax.psum_scatter(grad_gate, ("ctx", "seq"), scatter_dimension=0, tiled=True),
-        lax.psum_scatter(grad_up, ("ctx", "seq"), scatter_dimension=0, tiled=True),
-        lax.psum_scatter(grad_down, ("ctx", "seq"), scatter_dimension=1, tiled=True),
-        lax.psum_scatter(d_mlp_gain, ("ctx", "seq"), scatter_dimension=0, tiled=True),
+        grad_query,
+        grad_key,
+        grad_value,
+        g_query.reshape(heads, -1),
+        g_key.reshape(heads, -1),
+        grad_output.T,
+        g_attn,
+        grad_gate,
+        grad_up,
+        grad_down.T,
+        g_mlp,
     )
     return (
         block_out[None],

time: 1620 us -> 676 us (0.42)
  waiting for transfers between devices: 1220 us -> 40.2 us
  Pallas kernels: 0 us -> 331 us
  matrix products: 191 us -> 124 us
  blocking collectives: 50.6 us -> 25.2 us
    reduce_scatter x8 -> x1, waiting for transfers between devices: 634 us -> 35.2 us  [per_device(): lax.psum_scatter(kv_terms.reshape(count, 2 * local).astype(jnp.bfloat16),...]
    psum x4 -> x0, waiting for transfers between devices: 566 us -> none  [the longest x1 155 us: per_device(): proj = lax.psum(matmul(attn_flat, w_output), 'tp')]
    pallas_call x0 -> x4, Pallas kernels: none -> 331 us  [comm_call(): pl.pallas_call(body, out_shape=outs, in_specs=[vmem_spec()] * len(args),...]
    dot_general x21 -> x14, matrix products: 141 us -> 73.8 us  [matmul(): return jnp.dot(left, right, preferred_element_type=jnp.float32)]
    unnamed x1 -> x0, blocking collectives: 25.2 us -> none
    dynamic_update_slice x8 -> x0, local copies, waits for them, and re-layouts: 24.5 us -> none  [per_device(): lax.scan(back_block, zero_grads, (key_blocks, value_blocks, pos_blocks))]
    unnamed x97 -> x113, local copies, waits for them, and re-layouts: 27.4 us -> 37.6 us
  transfers between devices with their start and end apart: 16 -> 3, of which waited for: 13 -> 2; matrix products, arithmetic and copies ran while one was open for 7% -> 6% of each run, Pallas kernels for 0% -> 0%
where the time goes in v2:
time: 676 us; the launch traced here: 669 us
  Pallas kernels  331 us (49%)
  matrix products  124 us (18%)
  local copies, waits for them, and re-layouts  81.7 us (12%)
  other arithmetic  51.8 us (8%)
  waiting for transfers between devices  40.2 us (6%)
  blocking collectives  25.2 us (4%)
  between operations  14.8 us (2%)
    pallas_call x4, Pallas kernels, comm_call(): pl.pallas_call(body, out_shape=outs, in_specs=[vmem_spec()] * len(args),...  331 us
    dot_general x14, matrix products, matmul(): return jnp.dot(left, right, preferred_element_type=jnp.float32)  73.8 us
    unnamed x113, local copies, waits for them, and re-layouts  37.6 us
    reduce_scatter x1, waiting for transfers between devices, per_device(): lax.psum_scatter(kv_terms.reshape(count, 2 * local).astype(jnp.bfloat16),...  35.2 us
    pallas_call x4, local copies, waits for them, and re-layouts, comm_call(): pl.pallas_call(body, out_shape=outs, in_specs=[vmem_spec()] * len(args),...  15.1 us
  transfers between devices with their start and end apart: 3, of which 2 were waited for; matrix products, arithmetic and copies ran while one was open for 6% of the time, Pallas kernels for 0%

profile of v2, /device:TPU:0, one launch (start us, length us, event | category | flops | bytes accessed | tf_op | source)
XLA Modules:
  0.0 668.6 jit_solution(10631812530655657009)
XLA Ops:
  7.2 4.4 fusion.77
  19.3 13.5 %all-reduce.2 = (f32[512]{0:T(512)S(1)}, f32[512]{0:T(512)S(1)}) all-reduce(f32[512]{0:T(512)S(1)} %get-tuple-element.426, f32[512]{0:T(512)S(1)} %get-tuple-element.428), channel_id=1, replica_groups=mesh['ctx'=4,'seq'=2,'tp'=4] {'tp'}, use_global_device_ids=true, to_apply=%region_1.2 | all-reduce | flops 1024 | bytes 8192 | tf_op jit(solution)/shard_map/psum | solution.py:627
  57.3 4.9 all-gather.3.cloned.1.call-done
  69.5 23.4 %while.28 = (s32[]{:T(128)}, f32[4,512]{1,0:T(4,128)S(1)}, f32[4,512]{1,0:T(4,128)S(1)}, f32[4,512,128]{2,1,0:T(8,128)S(1)}, s32[4,512]{1,0:T(4,128)S(1)}, /*ind...) while((s32[]{:T(128)}, f32[4,512]{1,0:T(4,128)S(1)}, ...), condition=%wide.region_9.10_spmd.clone, body=%wide.region_6.9_spmd.clone.sunk | while | flops 549464064 | bytes 17440908 | solution.py:678
  94.3 4.2 convolution_convert_fusion.1.x_ref
  98.5 62.5 %tp_sum.2 = bf16[512,2048]{1,0:T(8,128)(2,1)} custom-call(bf16[512,2048]{1,0:T(8,128)(2,1)} %convolution_convert_fusion.1.x_ref), custom_call_target="tpu_custom_call" | custom-call | tf_op jit(solution)/shard_map/tp_sum/pallas_call | solution.py:455
  167.1 7.7 %fusion.101 = f32[512,2048]{1,0:T(8,128)S(1)} fusion(bf16[512,2048]{0,1:T(8,128)(2,1)S(1)} %fusion.70, bf16[2048,2048]{1,0:T(8,128)(2,1)} %param.28), kind=kOutput, calls=%fused_computation.188 | convolution fusion | flops 4294967296 | bytes 14680064 | tf_op jit(solution)/shard_map/dot_general | solution.py:556
  174.8 6.5 multiply_convert_fusion.2
  182.6 5.8 convolution_convert_fusion.x_ref
  188.4 60.6 %tp_sum.3 = bf16[512,2048]{1,0:T(8,128)(2,1)} custom-call(bf16[512,2048]{1,0:T(8,128)(2,1)} %convolution_convert_fusion.x_ref), custom_call_target="tpu_custom_call" | custom-call | tf_op jit(solution)/shard_map/tp_sum/pallas_call | solution.py:455
  249.0 4.1 copy.159
  260.9 13.1 %multiply_convert_fusion = (bf16[512,2048]{1,0:T(8,128)(2,1)}, bf16[512,2048]{1,0:T(8,128)(2,1)}) fusion(f32[512,2048]{1,0:T(8,128)} %copy-done.47, f32[512,2048]{1,0:T(8,128)} %get-tuple-element.431, bf16[2048,2048]{1,0:T(8,128)(2,1)} %param.30, bf16[512,2048]{0,1:T(8,128)(2,1)S(1)} %copy-done.5, bf16[1,512,2048]{1,2,0:T(8,128)(2,1)S(1)} %copy-done, ...), kind=kOutput, calls=%fused_computation.89 | convolution fusion | flops 4316987392 | bytes 25178112 | tf_op jit(solution)/shard_map/dot_general | solution.py:556
  274.0 7.8 %fusion.102 = f32[512,2048]{1,0:T(8,128)S(1)} fusion(bf16[512,2048]{1,0:T(8,128)(2,1)} %get-tuple-element.400.refs_3_, bf16[2048,2048]{1,0:T(8,128)(2,1)} %param.28), kind=kOutput, calls=%fused_computation.189 | convolution fusion | flops 4294967296 | bytes 14680064 | tf_op jit(solution)/shard_map/dot_general | solution.py:556
  281.7 9.4 %add_convert_fusion.1.x_ref = bf16[512,2048]{1,0:T(8,128)(2,1)} fusion(f32[512,2048]{1,0:T(8,128)S(1)} %fusion.102, bf16[512,2048]{1,0:T(8,128)(2,1)S(1)} %copy-done.21, bf16[2048,2048]{1,0:T(8,128)(2,1)} %param.29), kind=kOutput, calls=%fused_computation.88 | convolution fusion | flops 4297064448 | bytes 16777216 | tf_op jit(solution)/shard_map/dot_general | solution.py:556
  291.2 85.6 %sum_and_scatter.2 = (bf16[512,2048]{1,0:T(8,128)(2,1)}, f32[256,2048]{1,0:T(8,128)}, f32[256,1024]{1,0:T(8,128)}) custom-call(bf16[512,2048]{1,0:T(8,128)(2,1)} %add_convert_fusion.1.x_ref, bf16[2048,512]{1,0:T(8,128)(2,1)} %fusion.92.refs_0_, bf16[2048,512]{1,0:T(8,128)(2,1)} %bitcast.215, bf16[512,2048]{1,0:T(8,128)(2,1)} %copy-done.22, ...), custom_call_target="tpu_custom_call" | custom-call | tf_op jit(solution)/shard_map/sum_and_scatter/pallas_call | solution.py:455
  385.0 5.0 fusion.61
  392.5 36.6 %while.29 = (s32[]{:T(128)}, f32[512,4,128]{0,2,1:T(8,128)S(1)}, bf16[4,512,1024]{1,2,0:T(8,128)(2,1)}, bf16[4,512,4,128]{3,1,2,0:T(8,128)(2,1)}, s32[4,512]{1,0...) while((s32[]{:T(128)}, f32[512,4,128]{0,2,1:T(8,128)S(1)}, ...), condition=%wide.region_16.17_spmd.clone, body=%wide.region_15.16_spmd.clone.sunk | while | flops 1356595200 | bytes 30703808 | solution.py:772
  429.0 6.3 copy.165
  436.4 5.5 copy.172
  443.9 35.2 %reduce-scatter.2.cloned.1.call-done = bf16[512,1024]{1,0:T(8,128)(2,1)} async-done(((bf16[2048,1024]{1,0:T(8,128)(2,1)}), bf16[512,1024]{1,0:T(8,128)(2,1)}) %reduce-scatter.2.cloned.1.call-update) | async-done | bytes 1048592 | tf_op jit(solution)/shard_map/reduce_scatter | solution.py:773
  492.6 11.7 %all-reduce.1 = (f32[512]{0:T(512)S(1)}, f32[512]{0:T(512)S(1)}) all-reduce(f32[512]{0:T(512)S(1)} %get-tuple-element.346, f32[512]{0:T(512)S(1)} %get-tuple-element.348), channel_id=1, replica_groups=mesh['ctx'=4,'seq'=2,'tp'=4] {'tp'}, use_global_device_ids=true, to_apply=%region_18.19 | all-reduce | flops 1024 | bytes 8192 | tf_op jit(solution)/shard_map/psum | solution.py:785
  515.4 121.9 %sum_and_scatter.3 = (bf16[512,2048]{1,0:T(8,128)(2,1)}, f32[256,1024]{1,0:T(8,128)}, f32[256,2048]{1,0:T(8,128)}, f32[256,1536]{1,0:T(8,128)}, f32[256,512]{1,0:T(8,128)}, /*index=5*/f32[8,128]{1,0:T(8,128)}) custom-call(bf16[512,2048]{1,0:T(8,128)(2,1)} %add_convert_fusion.x_ref, bf16[2048,512]{1,0:T(8,128)(2,1)} %bitcast.216, ...), custom_call_target="tpu_custom_call" | custom-call | tf_op jit(solution)/shard_map/sum_and_scatter/pallas_call | solution.py:455
  641.4 5.0 add_bitcast_fusion
  646.4 5.3 copy.173
  (271 shorter events, 167.3 us)
Async XLA Ops:
  7.2 42.8 %all-gather.5.cloned.1.call-start = ((), (), s32[]{:S(2)}) async-start(), calls=%async_computation.2 | async-start | bytes 2621440 | tf_op jit(solution)/shard_map/all_gather | solution.py:649
  11.7 50.5 %all-gather.3.cloned.1.call-start = ((), (), s32[]{:S(2)}) async-start(), calls=%async_computation.1 | async-start | bytes 2621440 | tf_op jit(solution)/shard_map/all_gather | solution.py:648
  15.0 21.1 %copy-start.12 = (f32[512,512]{1,0:T(8,128)}, f32[512,512]{1,0:T(8,128)S(1)}, u32[]{:S(2)}) copy-start(f32[512,512]{1,0:T(8,128)S(1)} %copy.150) | copy-start | bytes 3145732
  15.0 18.4 %copy-start.42 = (f32[4,128]{1,0:T(4,128)S(1)}, f32[4,128]{1,0:T(4,128)}, u32[]{:S(2)}) copy-start(f32[4,128]{1,0:T(4,128)} %param.25) | copy-start | bytes 6148
  18.9 17.1 %copy-start.40 = (f32[4,128]{1,0:T(4,128)S(1)}, f32[4,128]{1,0:T(4,128)}, u32[]{:S(2)}) copy-start(f32[4,128]{1,0:T(4,128)} %param.24) | copy-start | bytes 6148
  19.3 19.5 %copy-start.10 = (f32[512,512]{1,0:T(8,128)}, f32[512,512]{1,0:T(8,128)S(1)}, u32[]{:S(2)}) copy-start(f32[512,512]{1,0:T(8,128)S(1)} %copy.146) | copy-start | bytes 3145732
  32.8 6.0 copy-start.38
  41.2 437.9 %reduce-scatter.2.cloned.1.call-start = ((), (), s32[]{:S(2)}) async-start(), calls=%async_computation.3 | async-start | bytes 5242880 | tf_op jit(solution)/shard_map/reduce_scatter | solution.py:773
  163.9 10.9 %copy-start.3 = (bf16[512,2048]{0,1:T(8,128)(2,1)}, bf16[512,2048]{0,1:T(8,128)(2,1)S(1)}, u32[]{:S(2)}) copy-start(bf16[512,2048]{0,1:T(8,128)(2,1)S(1)} %copy.158) | copy-start | bytes 6291460
  164.4 10.4 %slice-start.2 = ((s8[8388608]{0:T(1024)(128)(4,1)}), s8[4194304]{0:T(1024)(128)(4,1)S(1)}, s32[]{:S(2)}) async-start(s8[8388608]{0:T(1024)(128)(4,1)} %bitcast.248), calls=%async_computation.6 | async-start | bytes 8388608
  167.0 7.8 %copy-start.9 = (bf16[512,2048]{0,1:T(8,128)(2,1)}, bf16[512,2048]{0,1:T(8,128)(2,1)S(1)}, u32[]{:S(2)}) copy-start(bf16[512,2048]{0,1:T(8,128)(2,1)S(1)} %fusion.70) | copy-start | bytes 6291460
  167.0 7.8 %slice-start.3 = ((s8[8388608]{0:T(1024)(128)(4,1)}), s8[4194304]{0:T(1024)(128)(4,1)S(1)}, s32[]{:S(2)}) async-start(s8[8388608]{0:T(1024)(128)(4,1)} %bitcast.248), calls=%async_computation.7 | async-start | bytes 8388608
  167.0 15.6 %slice-start = ((s8[8388608]{0:T(1024)(128)(4,1)}), s8[4194304]{0:T(1024)(128)(4,1)S(1)}, s32[]{:S(2)}) async-start(s8[8388608]{0:T(1024)(128)(4,1)} %bitcast.246), calls=%async_computation.4 | async-start | bytes 8388608
  174.8 6.5 copy-start.47
  174.8 7.8 %slice-start.1 = ((s8[8388608]{0:T(1024)(128)(4,1)}), s8[4194304]{0:T(1024)(128)(4,1)S(1)}, s32[]{:S(2)}) async-start(s8[8388608]{0:T(1024)(128)(4,1)} %bitcast.246), calls=%async_computation.5 | async-start | bytes 8388608
  249.0 6.4 copy-start
  249.0 6.4 copy-start.35
  274.0 7.8 %copy-start.21 = (bf16[512,2048]{1,0:T(8,128)(2,1)S(1)}, bf16[512,2048]{1,0:T(8,128)(2,1)}, u32[]{:S(2)}) copy-start(bf16[512,2048]{1,0:T(8,128)(2,1)} %get-tuple-element.399.refs_4_) | copy-start | bytes 6291460
  441.9 39.7 %copy-start.28 = (f32[512,64]{0,1:T(8,128)S(1)}, f32[512,64]{0,1:T(8,128)}, u32[]{:S(2)}) copy-start(f32[512,64]{0,1:T(8,128)} %copy-done.27) | copy-start | bytes 393220
  441.9 39.7 %copy-start.30 = (f32[512,64]{0,1:T(8,128)S(1)}, f32[512,64]{0,1:T(8,128)}, u32[]{:S(2)}) copy-start(f32[512,64]{0,1:T(8,128)} %copy-done.29) | copy-start | bytes 393220
  484.0 7.0 %copy-start.13 = (f32[512,512]{1,0:T(8,128)S(1)}, f32[512,512]{1,0:T(8,128)}, u32[]{:S(2)}) copy-start(f32[512,512]{1,0:T(8,128)} %copy-done.12) | copy-start | bytes 3145732
  484.0 7.0 %copy-start.39 = (f32[512]{0:T(512)S(1)}, f32[512]{0:T(512)}, u32[]{:S(2)}) copy-start(f32[512]{0:T(512)} %copy-done.38) | copy-start | bytes 6148
  484.0 7.0 %copy-start.41 = (f32[4,128]{1,0:T(4,128)S(1)}, f32[4,128]{1,0:T(4,128)}, u32[]{:S(2)}) copy-start(f32[4,128]{1,0:T(4,128)} %param.24) | copy-start | bytes 6148
  653.0 7.5 %copy-start.25 = (f32[256,2048]{1,0:T(8,128)S(1)}, f32[256,2048]{1,0:T(8,128)}, u32[]{:S(2)}) copy-start(f32[256,2048]{1,0:T(8,128)} %get-tuple-element.659) | copy-start | bytes 6291460
  (34 other events, 104.9 us)
Sparse Core Ops, SparseCore 0:
  11.8 25.2 all-gather.4
  41.4 20.7 all-gather.2
  435.5 43.6 reduce-scatter.1

commit v3 on v2

--- a/solution.py
+++ b/solution.py
@@ -11,6 +11,8 @@
 lanes = 128
 row_blocks = 16
 row_chains = 8
+pace = 6
+norm_eps = 1e-06
 
 
 def remote(src, dst, send, recv, where):
@@ -87,69 +89,79 @@
         ).wait_recv()
 
     def step(self, t):
+        for g in range(row_chains):
+            self.sub_step(t, g)
+
+    def piece(self, e):
+        t = e // row_chains
+
+        @pl.when(t < self.steps)
+        def _():
+            self.sub_step(t, lax.rem(e, row_chains))
+
+    def sub_step(self, t, g):
         n, i, has_l, has_r = self.n, self.i, self.has_l, self.has_r
         own, from_l, from_r, res = self.own, self.from_l, self.from_r, self.res
-        for g in range(row_chains):
-            p = t - i
-            q = t - (n - 1 - i)
-            jr = n - 1 - lax.rem(p + n * self.total, n)
-            jl = lax.rem(q + n * self.total, n)
-            pv = (p >= 0) & (p < self.total)
-            qv = (q >= 0) & (q < self.total)
-
-            @pl.when(pv & has_l)
+        p = t - i
+        q = t - (n - 1 - i)
+        jr = n - 1 - lax.rem(p + n * self.total, n)
+        jl = lax.rem(q + n * self.total, n)
+        pv = (p >= 0) & (p < self.total)
+        qv = (q >= 0) & (q < self.total)
+
+        @pl.when(pv & has_l)
+        def _():
+            self.wait_l(g, p, jr)
+
+        @pl.when(qv & has_r)
+        def _():
+            self.wait_r(g, q, jl)
+
+        @pl.when(pv & (jr > i))
+        def _():
+            sl = self.rows_of(g, p)
+
+            @pl.when(has_l)
             def _():
-                self.wait_l(g, p, jr)
-
-            @pl.when(qv & has_r)
+                own[jr, sl] = (own[jr, sl].astype(f32) + from_l[jr, sl].astype(f32)).astype(bf16)
+
+            self.right(own, from_l, g, p, jr).start()
+
+        @pl.when(qv & (jl < i))
+        def _():
+            sl = self.rows_of(g, q)
+
+            @pl.when(has_r)
             def _():
-                self.wait_r(g, q, jl)
-
-            @pl.when(pv & (jr > i))
+                own[jl, sl] = (own[jl, sl].astype(f32) + from_r[jl, sl].astype(f32)).astype(bf16)
+
+            self.left(own, from_r, g, q, jl).start()
+
+        @pl.when(pv & (jr == i))
+        def _():
+            sl = self.rows_of(g, p)
+
+            @pl.when(has_l & has_r)
             def _():
-                sl = self.rows_of(g, p)
-
-                @pl.when(has_l)
-                def _():
-                    own[jr, sl] = (own[jr, sl].astype(f32) + from_l[jr, sl].astype(f32)).astype(bf16)
-
-                self.right(own, from_l, g, p, jr).start()
-
-            @pl.when(qv & (jl < i))
+                res[i, sl] = (
+                    own[i, sl].astype(f32) + from_l[i, sl].astype(f32) + from_r[i, sl].astype(f32)
+                ).astype(bf16)
+
+            @pl.when(jnp.logical_not(has_l))
             def _():
-                sl = self.rows_of(g, q)
-
-                @pl.when(has_r)
-                def _():
-                    own[jl, sl] = (own[jl, sl].astype(f32) + from_r[jl, sl].astype(f32)).astype(bf16)
-
-                self.left(own, from_r, g, q, jl).start()
-
-            @pl.when(pv & (jr == i))
+                res[i, sl] = (own[i, sl].astype(f32) + from_r[i, sl].astype(f32)).astype(bf16)
+
+            @pl.when(jnp.logical_not(has_r))
             def _():
-                sl = self.rows_of(g, p)
-
-                @pl.when(has_l & has_r)
-                def _():
-                    res[i, sl] = (
-                        own[i, sl].astype(f32) + from_l[i, sl].astype(f32) + from_r[i, sl].astype(f32)
-                    ).astype(bf16)
-
-                @pl.when(jnp.logical_not(has_l))
-                def _():
-                    res[i, sl] = (own[i, sl].astype(f32) + from_r[i, sl].astype(f32)).astype(bf16)
-
-                @pl.when(jnp.logical_not(has_r))
-                def _():
-                    res[i, sl] = (own[i, sl].astype(f32) + from_l[i, sl].astype(f32)).astype(bf16)
-
-            @pl.when(pv & (jr <= i) & has_r)
-            def _():
-                self.right(res, res, g, p, jr).start()
-
-            @pl.when(qv & (jl >= i) & has_l)
-            def _():
-                self.left(res, res, g, q, jl).start()
+                res[i, sl] = (own[i, sl].astype(f32) + from_l[i, sl].astype(f32)).astype(bf16)
+
+        @pl.when(pv & (jr <= i) & has_r)
+        def _():
+            self.right(res, res, g, p, jr).start()
+
+        @pl.when(qv & (jl >= i) & has_l)
+        def _():
+            self.left(res, res, g, q, jl).start()
 
     def drain(self):
         def one(p, carry):
@@ -451,11 +463,14 @@
     return pl.BlockSpec(memory_space=pltpu.VMEM)
 
 
-def comm_call(body, args, outs, scratch, cid, name):
+def comm_call(body, args, outs, scratch, cid, name, scalars=()):
     return pl.pallas_call(
         body,
         out_shape=outs,
-        in_specs=[vmem_spec()] * len(args),
+        in_specs=[
+            pl.BlockSpec(memory_space=pltpu.SMEM) if i in scalars else vmem_spec()
+            for i in range(len(args))
+        ],
         out_specs=[vmem_spec()] * len(outs),
         scratch_shapes=scratch,
         compiler_params=pltpu.CompilerParams(
@@ -486,7 +501,7 @@
 
     out = jax.ShapeDtypeStruct((rows, width), bf16)
     (summed,) = comm_call(body, [partial.astype(bf16)], [out], line.scratch(), cid, "tp_sum")
-    return summed.astype(f32)
+    return summed
 
 
 def sum_and_scatter(partial, ats, bs, jobs, out_widths, cid, gains=None):
@@ -521,15 +536,12 @@
 
         def one(it, carry):
             grads.early(it)
-
-            @pl.when(it < line.steps)
-            def _():
-                line.step(it)
-
+            for v in range(pace):
+                line.piece(it * pace + v)
             grads.late(it)
             return carry
 
-        lax.fori_loop(0, max(line.steps, grads.steps), one, 0)
+        lax.fori_loop(0, max(-(-line.steps * row_chains // pace), grads.steps), one, 0)
         if ns:
             small.finish()
         line.drain()
@@ -544,7 +556,270 @@
         body, [partial.astype(bf16)] + list(ats) + list(bs) + small_in, outs,
         line.scratch() + grads.scratch() + (small.scratch() if ns else []), cid, "sum_and_scatter",
     )
-    return res[0].astype(f32), res[1:]
+    return res[0], res[1:]
+
+
+class LineSmall:
+    def __init__(self, n, rows):
+        self.n, self.rows = n, rows
+
+    def scratch(self):
+        sem = pltpu.SemaphoreType.DMA
+        return [
+            pltpu.VMEM((8, self.rows), f32), pltpu.VMEM((self.n - 1, 8, self.rows), f32),
+            sem((self.n - 1,)), sem((self.n - 1,)),
+        ]
+
+    def bind(self, refs):
+        self.mine, self.got, self.sent, self.done = refs
+        self.i = lax.axis_index("tp")
+
+    def greet(self, bar):
+        for d in range(1, self.n):
+            pl.semaphore_signal(
+                bar, inc=1, device_id={"tp": lax.rem(self.i + d, self.n)}, device_id_type=MESH
+            )
+        return self.n - 1
+
+    def copy(self, d):
+        return remote(
+            self.mine, self.got.at[d - 1], self.sent.at[d - 1], self.done.at[d - 1],
+            {"tp": lax.rem(self.i + d, self.n)},
+        )
+
+    def total(self, columns):
+        self.mine[...] = jnp.transpose(columns)[:8]
+        for d in range(1, self.n):
+            self.copy(d).start()
+        acc = self.mine[...]
+        for d in range(1, self.n):
+            self.copy(d).wait_recv()
+            acc = acc + self.got[d - 1]
+        for d in range(1, self.n):
+            self.copy(d).wait_send()
+        return jnp.transpose(jnp.concatenate([acc, jnp.zeros((lanes - 8, self.rows), f32)], axis=0))
+
+
+def lane_pair(first, second, rows):
+    lane = lax.broadcasted_iota(jnp.int32, (rows, lanes), 1)
+    return jnp.where(lane == 0, first, 0.0) + jnp.where(lane == 1, second, 0.0)
+
+
+def dot_nt(left, right):
+    return lax.dot_general(left, right, (((1,), (1,)), ((), ())), preferred_element_type=f32)
+
+
+def dot_tn(left, right):
+    return lax.dot_general(left, right, (((0,), (0,)), ((), ())), preferred_element_type=f32)
+
+
+def attention_back(
+    back, grad, proj, attn_gain, w_output, query_rot, keys, values, attn, lse, pos_row, order,
+    query_norm, key_norm, scales, qgain, kgain, cosine, sine, cid,
+):
+    rows, width = back.shape
+    local = w_output.shape[0]
+    head_dim = lanes
+    heads = local // head_dim
+    count = keys.shape[0]
+    nx, n_tp = lax.axis_size("ctx") // 2, lax.axis_size("tp")
+    small = LineSmall(n_tp, rows)
+    n_small = len(small.scratch())
+    scale = head_dim ** (-0.5)
+    tile = 64
+    sub = rows // 2
+
+    def body(
+        back_ref, grad_ref, proj_ref, again_ref, w_ref, q_ref, k_ref, v_ref, attn_ref, lse_ref,
+        prow_ref, order_ref, qn_ref, kn_ref, sc_ref, qg_ref, kg_ref, cos_ref, sin_ref,
+        dqkv_ref, dprojt_ref, dagain_ref, dqg_ref, dkg_ref,
+        dproj, dout, columns, delta, dqs, dks, send0, keep, recv0, recv1,
+        s0, d0, s1, d1, *small_refs,
+    ):
+        small.bind(small_refs)
+        ctx = lax.axis_index("ctx")
+        mx, core = ctx // 2, lax.rem(ctx, 2)
+        bar = pltpu.get_barrier_semaphore()
+        mate = {"ctx": mx * 2 + 1 - core}
+        peers = small.greet(bar) + nx
+        pl.semaphore_signal(bar, inc=1, device_id=mate, device_id_type=MESH)
+        for d in range(1, nx):
+            pl.semaphore_signal(
+                bar, inc=1, device_id={"ctx": lax.rem(mx + d, nx) * 2 + core}, device_id_type=MESH
+            )
+
+        dagain_ref[...] = jnp.zeros_like(dagain_ref)
+
+        def norm_rows(t, carry):
+            sl = pl.ds(pl.multiple_of(t * tile, tile), tile)
+            dres = grad_ref[sl].astype(f32) + back_ref[sl].astype(f32)
+            out = proj_ref[sl].astype(f32)
+            inv = lax.rsqrt(jnp.mean(out * out, axis=1, keepdims=True) + norm_eps)
+            norm = out * inv
+            dagain_ref[...] += jnp.sum(dres * norm, axis=0, keepdims=True)
+            dnorm = dres * again_ref[...]
+            dot = jnp.mean(dnorm * norm, axis=1, keepdims=True)
+            dproj[sl] = (inv * (dnorm - norm * dot)).astype(bf16)
+            return carry
+
+        lax.fori_loop(0, rows // tile, norm_rows, 0)
+        for h in range(local // sub):
+            dout[:, h * sub : (h + 1) * sub] = dot_nt(
+                dproj[...], w_ref[h * sub : (h + 1) * sub, :]
+            ).astype(bf16)
+        lane = lax.broadcasted_iota(jnp.int32, (rows, lanes), 1)
+        acc = jnp.zeros((rows, lanes), f32)
+        for h in range(heads):
+            hs = slice(h * head_dim, (h + 1) * head_dim)
+            row_sum = jnp.sum(
+                dout[:, hs].astype(f32) * attn_ref[:, hs].astype(f32), axis=1, keepdims=True
+            )
+            acc = jnp.where(lane == h, row_sum, acc)
+        columns[...] = acc
+        delta[...] = jnp.transpose(columns[...])[:8]
+        dqs[...] = jnp.zeros_like(dqs)
+        pl.semaphore_wait(bar, peers)
+
+        def c0(h):
+            slot = lax.rem(h, 2)
+            return remote(send0.at[slot], recv0.at[h], s0.at[slot], d0.at[h], mate)
+
+        def c1(h, d):
+            to = lax.rem(mx + d, nx)
+            return remote(
+                recv0.at[h, to], recv1.at[h, d - 1], s1.at[h, d - 1], d1.at[h, d - 1],
+                {"ctx": to * 2 + core},
+            )
+
+        def one_block(h, hs, x, owner, write):
+            start = (x * 2 + owner) * rows
+            for part in range(rows // sub):
+                ks = pl.ds(pl.multiple_of(start + part * sub, sub), sub)
+                key, value = k_ref[ks, hs], v_ref[ks, hs]
+                query, dhead = q_ref[:, hs], dout[:, hs]
+                score = dot_nt(key, query) * scale
+                place = order_ref[0, (x * 2 + owner) * 2 + part] * sub
+                seen = place + lax.broadcasted_iota(jnp.int32, (sub, rows), 0) <= prow_ref[...]
+                share = jnp.where(seen, jnp.exp(score - lse_ref[pl.ds(h, 1), :]), 0.0)
+                dshare = dot_nt(value, dhead)
+                dscore = (share * (dshare - delta[pl.ds(h, 1), :]) * scale).astype(bf16)
+                dqs[:, hs] += dot_tn(dscore, key)
+                write(
+                    x, slice(part * sub, (part + 1) * sub),
+                    jnp.dot(dscore, query, preferred_element_type=f32),
+                    jnp.dot(share.astype(bf16), dhead, preferred_element_type=f32),
+                )
+
+        def one_head(h):
+            hs = pl.ds(pl.multiple_of(h * head_dim, head_dim), head_dim)
+            slot = lax.rem(h, 2)
+
+            def to_send(x, rs, dk, dv):
+                send0[slot, x, rs, :lanes] = dk.astype(bf16)
+                send0[slot, x, rs, lanes:] = dv.astype(bf16)
+
+            def to_keep(x, rs, dk, dv):
+                keep[slot, x, rs, :lanes] = dk.astype(bf16)
+                keep[slot, x, rs, lanes:] = dv.astype(bf16)
+
+            @pl.when(h >= 2)
+            def _():
+                c0(h).wait_send()
+
+            def mates(e, carry):
+                one_block(h, hs, lax.rem(mx + 1 + e, nx), 1 - core, to_send)
+                return carry
+
+            lax.fori_loop(0, nx, mates, 0)
+            c0(h).start()
+
+            def owns(e, carry):
+                one_block(h, hs, lax.rem(mx + 1 + e, nx), core, to_keep)
+                return carry
+
+            lax.fori_loop(0, nx, owns, 0)
+            c0(h).wait_recv()
+
+            def add(x, carry):
+                recv0[h, x] = (keep[slot, x].astype(f32) + recv0[h, x].astype(f32)).astype(bf16)
+                return carry
+
+            lax.fori_loop(0, nx, add, 0)
+            for d in range(1, nx):
+                c1(h, d).start()
+
+        def heads_loop(h, carry):
+            one_head(h)
+            return carry
+
+        lax.fori_loop(0, heads, heads_loop, 0)
+
+        dot_q = jnp.zeros((rows, 1), f32)
+        for h in range(heads):
+            hs = slice(h * head_dim, (h + 1) * head_dim)
+            dq = dqs[:, hs]
+            dq = dq * cos_ref[...] - pltpu.roll(dq, head_dim // 2, 1) * sin_ref[...]
+            norm = qn_ref[:, hs]
+            dqg_ref[:, hs] = jnp.sum(dq * norm, axis=0, keepdims=True)
+            dq = dq * qg_ref[:, hs]
+            dqs[:, hs] = dq
+            dot_q = dot_q + jnp.sum(dq * norm, axis=1, keepdims=True)
+        dprojt_ref[...] = jnp.transpose(dproj[...])
+        dot_k = jnp.zeros((rows, 1), f32)
+        for h in range(heads):
+            hs = slice(h * head_dim, (h + 1) * head_dim)
+            total = recv0[h, mx].astype(f32)
+            for d in range(1, nx):
+                c1(h, d).wait_recv()
+                total = total + recv1[h, d - 1].astype(f32)
+            dqkv_ref[:, 2 * local + h * head_dim : 2 * local + (h + 1) * head_dim] = total[
+                :, lanes:
+            ].astype(bf16)
+            dk = total[:, :lanes]
+            dk = dk * cos_ref[...] - pltpu.roll(dk, head_dim // 2, 1) * sin_ref[...]
+            norm = kn_ref[:, hs]
+            dkg_ref[:, hs] = jnp.sum(dk * norm, axis=0, keepdims=True)
+            dk = dk * kg_ref[:, hs]
+            dks[:, hs] = dk
+            dot_k = dot_k + jnp.sum(dk * norm, axis=1, keepdims=True)
+        dots = small.total(lane_pair(dot_q, dot_k, rows)) * (1.0 / width)
+        for h in range(heads):
+            hs = slice(h * head_dim, (h + 1) * head_dim)
+            dqkv_ref[:, hs] = (
+                sc_ref[:, 0:1] * (dqs[:, hs] - qn_ref[:, hs] * dots[:, 0:1])
+            ).astype(bf16)
+            dqkv_ref[:, local + h * head_dim : local + (h + 1) * head_dim] = (
+                sc_ref[:, 1:2] * (dks[:, hs] - kn_ref[:, hs] * dots[:, 1:2])
+            ).astype(bf16)
+        for h in range(heads):
+            if h >= heads - 2:
+                c0(h).wait_send()
+            for d in range(1, nx):
+                c1(h, d).wait_send()
+
+    sem = pltpu.SemaphoreType.DMA
+    pair = (rows, 2 * lanes)
+    return comm_call(
+        body,
+        [back, grad, proj, attn_gain, w_output, query_rot, keys, values, attn, lse, pos_row,
+         order, query_norm, key_norm, scales, qgain, kgain, cosine, sine],
+        [
+            jax.ShapeDtypeStruct((rows, 3 * local), bf16),
+            jax.ShapeDtypeStruct((width, rows), bf16),
+            jax.ShapeDtypeStruct((1, width), f32),
+            jax.ShapeDtypeStruct((1, local), f32),
+            jax.ShapeDtypeStruct((1, local), f32),
+        ],
+        [
+            pltpu.VMEM((rows, width), bf16), pltpu.VMEM((rows, local), bf16),
+            pltpu.VMEM((rows, lanes), f32), pltpu.VMEM((8, rows), f32),
+            pltpu.VMEM((rows, local), f32), pltpu.VMEM((rows, local), f32),
+            pltpu.VMEM((2, nx) + pair, bf16), pltpu.VMEM((2, nx) + pair, bf16),
+            pltpu.VMEM((heads, nx) + pair, bf16), pltpu.VMEM((heads, nx - 1) + pair, bf16),
+            sem((2,)), sem((heads,)), sem((heads, nx - 1)), sem((heads, nx - 1)),
+        ] + small.scratch(),
+        cid, "attention_back", {11},
+    )
 
 
 norm_eps = 1e-06
@@ -680,7 +955,8 @@
     log_total = peak + jnp.log(total)
     mixed = (accum / total[:, :, None]).astype(jnp.bfloat16)
     attn_flat = mixed.transpose(1, 0, 2).reshape(row_count, local)
-    proj = tp_sum(matmul(attn_flat, w_output), 1)
+    proj_sum = tp_sum(matmul(attn_flat, w_output), 1)
+    proj = proj_sum.astype(f32)
     attn_scale = lax.rsqrt(jnp.mean(proj * proj, axis=1) + norm_eps)
     attn_norm = proj * attn_scale[:, None]
     resid = inputs + attn_norm * attn_gain
@@ -690,7 +966,7 @@
     sigma = jax.nn.sigmoid(gate)
     active = gate * sigma
     inner = (active * up).astype(jnp.bfloat16)
-    down = tp_sum(matmul(inner, w_down), 2)
+    down = tp_sum(matmul(inner, w_down), 2).astype(f32)
     mlp_scale = lax.rsqrt(jnp.mean(down * down, axis=1) + norm_eps)
     mlp_norm = down * mlp_scale[:, None]
     block_out = resid + mlp_norm * mlp_gain
@@ -718,79 +994,20 @@
         [inner.shape[1], half * 2 * lanes],
         3,
     )
-    d_resid = upstream + back
-    d_attn_gain = jnp.sum(d_resid * attn_norm, axis=0)
-    d_anorm = d_resid * attn_gain
-    d_proj = (
-        attn_scale[:, None]
-        * (d_anorm - attn_norm * jnp.mean(d_anorm * attn_norm, axis=1, keepdims=True))
-    ).astype(jnp.bfloat16)
-    d_attn = matmul(d_proj, w_output.T).astype(jnp.bfloat16)
-    d_attn_heads = d_attn.reshape(row_count, heads, head_dim)
-    delta = jnp.sum(
-        d_attn_heads.transpose(1, 0, 2).astype(jnp.float32) * mixed.astype(jnp.float32), axis=2
-    )
-    whole_keys, whole_values = gather_pair(key_flat, values)
-    count = whole_keys.shape[0]
-    block = 512
-    key_blocks = whole_keys.reshape(count // block, block, heads, head_dim)
-    value_blocks = whole_values.reshape(count // block, block, heads, head_dim)
-    pos_blocks = key_positions(order, 0, count, group).reshape(count // block, block)
-    zero_grads = jnp.zeros((row_count, heads, head_dim), jnp.float32)
-
-    def back_block(query_grad, item):
-        key_block, value_block, pos_block = item
-        scores = (
-            jnp.einsum("qhd,khd->hqk", query_rot, key_block, preferred_element_type=jnp.float32)
-            * scale
-        )
-        mask = (pos_block[None, :] <= query_pos[:, None])[None]
-        share = jnp.where(mask, jnp.exp(scores - log_total[:, :, None]), 0.0)
-        share_grad = jnp.einsum(
-            "qhd,khd->hqk", d_attn_heads, value_block, preferred_element_type=jnp.float32
-        )
-        score_grad = (share * (share_grad - delta[:, :, None]) * scale).astype(jnp.bfloat16)
-        query_grad = query_grad + jnp.einsum(
-            "hqk,khd->qhd", score_grad, key_block, preferred_element_type=jnp.float32
-        )
-        key_grad = jnp.einsum(
-            "hqk,qhd->khd", score_grad, query_rot, preferred_element_type=jnp.float32
-        )
-        value_grad = jnp.einsum(
-            "hqk,qhd->khd",
-            share.astype(jnp.bfloat16),
-            d_attn_heads,
-            preferred_element_type=jnp.float32,
-        )
-        return (
-            query_grad,
-            jnp.concatenate(
-                [key_grad.reshape(block, local), value_grad.reshape(block, local)], axis=1
-            ),
-        )
-
-    d_qrot, kv_terms = lax.scan(back_block, zero_grads, (key_blocks, value_blocks, pos_blocks))
-    kv_grads = lax.psum_scatter(
-        kv_terms.reshape(count, 2 * local).astype(jnp.bfloat16), "ctx", scatter_dimension=0, tiled=True
-    )
-    kv_grads = kv_grads.astype(jnp.float32)
-    d_krot = kv_grads[:, :local].reshape(row_count, heads, head_dim)
-    d_value = kv_grads[:, local:].astype(jnp.bfloat16)
-    d_qhead = unrotate(d_qrot, cosine, sine).reshape(row_count, local)
-    d_khead = unrotate(d_krot, cosine, sine).reshape(row_count, local)
-    d_query_gain = jnp.sum(d_qhead * query_norm, axis=0).reshape(heads, head_dim)
-    d_key_gain = jnp.sum(d_khead * key_norm, axis=0).reshape(heads, head_dim)
-    d_qnorm = d_qhead * qgain
-    d_knorm = d_khead * kgain
-    query_dot, key_dot = lax.psum(
-        (jnp.sum(d_qnorm * query_norm, axis=1), jnp.sum(d_knorm * key_norm, axis=1)), "tp"
-    )
-    d_query = (query_scale[:, None] * (d_qnorm - query_norm * (query_dot / width)[:, None])).astype(
-        jnp.bfloat16
-    )
-    d_key = (key_scale[:, None] * (d_knorm - key_norm * (key_dot / width)[:, None])).astype(
-        jnp.bfloat16
-    )
+    whole_keys = keys_in.reshape(count, local)
+    whole_values = values_in.reshape(count, local)
+    angle_cos = jnp.concatenate([cosine, cosine], axis=1)
+    angle_sin = jnp.concatenate([-sine, sine], axis=1)
+    lse = jnp.pad(log_total, ((0, 8 - heads), (0, 0)))
+    scales = jnp.stack([query_scale, key_scale], axis=1)
+    d_qkv, d_proj_t, d_attn_gain, d_query_gain, d_key_gain = attention_back(
+        back, out_grad[0], proj_sum, attn_gain[None], w_output, query_rot.reshape(row_count, local),
+        whole_keys, whole_values, attn_flat, lse, query_pos[None], group_order,
+        query_norm, key_norm, scales, qgain[None], kgain[None], angle_cos, angle_sin, 5,
+    )
+    d_query_gain = d_query_gain.reshape(heads, head_dim)
+    d_key_gain = d_key_gain.reshape(heads, head_dim)
+    d_query, d_key, d_value = (d_qkv[:, i * local : (i + 1) * local] for i in range(3))
     thin = local // (2 * lanes)
     owners = lax.axis_size("ctx") * lax.axis_size("seq")
     pieces = [
@@ -802,17 +1019,15 @@
     cuts = [piece.shape[1] for piece in pieces]
     packed = jnp.concatenate(pieces, axis=1)
     packed = jnp.pad(packed, ((0, 0), (0, 8 * lanes - packed.shape[1]))).reshape(owners, 8, lanes)
-    back, (grad_gate_b, grad_up, grad_qkv, grad_output, small) = sum_and_scatter(
+    last, (grad_gate_b, grad_up, grad_qkv, grad_output, small) = sum_and_scatter(
         matmul(d_query, w_query.T) + matmul(d_key, w_key.T) + matmul(d_value, w_value.T),
-        [hidden_t, inputs_bf.T, d_proj.T],
-        [d_gate, d_up, d_query, d_key, d_value, attn_flat],
+        [hidden_t, inputs_bf.T, d_proj_t],
+        [d_gate, d_up, d_qkv, attn_flat],
         [
             dict(a=0, b=0, first=half, count=wide - half, out=0, place=0),
             dict(a=0, b=1, first=0, count=wide, out=1, place=0),
-            dict(a=2, b=5, first=0, count=thin, out=3, place=0),
-            dict(a=1, b=2, first=0, count=thin, out=2, place=0),
-            dict(a=1, b=3, first=0, count=thin, out=2, place=thin),
-            dict(a=1, b=4, first=0, count=thin, out=2, place=2 * thin),
+            dict(a=2, b=3, first=0, count=thin, out=3, place=0),
+            dict(a=1, b=2, first=0, count=3 * thin, out=2, place=0),
         ],
         [(wide - half) * 2 * lanes, inner.shape[1], 3 * local, local],
         4,
@@ -822,7 +1037,7 @@
     g_attn, g_mlp, g_query, g_key = jnp.split(
         small[: sum(cuts)], [cuts[0], cuts[0] + cuts[1], cuts[0] + cuts[1] + cuts[2]]
     )
-    input_grad = d_resid + back
+    input_grad = upstream + back.astype(f32) + last.astype(f32)
     grad_query, grad_key, grad_value = jnp.split(grad_qkv, 3, axis=1)
     grad_gate = jnp.concatenate([grad_gate_a, grad_gate_b], axis=1)
     summed = (

time: 676 us -> 604 us (0.89)
  matrix products: 124 us -> 94.9 us
  waiting for transfers between devices: 40.2 us -> 22.3 us
  local copies, waits for them, and re-layouts: 81.7 us -> 65 us
  Pallas kernels: 331 us -> 347 us
  blocking collectives: 25.2 us -> 13.5 us
  other arithmetic: 51.8 us -> 40.2 us
    reduce_scatter x1 -> x0, waiting for transfers between devices: 35.2 us -> none  [per_device(): lax.psum_scatter(kv_terms.reshape(count, 2 * local).astype(jnp.bfloat16),...]
    dot_general x20 -> x0, matrix products: 31.3 us -> none  [the longest x4 10.2 us: back_block(): jnp.einsum('qhd,khd->hqk', d_attn_heads, value_block, preferred_element_t...]
    all_gather x1, waiting for transfers between devices: 0.02 us -> 22.1 us  [per_device(): values_in = lax.all_gather(values, 'ctx', axis=0, tiled=True)]
    pallas_call x4 -> x5, Pallas kernels: 331 us -> 347 us  [comm_call(): pl.pallas_call(body, out_shape=outs, in_specs=[pl.BlockSpec(memory_space=...]
    unnamed x113 -> x78, local copies, waits for them, and re-layouts: 37.6 us -> 25.3 us
    psum x1 -> x0, blocking collectives: 11.7 us -> none  [per_device(): lax.psum((jnp.sum(d_qnorm * query_norm, axis=1), jnp.sum(d_knorm * key_no...]
    convert_element_type x2 -> x0, local copies, waits for them, and re-layouts: 7.29 us -> none  [the longest x1 6.29 us: per_device(): kv_terms.reshape(count, 2 * local).astype(jnp.bfloat16)]
    dot_general x14 -> x13, matrix products: 73.8 us -> 80.1 us  [matmul(): return jnp.dot(left, right, preferred_element_type=jnp.float32)]
  transfers between devices with their start and end apart: 3 -> 2, of which waited for: 2 -> 2; matrix products, arithmetic and copies ran while one was open for 6% -> 4% of each run, Pallas kernels for 0% -> 0%
where the time goes in v3:
time: 604 us; the launch traced here: 598 us
  Pallas kernels  347 us (57%)
  matrix products  94.9 us (16%)
  local copies, waits for them, and re-layouts  65 us (11%)
  other arithmetic  40.2 us (7%)
  waiting for transfers between devices  22.3 us (4%)
  between operations  15.1 us (2%)
  blocking collectives  13.5 us (2%)
    pallas_call x5, Pallas kernels, comm_call(): pl.pallas_call(body, out_shape=outs, in_specs=[pl.BlockSpec(memory_space=...  347 us
    dot_general x13, matrix products, matmul(): return jnp.dot(left, right, preferred_element_type=jnp.float32)  80.1 us
    unnamed x78, local copies, waits for them, and re-layouts  25.3 us
    all_gather x1, waiting for transfers between devices, per_device(): values_in = lax.all_gather(values, 'ctx', axis=0, tiled=True)  22.1 us
    pallas_call x5, local copies, waits for them, and re-layouts, comm_call(): pl.pallas_call(body, out_shape=outs, in_specs=[pl.BlockSpec(memory_space=...  16.7 us
    psum x1, blocking collectives, per_device(): lax.psum((jnp.sum(query * query, axis=1), jnp.sum(keyraw * keyraw, axis=1...  13.5 us
  transfers between devices with their start and end apart: 2, of which 2 were waited for; matrix products, arithmetic and copies ran while one was open for 4% of the time, Pallas kernels for 0%

profile of v3, /device:TPU:0, one launch (start us, length us, event | category | flops | bytes accessed | tf_op | source)
XLA Modules:
  0.0 598.2 jit_solution(1753625357647409867)
XLA Ops:
  8.0 4.6 multiply_reduce_fusion
  14.3 13.5 %all-reduce.2 = (f32[512]{0:T(512)S(1)}, f32[512]{0:T(512)S(1)}) all-reduce(f32[512]{0:T(512)S(1)} %get-tuple-element.268, f32[512]{0:T(512)S(1)} %get-tuple-element.270), channel_id=1, replica_groups=mesh['ctx'=4,'seq'=2,'tp'=4] {'tp'}, use_global_device_ids=true, to_apply=%region_1.2 | all-reduce | flops 1024 | bytes 8192 | tf_op jit(solution)/shard_map/psum | solution.py:902
  34.1 4.4 fusion.42
  57.4 22.1 %all-gather.5.cloned.1.call-done.v_ref = bf16[2048,512]{1,0:T(8,128)(2,1)} async-done(((bf16[512,512]{1,0:T(8,128)(2,1)}), bf16[2048,512]{1,0:T(8,128)(2,1)}) %all-gather.5.cloned.1.call-update) | async-done | bytes 2097168 | tf_op jit(solution)/shard_map/all_gather | solution.py:924
  83.5 25.2 %while.15 = (s32[]{:T(128)}, f32[4,512]{1,0:T(4,128)S(1)}, f32[4,512]{1,0:T(4,128)S(1)}, f32[4,512,128]{2,1,0:T(8,128)S(1)}, s32[4,512]{1,0:T(4,128)S(1)}, /*ind...) while((s32[]{:T(128)}, f32[4,512]{1,0:T(4,128)S(1)}, ...), condition=%wide.region_9.10_spmd.clone, body=%wide.region_6.9_spmd.clone.sunk | while | flops 549464064 | bytes 19538056 | solution.py:953
  109.9 4.2 convolution_convert_fusion.1.x_ref
  114.1 62.4 %tp_sum.2.proj_ref = bf16[512,2048]{1,0:T(8,128)(2,1)} custom-call(bf16[512,2048]{1,0:T(8,128)(2,1)} %convolution_convert_fusion.1.x_ref), custom_call_target="tpu_custom_call" | custom-call | tf_op jit(solution)/shard_map/tp_sum/pallas_call | solution.py:467
  176.5 4.1 copy.117
  185.3 7.7 %fusion.73 = f32[512,2048]{1,0:T(8,128)S(1)} fusion(bf16[512,2048]{0,1:T(8,128)(2,1)S(1)} %fusion.35, bf16[2048,2048]{1,0:T(8,128)(2,1)} %param.26), kind=kOutput, calls=%fused_computation.152 | convolution fusion | flops 4294967296 | bytes 14680064 | tf_op jit(solution)/shard_map/dot_general | solution.py:831
  193.1 6.5 %multiply_convert_fusion.2 = (bf16[512,2048]{1,0:T(8,128)(2,1)S(1)}, f32[512,2048]{1,0:T(8,128)}) fusion(f32[512,2048]{1,0:T(8,128)S(1)} %fusion.73, bf16[512,2048]{0,1:T(8,128)(2,1)S(1)} %fusion.35, bf16[2048,2048]{1,0:T(8,128)(2,1)S(1)} %bitcast.162), kind=kOutput, calls=%fused_computation.54 | convolution fusion | flops 4301258752 | bytes 20971520 | tf_op jit(solution)/shard_map/dot_general | solution.py:831
  200.9 5.7 convolution_convert_fusion.x_ref
  206.6 60.3 %tp_sum.3 = bf16[512,2048]{1,0:T(8,128)(2,1)} custom-call(bf16[512,2048]{1,0:T(8,128)(2,1)} %convolution_convert_fusion.x_ref), custom_call_target="tpu_custom_call" | custom-call | tf_op jit(solution)/shard_map/tp_sum/pallas_call | solution.py:467
  280.4 13.1 %multiply_convert_fusion = (bf16[512,2048]{1,0:T(8,128)(2,1)}, bf16[512,2048]{1,0:T(8,128)(2,1)}) fusion(f32[512,2048]{1,0:T(8,128)} %copy-done.30, f32[512,2048]{1,0:T(8,128)} %get-tuple-element.273, bf16[2048,2048]{1,0:T(8,128)(2,1)} %param.28, bf16[512,2048]{0,1:T(8,128)(2,1)S(1)} %copy-done.5, bf16[1,512,2048]{1,2,0:T(8,128)(2,1)S(1)} %copy-done.2, ...), kind=kOutput, calls=%fused_computation.52 | convolution fusion | flops 4316987392 | bytes 25178112 | tf_op jit(solution)/shard_map/dot_general | solution.py:831
  293.5 7.8 %fusion.74 = f32[512,2048]{1,0:T(8,128)S(1)} fusion(bf16[512,2048]{1,0:T(8,128)(2,1)} %get-tuple-element.246.refs_3_, bf16[2048,2048]{1,0:T(8,128)(2,1)} %param.26), kind=kOutput, calls=%fused_computation.153 | convolution fusion | flops 4294967296 | bytes 14680064 | tf_op jit(solution)/shard_map/dot_general | solution.py:831
  301.3 9.6 %add_convert_fusion.1.x_ref = bf16[512,2048]{1,0:T(8,128)(2,1)} fusion(f32[512,2048]{1,0:T(8,128)S(1)} %fusion.74, bf16[512,2048]{1,0:T(8,128)(2,1)S(1)} %copy-done.11, bf16[2048,2048]{1,0:T(8,128)(2,1)} %param.27), kind=kOutput, calls=%fused_computation.51 | convolution fusion | flops 4297064448 | bytes 16777216 | tf_op jit(solution)/shard_map/dot_general | solution.py:831
  310.9 70.0 %sum_and_scatter.2 = (bf16[512,2048]{1,0:T(8,128)(2,1)}, f32[256,2048]{1,0:T(8,128)}, f32[256,1024]{1,0:T(8,128)}) custom-call(bf16[512,2048]{1,0:T(8,128)(2,1)} %add_convert_fusion.1.x_ref, bf16[2048,512]{1,0:T(8,128)(2,1)} %get-tuple-element.251.refs_0_, bf16[2048,512]{1,0:T(8,128)(2,1)} %bitcast.139, bf16[512,2048]{1,0:T(8,128)(2,1)} %copy-done.12, ...), custom_call_target="tpu_custom_call" | custom-call | tf_op jit(solution)/shard_map/sum_and_scatter/pallas_call | solution.py:467
  385.5 47.2 %attention_back.1 = (bf16[512,1536]{1,0:T(8,128)(2,1)}, bf16[2048,512]{1,0:T(8,128)(2,1)}, f32[1,2048]{1,0:T(1,128)}, f32[1,512]{1,0:T(1,128)}, f32[1,512]{1,0:T(1,128)}) custom-call(bf16[512,2048]{1,0:T(8,128)(2,1)} %get-tuple-element.78.back_ref, bf16[512,2048]{1,0:T(8,128)(2,1)} %bitcast.141, bf16[512,2048]{1,0:T(8,128)(2,1)} %tp_sum.2.proj_ref, ...), custom_call_target="tpu_custom_call" | custom-call | tf_op jit(solution)/shard_map/attention_back/pallas_call | solution.py:467
  432.7 5.2 fusion.46
  441.3 5.3 copy.127
  453.1 6.7 %add_convert_fusion.x_ref = bf16[512,2048]{1,0:T(8,128)(2,1)} fusion(f32[512,2048]{1,0:T(8,128)} %fusion.48, f32[512,2048]{1,0:T(8,128)} %fusion.46, bf16[2048,512]{1,0:T(8,128)(2,1)} %param.21, bf16[512,1536]{1,0:T(8,128)(2,1)S(1)} %copy-done.7), kind=kOutput, calls=%fused_computation.50 | convolution fusion | flops 1076887552 | bytes 13107200 | tf_op jit(solution)/shard_map/dot_general | solution.py:831
  459.8 106.6 %sum_and_scatter.3 = (bf16[512,2048]{1,0:T(8,128)(2,1)}, f32[256,1024]{1,0:T(8,128)}, f32[256,2048]{1,0:T(8,128)}, f32[256,1536]{1,0:T(8,128)}, f32[256,512]{1,0:T(8,128)}, /*index=5*/f32[8,128]{1,0:T(8,128)}) custom-call(bf16[512,2048]{1,0:T(8,128)(2,1)} %add_convert_fusion.x_ref, bf16[2048,512]{1,0:T(8,128)(2,1)} %bitcast.140, ...), custom_call_target="tpu_custom_call" | custom-call | tf_op jit(solution)/shard_map/sum_and_scatter/pallas_call | solution.py:467
  566.4 4.1 copy.126
  570.5 5.0 fusion.32
  575.5 5.3 copy.128
  (185 shorter events, 101.3 us)
Async XLA Ops:
  7.2 47.6 %all-gather.3.cloned.1.call-start = ((), (), s32[]{:S(2)}) async-start(), calls=%async_computation | async-start | bytes 2621440 | tf_op jit(solution)/shard_map/all_gather | solution.py:923
  12.7 15.2 %copy-start.24 = (f32[4,128]{1,0:T(4,128)S(1)}, f32[4,128]{1,0:T(4,128)}, u32[]{:S(2)}) copy-start(f32[4,128]{1,0:T(4,128)} %param.23) | copy-start | bytes 6148
  33.9 45.7 %all-gather.5.cloned.1.call-start = ((), (), s32[]{:S(2)}) async-start(), calls=%async_computation.1 | async-start | bytes 2621440 | tf_op jit(solution)/shard_map/all_gather | solution.py:924
  38.5 5.3 copy-start.25
  41.1 5.8 copy-start.8
  54.5 28.9 %copy-start.18 = (f32[4,512,128]{2,1,0:T(8,128)S(1)}, f32[4,512,128]{2,1,0:T(8,128)}, u32[]{:S(2)}) copy-start(f32[4,512,128]{2,1,0:T(8,128)} %custom-call.2) | copy-start | bytes 3145732
  176.5 6.2 %copy-start = (bf16[1,512,2048]{1,2,0:T(8,128)(2,1)S(1)}, bf16[1,512,2048]{1,2,0:T(8,128)(2,1)}, u32[]{:S(2)}) copy-start(bf16[1,512,2048]{1,2,0:T(8,128)(2,1)} %copy.106) | copy-start | bytes 6291460
  176.5 6.2 %copy-start.21 = (f32[2048]{0:T(1024)S(1)}, f32[2048]{0:T(1024)}, u32[]{:S(2)}) copy-start(f32[2048]{0:T(1024)} %param.25) | copy-start | bytes 24580
  182.7 10.3 %slice-start.2 = ((s8[8388608]{0:T(1024)(128)(4,1)}), s8[4194304]{0:T(1024)(128)(4,1)S(1)}, s32[]{:S(2)}) async-start(s8[8388608]{0:T(1024)(128)(4,1)} %bitcast.161), calls=%async_computation.4 | async-start | bytes 8388608
  185.3 7.7 %copy-start.6 = (bf16[512,2048]{0,1:T(8,128)(2,1)}, bf16[512,2048]{0,1:T(8,128)(2,1)S(1)}, u32[]{:S(2)}) copy-start(bf16[512,2048]{0,1:T(8,128)(2,1)S(1)} %fusion.35) | copy-start | bytes 6291460
  185.3 7.8 %slice-start.3 = ((s8[8388608]{0:T(1024)(128)(4,1)}), s8[4194304]{0:T(1024)(128)(4,1)S(1)}, s32[]{:S(2)}) async-start(s8[8388608]{0:T(1024)(128)(4,1)} %bitcast.161), calls=%async_computation.5 | async-start | bytes 8388608
  185.3 15.6 %slice-start = ((s8[8388608]{0:T(1024)(128)(4,1)}), s8[4194304]{0:T(1024)(128)(4,1)S(1)}, s32[]{:S(2)}) async-start(s8[8388608]{0:T(1024)(128)(4,1)} %bitcast.159), calls=%async_computation.2 | async-start | bytes 8388608
  193.1 6.5 %copy-start.30 = (f32[512,2048]{1,0:T(8,128)}, f32[512,2048]{1,0:T(8,128)S(1)}, u32[]{:S(2)}) copy-start(f32[512,2048]{1,0:T(8,128)S(1)} %fusion.73) | copy-start | bytes 12582916
  193.1 7.8 %slice-start.1 = ((s8[8388608]{0:T(1024)(128)(4,1)}), s8[4194304]{0:T(1024)(128)(4,1)S(1)}, s32[]{:S(2)}) async-start(s8[8388608]{0:T(1024)(128)(4,1)} %bitcast.159), calls=%async_computation.3 | async-start | bytes 8388608
  266.9 6.4 %copy-start.2 = (bf16[1,512,2048]{1,2,0:T(8,128)(2,1)S(1)}, bf16[1,512,2048]{1,2,0:T(8,128)(2,1)}, u32[]{:S(2)}) copy-start(bf16[1,512,2048]{1,2,0:T(8,128)(2,1)} %copy.119) | copy-start | bytes 6291460
  266.9 6.4 %copy-start.22 = (f32[2048]{0:T(1024)S(1)}, f32[2048]{0:T(1024)}, u32[]{:S(2)}) copy-start(f32[2048]{0:T(1024)} %param.29) | copy-start | bytes 24580
  271.0 5.5 copy-start.1
  271.0 5.5 copy-start.4
  271.0 5.5 copy-start.5
  293.5 7.8 %copy-start.11 = (bf16[512,2048]{1,0:T(8,128)(2,1)S(1)}, bf16[512,2048]{1,0:T(8,128)(2,1)}, u32[]{:S(2)}) copy-start(bf16[512,2048]{1,0:T(8,128)(2,1)} %get-tuple-element.245.refs_4_) | copy-start | bytes 6291460
  432.7 5.2 copy-start.7
  575.5 5.3 copy-start.23
  580.8 6.0 copy-start.20
  582.1 7.5 %copy-start.15 = (f32[256,2048]{1,0:T(8,128)S(1)}, f32[256,2048]{1,0:T(8,128)}, u32[]{:S(2)}) copy-start(f32[256,2048]{1,0:T(8,128)} %get-tuple-element.401) | copy-start | bytes 6291460
  (13 other events, 44.0 us)
Sparse Core Ops, SparseCore 0:
  34.0 20.7 all-gather.2
  56.9 22.5 all-gather.4

commit v4 on v3

--- a/solution.py
+++ b/solution.py
@@ -822,6 +822,240 @@
     )
 
 
+def front(tokens, w_query, w_key, w_value, w_output, qgain, kgain, cosine, sine, order, cid):
+    rows, width = tokens.shape
+    local = w_query.shape[1]
+    head_dim = lanes
+    heads = local // head_dim
+    nx = lax.axis_size("ctx") // 2
+    count = nx * 2 * rows
+    n_tp = lax.axis_size("tp")
+    small = LineSmall(n_tp, rows)
+    line = LineSum(n_tp, rows, width)
+    n_small, n_line = len(small.scratch()), len(line.scratch())
+    scale = head_dim ** (-0.5)
+    group = rows // 2
+
+    def body(
+        tok_hbm, wq_hbm, wk_hbm, wv_hbm, wo_hbm, qg_ref, kg_ref, cos_ref, sin_ref, order_ref,
+        qrot_out, key_out, value_out, qn_out, kn_out, attn_out, sc_out, lse_out, proj_out,
+        tok, w3, wo, qn, kn, qrot, keys, values, peak, total, acc, attn, loads, stores,
+        sx, dx, sm, dm, sf, df, *rest,
+    ):
+        small.bind(rest[:n_small])
+        line.bind(rest[n_small : n_small + n_line])
+        copies = [
+            pltpu.make_async_copy(src, dst, loads.at[i])
+            for i, (src, dst) in enumerate(
+                [(tok_hbm, tok), (wv_hbm, w3.at[2]), (wq_hbm, w3.at[0]), (wk_hbm, w3.at[1]),
+                 (wo_hbm, wo)]
+            )
+        ]
+        for copy in copies:
+            copy.start()
+        ctx = lax.axis_index("ctx")
+        mx, core = ctx // 2, lax.rem(ctx, 2)
+        mate = {"ctx": mx * 2 + 1 - core}
+
+        def peer(d):
+            return {"ctx": lax.rem(mx + d, nx) * 2 + core}
+
+        bar = pltpu.get_barrier_semaphore()
+        pl.semaphore_signal(bar, inc=1, device_id=mate, device_id_type=MESH)
+        for d in range(1, nx):
+            pl.semaphore_signal(bar, inc=1, device_id=peer(d), device_id_type=MESH)
+        peers = small.greet(bar) + nx
+
+        def at(x, owner):
+            return pl.ds(pl.multiple_of((x * 2 + owner) * rows, rows), rows)
+
+        mine = at(mx, core)
+        boxes = [keys, values]
+
+        def to_peer(b, d):
+            box = boxes[b]
+            return remote(
+                box.at[mine], box.at[mine], sx.at[b, d - 1], dx.at[b, d - 1], peer(d)
+            )
+
+        def from_peer(b, d):
+            box = boxes[b]
+            rs = at(lax.rem(mx + nx - d, nx), core)
+            return remote(box.at[rs], box.at[rs], sx.at[b, d - 1], dx.at[b, d - 1], peer(d))
+
+        def to_mate(b):
+            box = boxes[b]
+            return remote(box.at[mine], box.at[mine], sm.at[b], dm.at[b], mate)
+
+        def from_mate(b):
+            box = boxes[b]
+            rs = at(mx, 1 - core)
+            return remote(box.at[rs], box.at[rs], sm.at[b], dm.at[b], mate)
+
+        def pass_on(b, d):
+            box = boxes[b]
+            rs = at(lax.rem(mx + nx - d, nx), core)
+            return remote(box.at[rs], box.at[rs], sf.at[b, d - 1], df.at[b, d - 1], mate)
+
+        def passed(b, d):
+            box = boxes[b]
+            rs = at(lax.rem(mx + nx - d, nx), 1 - core)
+            return remote(box.at[rs], box.at[rs], sf.at[b, d - 1], df.at[b, d - 1], mate)
+
+        copies[0].wait()
+        copies[1].wait()
+        values[mine] = jnp.dot(tok[...], w3[2], preferred_element_type=f32).astype(bf16)
+        pl.semaphore_wait(bar, peers)
+        for d in range(1, nx):
+            to_peer(1, d).start()
+        to_mate(1).start()
+        copies[2].wait()
+        qn[...] = jnp.dot(tok[...], w3[0], preferred_element_type=f32)
+        copies[3].wait()
+        kn[...] = jnp.dot(tok[...], w3[1], preferred_element_type=f32)
+
+        def squares(ref):
+            acc_sq = jnp.zeros((rows, 1), f32)
+            for h in range(heads):
+                part = ref[:, h * head_dim : (h + 1) * head_dim]
+                acc_sq = acc_sq + jnp.sum(part * part, axis=1, keepdims=True)
+            return acc_sq
+
+        sums = small.total(lane_pair(squares(qn), squares(kn), rows))
+        scales = lax.rsqrt(sums * (1.0 / width) + norm_eps)
+        sc_out[...] = scales
+
+        def rotated(ref, column, gain_ref, h):
+            hs = slice(h * head_dim, (h + 1) * head_dim)
+            norm = ref[:, hs] * sc_out[:, column : column + 1]
+            ref[:, hs] = norm
+            norm = norm * gain_ref[:, hs]
+            return (
+                norm * cos_ref[...] + pltpu.roll(norm, head_dim // 2, 1) * sin_ref[...]
+            ).astype(bf16)
+
+        for h in range(heads):
+            keys[mine, h * head_dim : (h + 1) * head_dim] = rotated(kn, 1, kg_ref, h)
+        for d in range(1, nx):
+            to_peer(0, d).start()
+        to_mate(0).start()
+        for h in range(heads):
+            qrot[:, h * head_dim : (h + 1) * head_dim] = rotated(qn, 0, qg_ref, h)
+        peak[...] = jnp.full_like(peak, masked_score)
+        total[...] = jnp.zeros_like(total)
+        acc[...] = jnp.zeros_like(acc)
+
+        def places(block, shape, axis):
+            spot = lax.broadcasted_iota(jnp.int32, shape, axis)
+            first, second = order_ref[0, block * 2], order_ref[0, block * 2 + 1]
+            return jnp.where(spot < group, first * group + spot, (second - 1) * group + spot)
+
+        def attend(x, owner):
+            block = x * 2 + owner
+            rs = at(x, owner)
+
+            def one(h, carry):
+                hs = pl.ds(pl.multiple_of(h * head_dim, head_dim), head_dim)
+                score = dot_nt(qrot[:, hs], keys[rs, hs]) * scale
+                seen = places(block, (1, rows), 1) <= places(ctx, (rows, 1), 0)
+                old = peak[h]
+                new = jnp.maximum(
+                    old, jnp.max(jnp.where(seen, score, masked_score), axis=1, keepdims=True)
+                )
+                share = jnp.where(seen, jnp.exp(score - new), 0.0)
+                fade = jnp.exp(old - new)
+                peak[h] = new
+                total[h] = total[h] * fade + jnp.sum(share, axis=1, keepdims=True)
+                acc[:, hs] = acc[:, hs] * fade + jnp.dot(
+                    share.astype(bf16), values[rs, hs], preferred_element_type=f32
+                )
+                return carry
+
+            lax.fori_loop(0, heads, one, 0)
+
+        attend(mx, core)
+        for d in range(1, nx):
+            from_peer(1, d).wait_recv()
+            pass_on(1, d).start()
+        from_mate(1).wait_recv()
+        from_mate(0).wait_recv()
+        attend(mx, 1 - core)
+        for d in range(1, nx):
+            from_peer(0, d).wait_recv()
+            pass_on(0, d).start()
+            attend(lax.rem(mx + nx - d, nx), core)
+        for d in range(1, nx):
+            passed(1, d).wait_recv()
+            passed(0, d).wait_recv()
+            attend(lax.rem(mx + nx - d, nx), 1 - core)
+
+        lane = lax.broadcasted_iota(jnp.int32, (rows, lanes), 1)
+        logs = jnp.zeros((rows, lanes), f32)
+        for h in range(heads):
+            hs = slice(h * head_dim, (h + 1) * head_dim)
+            attn[:, hs] = (acc[:, hs] / total[h]).astype(bf16)
+            logs = jnp.where(lane == h, peak[h] + jnp.log(total[h]), logs)
+        lse_out[...] = jnp.transpose(logs)[:8]
+        outs = [
+            pltpu.make_async_copy(src, dst, stores.at[i])
+            for i, (src, dst) in enumerate(
+                [(qrot, qrot_out), (keys, key_out), (values, value_out), (qn, qn_out),
+                 (kn, kn_out), (attn, attn_out)]
+            )
+        ]
+        for copy in outs:
+            copy.start()
+        copies[4].wait()
+        for j in range(n_tp):
+            line.own[j] = jnp.dot(
+                attn[...], wo[:, j * line.part : (j + 1) * line.part], preferred_element_type=f32
+            ).astype(bf16)
+
+        def one(t, carry):
+            line.step(t)
+            return carry
+
+        lax.fori_loop(0, line.steps, one, 0)
+        line.drain()
+        line.store(proj_out)
+        for copy in outs:
+            copy.wait()
+        for b in range(2):
+            to_mate(b).wait_send()
+            for d in range(1, nx):
+                to_peer(b, d).wait_send()
+                pass_on(b, d).wait_send()
+
+    sem = pltpu.SemaphoreType.DMA
+    hbm = pl.BlockSpec(memory_space=pl.ANY)
+    block = jax.ShapeDtypeStruct
+    return pl.pallas_call(
+        body,
+        out_shape=[
+            block((rows, local), bf16), block((count, local), bf16), block((count, local), bf16),
+            block((rows, local), f32), block((rows, local), f32), block((rows, local), bf16),
+            block((rows, lanes), f32), block((8, rows), f32), block((rows, width), bf16),
+        ],
+        in_specs=[hbm] * 5 + [vmem_spec()] * 4 + [pl.BlockSpec(memory_space=pltpu.SMEM)],
+        out_specs=[hbm] * 6 + [vmem_spec()] * 3,
+        scratch_shapes=[
+            pltpu.VMEM((rows, width), bf16), pltpu.VMEM((3, width, local), bf16),
+            pltpu.VMEM((local, width), bf16), pltpu.VMEM((rows, local), f32),
+            pltpu.VMEM((rows, local), f32), pltpu.VMEM((rows, local), bf16),
+            pltpu.VMEM((count, local), bf16), pltpu.VMEM((count, local), bf16),
+            pltpu.VMEM((heads, rows, 1), f32), pltpu.VMEM((heads, rows, 1), f32),
+            pltpu.VMEM((rows, local), f32), pltpu.VMEM((rows, local), bf16),
+            sem((5,)), sem((6,)),
+            sem((2, nx - 1)), sem((2, nx - 1)), sem((2,)), sem((2,)),
+            sem((2, nx - 1)), sem((2, nx - 1)),
+        ] + small.scratch() + line.scratch(),
+        compiler_params=pltpu.CompilerParams(
+            collective_id=cid, has_side_effects=True, vmem_limit_bytes=62 * 2**20
+        ),
+        name="front",
+    )(tokens, w_query, w_key, w_value, w_output, qgain, kgain, cosine, sine, order)
+
+
 norm_eps = 1e-06
 rope_base = 500000.0
 masked_score = -1e30
@@ -838,36 +1072,11 @@
     return (jnp.cos(angle), jnp.sin(angle))
 
 
-def rotate(heads_in, cosine, sine):
-    half = heads_in.shape[-1] // 2
-    first, second = (heads_in[..., :half], heads_in[..., half:])
-    cosine, sine = (cosine[:, None, :], sine[:, None, :])
-    return jnp.concatenate(
-        [first * cosine - second * sine, second * cosine + first * sine], axis=-1
-    )
-
-
-def unrotate(grads_in, cosine, sine):
-    half = grads_in.shape[-1] // 2
-    first, second = (grads_in[..., :half], grads_in[..., half:])
-    cosine, sine = (cosine[:, None, :], sine[:, None, :])
-    return jnp.concatenate(
-        [first * cosine + second * sine, second * cosine - first * sine], axis=-1
-    )
-
-
 def key_positions(order, first_row, count, group):
     row_ids = first_row + jnp.arange(count, dtype=jnp.int32)
     slots = row_ids // group
     picks = slots[:, None] == jnp.arange(order.shape[0], dtype=jnp.int32)[None, :]
     return jnp.sum(jnp.where(picks, order[None, :], 0), axis=1) * group + row_ids % group
-
-
-def gather_pair(keys, values):
-    return (
-        lax.all_gather(keys, "ctx", axis=0, tiled=True),
-        lax.all_gather(values, "ctx", axis=0, tiled=True),
-    )
 
 
 def per_device(
@@ -892,70 +1101,18 @@
     heads, head_dim = query_gain.shape
     local = heads * head_dim
     group = row_count // 2
-    scale = head_dim ** (-0.5)
     query_pos = key_positions(order, lax.axis_index("ctx") * row_count, row_count, group)
     cosine, sine = rope_tables(query_pos, head_dim)
     inputs = inputs_bf.astype(jnp.float32)
-    query = matmul(inputs_bf, w_query)
-    keyraw = matmul(inputs_bf, w_key)
-    values = matmul(inputs_bf, w_value).astype(jnp.bfloat16)
-    query_sq, key_sq = lax.psum(
-        (jnp.sum(query * query, axis=1), jnp.sum(keyraw * keyraw, axis=1)), "tp"
-    )
-    query_scale = lax.rsqrt(query_sq / width + norm_eps)
-    key_scale = lax.rsqrt(key_sq / width + norm_eps)
-    query_norm = query * query_scale[:, None]
-    key_norm = keyraw * key_scale[:, None]
     qgain = query_gain.reshape(local)
     kgain = key_gain.reshape(local)
-    query_rot = rotate(
-        (query_norm * qgain).reshape(row_count, heads, head_dim), cosine, sine
-    ).astype(jnp.bfloat16)
-    key_rot = rotate((key_norm * kgain).reshape(row_count, heads, head_dim), cosine, sine).astype(
-        jnp.bfloat16
+    angle_cos = jnp.concatenate([cosine, cosine], axis=1)
+    angle_sin = jnp.concatenate([-sine, sine], axis=1)
+    (query_rot, whole_keys, whole_values, query_norm, key_norm, attn_flat, scales, lse,
+     proj_sum) = front(
+        inputs_bf, w_query, w_key, w_value, w_output, qgain[None], kgain[None], angle_cos,
+        angle_sin, group_order, 1,
     )
-    key_flat = key_rot.reshape(row_count, local)
-    start_state = (
-        jnp.full((heads, row_count), masked_score, jnp.float32),
-        jnp.zeros((heads, row_count), jnp.float32),
-        jnp.zeros((heads, row_count, head_dim), jnp.float32),
-    )
-    keys_in = lax.all_gather(key_flat, "ctx", axis=0, tiled=True)
-    values_in = lax.all_gather(values, "ctx", axis=0, tiled=True)
-    count = keys_in.shape[0]
-    attend_block = 512
-    keys_in = keys_in.reshape(count // attend_block, attend_block, heads, head_dim)
-    values_in = values_in.reshape(count // attend_block, attend_block, heads, head_dim)
-    key_pos = key_positions(order, jnp.int32(0), count, group).reshape(
-        count // attend_block, attend_block
-    )
-
-    def one_block(state, item):
-        peak_old, total, accum = state
-        key_block, value_block, pos_block = item
-        scores = (
-            jnp.einsum("qhd,khd->hqk", query_rot, key_block, preferred_element_type=jnp.float32)
-            * scale
-        )
-        mask = (pos_block[None, :] <= query_pos[:, None])[None]
-        peak = jnp.maximum(peak_old, jnp.max(jnp.where(mask, scores, masked_score), axis=2))
-        share = jnp.where(mask, jnp.exp(scores - peak[:, :, None]), 0.0)
-        fade = jnp.exp(peak_old - peak)
-        total = total * fade + jnp.sum(share, axis=2)
-        accum = accum * fade[:, :, None] + jnp.einsum(
-            "hqk,khd->hqd",
-            share.astype(jnp.bfloat16),
-            value_block,
-            preferred_element_type=jnp.float32,
-        )
-        return ((peak, total, accum), None)
-
-    state, unused = lax.scan(one_block, start_state, (keys_in, values_in, key_pos))
-    peak, total, accum = state
-    log_total = peak + jnp.log(total)
-    mixed = (accum / total[:, :, None]).astype(jnp.bfloat16)
-    attn_flat = mixed.transpose(1, 0, 2).reshape(row_count, local)
-    proj_sum = tp_sum(matmul(attn_flat, w_output), 1)
     proj = proj_sum.astype(f32)
     attn_scale = lax.rsqrt(jnp.mean(proj * proj, axis=1) + norm_eps)
     attn_norm = proj * attn_scale[:, None]
@@ -994,14 +1151,8 @@
         [inner.shape[1], half * 2 * lanes],
         3,
     )
-    whole_keys = keys_in.reshape(count, local)
-    whole_values = values_in.reshape(count, local)
-    angle_cos = jnp.concatenate([cosine, cosine], axis=1)
-    angle_sin = jnp.concatenate([-sine, sine], axis=1)
-    lse = jnp.pad(log_total, ((0, 8 - heads), (0, 0)))
-    scales = jnp.stack([query_scale, key_scale], axis=1)
     d_qkv, d_proj_t, d_attn_gain, d_query_gain, d_key_gain = attention_back(
-        back, out_grad[0], proj_sum, attn_gain[None], w_output, query_rot.reshape(row_count, local),
+        back, out_grad[0], proj_sum, attn_gain[None], w_output, query_rot,
         whole_keys, whole_values, attn_flat, lse, query_pos[None], group_order,
         query_norm, key_norm, scales, qgain[None], kgain[None], angle_cos, angle_sin, 5,
     )

time: 604 us -> 530 us (0.88)
  Pallas kernels: 347 us -> 386 us
  matrix products: 94.9 us -> 58.4 us
  waiting for transfers between devices: 22.3 us -> 0 us
  local copies, waits for them, and re-layouts: 65 us -> 45.9 us
  between operations: 15.1 us -> 1.43 us
  blocking collectives: 13.5 us -> 0 us
  other arithmetic: 40.2 us -> 28.5 us
    pallas_call x0 -> x1, Pallas kernels: none -> 102 us  [front(): pl.pallas_call(body, out_shape=[block((rows, local), bf16), block((count,...]
    pallas_call x5 -> x4, Pallas kernels: 347 us -> 285 us  [comm_call(): pl.pallas_call(body, out_shape=outs, in_specs=[pl.BlockSpec(memory_space=...]
    all_gather x2 -> x0, waiting for transfers between devices: 22.3 us -> none  [the longest x1 22.1 us: per_device(): values_in = lax.all_gather(values, 'ctx', axis=0, tiled=True)]
    dot_general x13 -> x9, matrix products: 80.1 us -> 58.4 us  [matmul(): return jnp.dot(left, right, preferred_element_type=jnp.float32)]
    dot_general x8 -> x0, matrix products: 14.7 us -> none  [the longest x4 7.94 us: one_block(): jnp.einsum('qhd,khd->hqk', query_rot, key_block, preferred_element_type=j...]
    psum x1 -> x0, blocking collectives: 13.5 us -> none  [per_device(): lax.psum((jnp.sum(query * query, axis=1), jnp.sum(keyraw * keyraw, axis=1...]
    reshape x4 -> x0, local copies, waits for them, and re-layouts: 8.53 us -> none  [the longest x1 3.95 us: per_device(): values_in.reshape(count // attend_block, attend_block, heads, head_dim)]
    pallas_call x5 -> x4, local copies, waits for them, and re-layouts: 16.7 us -> 12.8 us  [comm_call(): pl.pallas_call(body, out_shape=outs, in_specs=[pl.BlockSpec(memory_space=...]
  transfers between devices with their start and end apart: 2 -> 0, of which waited for: 2 -> 0; matrix products, arithmetic and copies ran while one was open for 4% -> 0% of each run, Pallas kernels for 0% -> 0%
where the time goes in v4:
time: 530 us; the launch traced here: 521 us
  Pallas kernels  386 us (73%)
  matrix products  58.4 us (11%)
  local copies, waits for them, and re-layouts  45.9 us (9%)
  other arithmetic  28.5 us (5%)
    pallas_call x4, Pallas kernels, comm_call(): pl.pallas_call(body, out_shape=outs, in_specs=[pl.BlockSpec(memory_space=...  285 us
    pallas_call x1, Pallas kernels, front(): pl.pallas_call(body, out_shape=[block((rows, local), bf16), block((count,...  102 us
    dot_general x9, matrix products, matmul(): return jnp.dot(left, right, preferred_element_type=jnp.float32)  58.4 us
    unnamed x60, local copies, waits for them, and re-layouts  26.3 us
    pallas_call x4, local copies, waits for them, and re-layouts, comm_call(): pl.pallas_call(body, out_shape=outs, in_specs=[pl.BlockSpec(memory_space=...  12.8 us

profile of v4, /device:TPU:0, one launch (start us, length us, event | category | flops | bytes accessed | tf_op | source)
XLA Modules:
  0.0 520.6 jit_solution(17570718205442042518)
XLA Ops:
  4.2 3.9 copy.59
  10.6 101.8 %front.1 = (bf16[512,512]{1,0:T(8,128)(2,1)}, bf16[2048,512]{1,0:T(8,128)(2,1)}, bf16[2048,512]{1,0:T(8,128)(2,1)}, f32[512,512]{1,0:T(8,128)}, f32[512,512]{1,0...) custom-call(bf16[512,2048]{1,0:T(8,128)(2,1)} %bitcast.60, ...), custom_call_target="tpu_custom_call" | custom-call | tf_op jit(solution)/shard_map/front/pallas_call | solution.py:1032
  112.4 4.1 copy.57
  121.2 7.7 %fusion.37 = f32[512,2048]{1,0:T(8,128)S(1)} fusion(bf16[512,2048]{0,1:T(8,128)(2,1)S(1)} %fusion.17, bf16[2048,2048]{1,0:T(8,128)(2,1)} %param.24), kind=kOutput, calls=%fused_computation.79 | convolution fusion | flops 4294967296 | bytes 14680064 | tf_op jit(solution)/shard_map/dot_general | solution.py:1065
  128.9 6.5 %multiply_convert_fusion.2 = (bf16[512,2048]{1,0:T(8,128)(2,1)S(1)}, f32[512,2048]{1,0:T(8,128)}) fusion(f32[512,2048]{1,0:T(8,128)S(1)} %fusion.37, bf16[512,2048]{0,1:T(8,128)(2,1)S(1)} %fusion.17, bf16[2048,2048]{1,0:T(8,128)(2,1)S(1)} %bitcast.78), kind=kOutput, calls=%fused_computation.27 | convolution fusion | flops 4301258752 | bytes 20971520 | tf_op jit(solution)/shard_map/dot_general | solution.py:1065
  136.8 5.7 %convolution_convert_fusion.x_ref = bf16[512,2048]{1,0:T(8,128)(2,1)} fusion(bf16[512,2048]{1,0:T(8,128)(2,1)S(1)} %get-tuple-element.116.refs_2_, bf16[2048,2048]{1,0:T(8,128)(2,1)S(1)} %bitcast.76), kind=kOutput, calls=%fused_computation.31 | convolution fusion | flops 4296015872 | bytes 12582912 | tf_op jit(solution)/shard_map/dot_general | solution.py:1065
  142.5 59.8 %tp_sum.1 = bf16[512,2048]{1,0:T(8,128)(2,1)} custom-call(bf16[512,2048]{1,0:T(8,128)(2,1)} %convolution_convert_fusion.x_ref), custom_call_target="tpu_custom_call" | custom-call | tf_op jit(solution)/shard_map/tp_sum/pallas_call | solution.py:467
  202.3 4.1 copy.58
  208.5 3.0 fusion.15
  211.5 14.9 %multiply_convert_fusion = (bf16[512,2048]{1,0:T(8,128)(2,1)}, bf16[512,2048]{1,0:T(8,128)(2,1)}) fusion(f32[512,2048]{1,0:T(8,128)} %copy-done.21, f32[512,2048]{1,0:T(8,128)} %get-tuple-element.117, bf16[2048,2048]{1,0:T(8,128)(2,1)} %param.26, bf16[512,2048]{0,1:T(8,128)(2,1)} %copy.58, bf16[1,512,2048]{1,2,0:T(8,128)(2,1)S(1)} %copy-done.2, ...), kind=kOutput, calls=%fused_computation.25 | convolution fusion | flops 4316987392 | bytes 25178112 | tf_op jit(solution)/shard_map/dot_general | solution.py:1065
  226.4 5.3 %fusion.32 = (bf16[2048,512]{1,0:T(8,128)(2,1)}, f32[1,512,2048]{1,2,0:T(8,128)}) fusion(f32[512]{0:T(512)S(1)} %broadcast_multiply_fusion, bf16[512,2048]{0,1:T(8,128)(2,1)} %copy.58, f32[2048]{0:T(1024)S(1)} %copy-done.16, bf16[1,512,2048]{1,2,0:T(8,128)(2,1)S(1)} %copy-done.2, f32[512]{0:T(512)S(1)} %add_rsqrt_fusion, f32[2048]{0:T(1024)S(1)} %copy-done.15, ...), kind=kLoop, calls=%fused_computation.75 | loop fusion | flops 15728640 | bytes 14702592 | tf_op jit(solution)/shard_map/transpose | solution.py:1145
  231.7 5.5 %copy.65 = f32[1,512,2048]{2,1,0:T(8,128)} copy(f32[1,512,2048]{1,2,0:T(8,128)} %get-tuple-element.103) | data formatting | bytes 8388608
  237.2 7.2 %fusion.38 = f32[512,2048]{1,0:T(8,128)S(1)} fusion(bf16[512,2048]{1,0:T(8,128)(2,1)S(1)} %copy-done.7, bf16[2048,2048]{1,0:T(8,128)(2,1)} %param.24), kind=kOutput, calls=%fused_computation.80 | convolution fusion | flops 4294967296 | bytes 14680064 | tf_op jit(solution)/shard_map/dot_general | solution.py:1065
  244.5 9.4 %add_convert_fusion.1.x_ref = bf16[512,2048]{1,0:T(8,128)(2,1)} fusion(f32[512,2048]{1,0:T(8,128)S(1)} %fusion.38, bf16[512,2048]{1,0:T(8,128)(2,1)S(1)} %copy-done.10, bf16[2048,2048]{1,0:T(8,128)(2,1)} %param.25), kind=kOutput, calls=%fused_computation.24 | convolution fusion | flops 4297064448 | bytes 16777216 | tf_op jit(solution)/shard_map/dot_general | solution.py:1065
  253.9 71.1 %sum_and_scatter.2 = (bf16[512,2048]{1,0:T(8,128)(2,1)}, f32[256,2048]{1,0:T(8,128)}, f32[256,1024]{1,0:T(8,128)}) custom-call(bf16[512,2048]{1,0:T(8,128)(2,1)} %add_convert_fusion.1.x_ref, bf16[2048,512]{1,0:T(8,128)(2,1)} %get-tuple-element.102.refs_0_, bf16[2048,512]{1,0:T(8,128)(2,1)} %bitcast.58, bf16[512,2048]{1,0:T(8,128)(2,1)} %copy-done.11, ...), custom_call_target="tpu_custom_call" | custom-call | tf_op jit(solution)/shard_map/sum_and_scatter/pallas_call | solution.py:467
  325.0 47.3 %attention_back.1 = (bf16[512,1536]{1,0:T(8,128)(2,1)}, bf16[2048,512]{1,0:T(8,128)(2,1)}, f32[1,2048]{1,0:T(1,128)}, f32[1,512]{1,0:T(1,128)}, f32[1,512]{1,0:T(1,128)}) custom-call(bf16[512,2048]{1,0:T(8,128)(2,1)} %get-tuple-element.37.back_ref, bf16[512,2048]{1,0:T(8,128)(2,1)} %bitcast.61, bf16[512,2048]{1,0:T(8,128)(2,1)} %get-tuple-element.36.proj_ref, ...), custom_call_target="tpu_custom_call" | custom-call | tf_op jit(solution)/shard_map/attention_back/pallas_call | solution.py:467
  372.4 3.0 copy.68
  379.0 4.1 copy.60
  383.1 3.0 fusion.19
  390.5 106.5 %sum_and_scatter.3 = (bf16[512,2048]{1,0:T(8,128)(2,1)}, f32[256,1024]{1,0:T(8,128)}, f32[256,2048]{1,0:T(8,128)}, f32[256,1536]{1,0:T(8,128)}, f32[256,512]{1,0:T(8,128)}, /*index=5*/f32[8,128]{1,0:T(8,128)}) custom-call(bf16[512,2048]{1,0:T(8,128)(2,1)} %add_convert_fusion.x_ref, bf16[2048,512]{1,0:T(8,128)(2,1)} %bitcast.59, bf16[2048,512]{1,0:T(8,128)(2,1)} %bitcast.57, ...), custom_call_target="tpu_custom_call" | custom-call | tf_op jit(solution)/shard_map/sum_and_scatter/pallas_call | solution.py:467
  496.9 4.1 copy.64
  501.0 5.0 fusion.14
  506.0 5.4 %copy.66 = f32[1,512,2048]{2,1,0:T(8,128)} copy(f32[1,512,2048]{1,2,0:T(8,128)} %fusion.14) | data formatting | bytes 8388608
  514.9 2.8 pad_maximum_fusion
  (90 shorter events, 28.0 us)
Async XLA Ops:
  0.6 7.5 %copy-start.8 = (bf16[1,512,2048]{2,1,0:T(8,128)(2,1)S(1)}, bf16[1,512,2048]{2,1,0:T(8,128)(2,1)}, u32[]{:S(2)}) copy-start(bf16[1,512,2048]{2,1,0:T(8,128)(2,1)} %param.14) | copy-start | bytes 6291460
  112.4 6.2 %copy-start = (bf16[1,512,2048]{1,2,0:T(8,128)(2,1)S(1)}, bf16[1,512,2048]{1,2,0:T(8,128)(2,1)}, u32[]{:S(2)}) copy-start(bf16[1,512,2048]{1,2,0:T(8,128)(2,1)} %copy.55) | copy-start | bytes 6291460
  112.4 6.2 %copy-start.15 = (f32[2048]{0:T(1024)S(1)}, f32[2048]{0:T(1024)}, u32[]{:S(2)}) copy-start(f32[2048]{0:T(1024)} %param.23) | copy-start | bytes 24580
  118.6 10.3 %slice-start.2 = ((s8[8388608]{0:T(1024)(128)(4,1)}), s8[4194304]{0:T(1024)(128)(4,1)S(1)}, s32[]{:S(2)}) async-start(s8[8388608]{0:T(1024)(128)(4,1)} %bitcast.77), calls=%async_computation.2 | async-start | bytes 8388608
  121.1 7.7 %copy-start.4 = (bf16[512,2048]{0,1:T(8,128)(2,1)}, bf16[512,2048]{0,1:T(8,128)(2,1)S(1)}, u32[]{:S(2)}) copy-start(bf16[512,2048]{0,1:T(8,128)(2,1)S(1)} %fusion.17) | copy-start | bytes 6291460
  121.1 7.8 %slice-start.3 = ((s8[8388608]{0:T(1024)(128)(4,1)}), s8[4194304]{0:T(1024)(128)(4,1)S(1)}, s32[]{:S(2)}) async-start(s8[8388608]{0:T(1024)(128)(4,1)} %bitcast.77), calls=%async_computation.3 | async-start | bytes 8388608
  121.2 15.6 %slice-start = ((s8[8388608]{0:T(1024)(128)(4,1)}), s8[4194304]{0:T(1024)(128)(4,1)S(1)}, s32[]{:S(2)}) async-start(s8[8388608]{0:T(1024)(128)(4,1)} %bitcast.75), calls=%async_computation | async-start | bytes 8388608
  128.9 6.5 %copy-start.21 = (f32[512,2048]{1,0:T(8,128)}, f32[512,2048]{1,0:T(8,128)S(1)}, u32[]{:S(2)}) copy-start(f32[512,2048]{1,0:T(8,128)S(1)} %fusion.37) | copy-start | bytes 12582916
  128.9 7.9 %slice-start.1 = ((s8[8388608]{0:T(1024)(128)(4,1)}), s8[4194304]{0:T(1024)(128)(4,1)S(1)}, s32[]{:S(2)}) async-start(s8[8388608]{0:T(1024)(128)(4,1)} %bitcast.75), calls=%async_computation.1 | async-start | bytes 8388608
  202.3 6.2 %copy-start.2 = (bf16[1,512,2048]{1,2,0:T(8,128)(2,1)S(1)}, bf16[1,512,2048]{1,2,0:T(8,128)(2,1)}, u32[]{:S(2)}) copy-start(bf16[1,512,2048]{1,2,0:T(8,128)(2,1)} %copy.59) | copy-start | bytes 6291460
  202.3 6.2 %copy-start.16 = (f32[2048]{0:T(1024)S(1)}, f32[2048]{0:T(1024)}, u32[]{:S(2)}) copy-start(f32[2048]{0:T(1024)} %param.27) | copy-start | bytes 24580
  211.5 14.9 %copy-start.1 = (bf16[1,512,2048]{1,2,0:T(8,128)(2,1)S(1)}, bf16[1,512,2048]{1,2,0:T(8,128)(2,1)}, u32[]{:S(2)}) copy-start(bf16[1,512,2048]{1,2,0:T(8,128)(2,1)} %copy.55) | copy-start | bytes 6291460
  231.7 5.5 %copy-start.7 = (bf16[512,2048]{1,0:T(8,128)(2,1)S(1)}, bf16[512,2048]{1,0:T(8,128)(2,1)}, u32[]{:S(2)}) copy-start(bf16[512,2048]{1,0:T(8,128)(2,1)} %get-tuple-element.101.refs_3_) | copy-start | bytes 6291460
  237.2 7.2 %copy-start.10 = (bf16[512,2048]{1,0:T(8,128)(2,1)S(1)}, bf16[512,2048]{1,0:T(8,128)(2,1)}, u32[]{:S(2)}) copy-start(bf16[512,2048]{1,0:T(8,128)(2,1)} %get-tuple-element.100.refs_4_) | copy-start | bytes 6291460
  372.4 3.6 copy-start.20
  372.4 4.2 copy-start.19
  372.4 4.9 copy-start.18
  372.4 10.7 %copy-start.5 = (bf16[512,1536]{1,0:T(8,128)(2,1)S(1)}, bf16[512,1536]{1,0:T(8,128)(2,1)}, u32[]{:S(2)}) copy-start(bf16[512,1536]{1,0:T(8,128)(2,1)} %get-tuple-element.46.refs_5_) | copy-start | bytes 4718596
  383.1 3.0 copy-start.9
  496.9 4.1 copy-start.3
  506.0 5.4 %copy-start.17 = (f32[8,128]{1,0:T(8,128)S(1)}, f32[8,128]{1,0:T(8,128)}, u32[]{:S(2)}) copy-start(f32[8,128]{1,0:T(8,128)} %get-tuple-element.53) | copy-start | bytes 12292
  506.0 8.9 %copy-start.14 = (f32[256,1024]{1,0:T(8,128)S(1)}, f32[256,1024]{1,0:T(8,128)}, u32[]{:S(2)}) copy-start(f32[256,1024]{1,0:T(8,128)} %get-tuple-element.55) | copy-start | bytes 3145732
  512.7 6.2 %copy-start.12 = (f32[256,2048]{1,0:T(8,128)S(1)}, f32[256,2048]{1,0:T(8,128)}, u32[]{:S(2)}) copy-start(f32[256,2048]{1,0:T(8,128)} %get-tuple-element.143) | copy-start | bytes 6291460
  514.9 2.9 copy-start.13
  (2 other events, 3.0 us)

commit v5 on v4

--- a/solution.py
+++ b/solution.py
@@ -4,6 +4,25 @@
 from jax.sharding import PartitionSpec as P
 from jax.experimental import pallas as pl
 from jax.experimental.pallas import tpu as pltpu
+
+norm_eps = 1e-06
+rope_base = 500000.0
+masked_score = -1e30
+
+
+def rope_tables(positions, head_dim):
+    half = head_dim // 2
+    rates = rope_base ** (-(jnp.arange(half, dtype=jnp.float32) * 2.0 / head_dim))
+    angle = positions.astype(jnp.float32)[:, None] * rates[None, :]
+    return (jnp.cos(angle), jnp.sin(angle))
+
+
+def key_positions(order, first_row, count, group):
+    row_ids = first_row + jnp.arange(count, dtype=jnp.int32)
+    slots = row_ids // group
+    picks = slots[:, None] == jnp.arange(order.shape[0], dtype=jnp.int32)[None, :]
+    return jnp.sum(jnp.where(picks, order[None, :], 0), axis=1) * group + row_ids % group
+
 
 MESH = pl.DeviceIdType.MESH
 bf16 = jnp.bfloat16
@@ -12,7 +31,6 @@
 row_blocks = 16
 row_chains = 8
 pace = 6
-norm_eps = 1e-06
 
 
 def remote(src, dst, send, recv, where):
@@ -178,6 +196,16 @@
             return carry
 
         lax.fori_loop(0, self.total, one, 0)
+
+    def ship(self, out_ref, sems, base):
+        copies = []
+        for j in range(self.n):
+            cols = pl.ds(j * self.part, self.part)
+            copy = pltpu.make_async_copy(self.res.at[j], out_ref.at[:, cols], sems.at[base + j])
+            copy.start()
+            copies.append(copy)
+        for copy in copies:
+            copy.wait()
 
     def store(self, out_ref):
         for j in range(self.n):
@@ -478,85 +506,6 @@
         ),
         name=name,
     )(*args)
-
-
-def tp_sum(partial, cid):
-    rows, width = partial.shape
-    line = LineSum(lax.axis_size("tp"), rows, width)
-
-    def body(x_ref, out_ref, *refs):
-        line.bind(refs)
-        bar = pltpu.get_barrier_semaphore()
-        peers = line.greet(bar)
-        line.load(x_ref)
-        pl.semaphore_wait(bar, peers)
-
-        def one(t, carry):
-            line.step(t)
-            return carry
-
-        lax.fori_loop(0, line.steps, one, 0)
-        line.drain()
-        line.store(out_ref)
-
-    out = jax.ShapeDtypeStruct((rows, width), bf16)
-    (summed,) = comm_call(body, [partial.astype(bf16)], [out], line.scratch(), cid, "tp_sum")
-    return summed
-
-
-def sum_and_scatter(partial, ats, bs, jobs, out_widths, cid, gains=None):
-    rows, width = partial.shape
-    n_ctx, n_seq = lax.axis_size("ctx"), lax.axis_size("seq")
-    line = LineSum(lax.axis_size("tp"), rows, width)
-    grads = GradScatter(n_ctx, n_seq, width, jobs)
-    small = GainSum(n_ctx, n_seq)
-    small_in = [] if gains is None else [gains]
-    na, nb, no, ns = len(ats), len(bs), len(out_widths), len(small_in)
-    n_line, n_grads = len(line.scratch()), len(grads.scratch())
-
-    def body(x_ref, *refs):
-        at_refs, b_refs = refs[:na], refs[na : na + nb]
-        refs = refs[na + nb :]
-        small_refs, refs = refs[:ns], refs[ns:]
-        out_ref, grad_refs, refs = refs[0], refs[1 : 1 + no], refs[1 + no :]
-        small_out, scratch = refs[:ns], refs[ns:]
-        line.bind(scratch[:n_line])
-        grads.bind(scratch[n_line : n_line + n_grads], at_refs, b_refs, grad_refs)
-        bar = pltpu.get_barrier_semaphore()
-        peers = line.greet(bar)
-        if ns:
-            small.bind(scratch[n_line + n_grads :], small_refs[0], small_out[0])
-            peers = peers + small.greet(bar)
-        else:
-            peers = peers + grads.greet(bar)
-        line.load(x_ref)
-        pl.semaphore_wait(bar, peers)
-        if ns:
-            small.start()
-
-        def one(it, carry):
-            grads.early(it)
-            for v in range(pace):
-                line.piece(it * pace + v)
-            grads.late(it)
-            return carry
-
-        lax.fori_loop(0, max(-(-line.steps * row_chains // pace), grads.steps), one, 0)
-        if ns:
-            small.finish()
-        line.drain()
-        grads.drain()
-        line.store(out_ref)
-
-    outs = [jax.ShapeDtypeStruct((rows, width), bf16)] + [
-        jax.ShapeDtypeStruct((grads.rows, w), f32) for w in out_widths
-    ]
-    outs += [jax.ShapeDtypeStruct((8, lanes), f32)] * ns
-    res = comm_call(
-        body, [partial.astype(bf16)] + list(ats) + list(bs) + small_in, outs,
-        line.scratch() + grads.scratch() + (small.scratch() if ns else []), cid, "sum_and_scatter",
-    )
-    return res[0], res[1:]
 
 
 class LineSmall:
@@ -838,8 +787,8 @@
 
     def body(
         tok_hbm, wq_hbm, wk_hbm, wv_hbm, wo_hbm, qg_ref, kg_ref, cos_ref, sin_ref, order_ref,
-        qrot_out, key_out, value_out, qn_out, kn_out, attn_out, sc_out, lse_out, proj_out,
-        tok, w3, wo, qn, kn, qrot, keys, values, peak, total, acc, attn, loads, stores,
+        qrot_out, key_out, value_out, qn_out, kn_out, attn_out, tokt_out, proj_out, sc_out, lse_out,
+        tok, tokt, w3, wo, qn, kn, qrot, keys, values, peak, total, acc, attn, loads, stores,
         sx, dx, sm, dm, sf, df, *rest,
     ):
         small.bind(rest[:n_small])
@@ -980,6 +929,7 @@
         from_mate(1).wait_recv()
         from_mate(0).wait_recv()
         attend(mx, 1 - core)
+        tokt[...] = jnp.transpose(tok[...])
         for d in range(1, nx):
             from_peer(0, d).wait_recv()
             pass_on(0, d).start()
@@ -1000,7 +950,7 @@
             pltpu.make_async_copy(src, dst, stores.at[i])
             for i, (src, dst) in enumerate(
                 [(qrot, qrot_out), (keys, key_out), (values, value_out), (qn, qn_out),
-                 (kn, kn_out), (attn, attn_out)]
+                 (kn, kn_out), (attn, attn_out), (tokt, tokt_out)]
             )
         ]
         for copy in outs:
@@ -1016,8 +966,8 @@
             return carry
 
         lax.fori_loop(0, line.steps, one, 0)
+        line.ship(proj_out, stores, 7)
         line.drain()
-        line.store(proj_out)
         for copy in outs:
             copy.wait()
         for b in range(2):
@@ -1034,18 +984,20 @@
         out_shape=[
             block((rows, local), bf16), block((count, local), bf16), block((count, local), bf16),
             block((rows, local), f32), block((rows, local), f32), block((rows, local), bf16),
-            block((rows, lanes), f32), block((8, rows), f32), block((rows, width), bf16),
+            block((width, rows), bf16), block((rows, width), bf16),
+            block((rows, lanes), f32), block((8, rows), f32),
         ],
         in_specs=[hbm] * 5 + [vmem_spec()] * 4 + [pl.BlockSpec(memory_space=pltpu.SMEM)],
-        out_specs=[hbm] * 6 + [vmem_spec()] * 3,
+        out_specs=[hbm] * 8 + [vmem_spec()] * 2,
         scratch_shapes=[
-            pltpu.VMEM((rows, width), bf16), pltpu.VMEM((3, width, local), bf16),
+            pltpu.VMEM((rows, width), bf16), pltpu.VMEM((width, rows), bf16),
+            pltpu.VMEM((3, width, local), bf16),
             pltpu.VMEM((local, width), bf16), pltpu.VMEM((rows, local), f32),
             pltpu.VMEM((rows, local), f32), pltpu.VMEM((rows, local), bf16),
             pltpu.VMEM((count, local), bf16), pltpu.VMEM((count, local), bf16),
             pltpu.VMEM((heads, rows, 1), f32), pltpu.VMEM((heads, rows, 1), f32),
             pltpu.VMEM((rows, local), f32), pltpu.VMEM((rows, local), bf16),
-            sem((5,)), sem((6,)),
+            sem((5,)), sem((7 + n_tp,)),
             sem((2, nx - 1)), sem((2, nx - 1)), sem((2,)), sem((2,)),
             sem((2, nx - 1)), sem((2, nx - 1)),
         ] + small.scratch() + line.scratch(),
@@ -1056,27 +1008,327 @@
     )(tokens, w_query, w_key, w_value, w_output, qgain, kgain, cosine, sine, order)
 
 
-norm_eps = 1e-06
-rope_base = 500000.0
-masked_score = -1e30
-
-
-def matmul(left, right):
-    return jnp.dot(left, right, preferred_element_type=jnp.float32)
-
-
-def rope_tables(positions, head_dim):
-    half = head_dim // 2
-    rates = rope_base ** (-(jnp.arange(half, dtype=jnp.float32) * 2.0 / head_dim))
-    angle = positions.astype(jnp.float32)[:, None] * rates[None, :]
-    return (jnp.cos(angle), jnp.sin(angle))
-
-
-def key_positions(order, first_row, count, group):
-    row_ids = first_row + jnp.arange(count, dtype=jnp.int32)
-    slots = row_ids // group
-    picks = slots[:, None] == jnp.arange(order.shape[0], dtype=jnp.int32)[None, :]
-    return jnp.sum(jnp.where(picks, order[None, :], 0), axis=1) * group + row_ids % group
+def load_list(pairs, sems):
+    copies = [pltpu.make_async_copy(src, dst, sems.at[i]) for i, (src, dst) in enumerate(pairs)]
+    for copy in copies:
+        copy.start()
+    return copies
+
+
+def kernel_call(body, args, kinds, outs, out_kinds, scratch, cid, name):
+    spec = {
+        "v": vmem_spec(),
+        "h": pl.BlockSpec(memory_space=pl.ANY),
+        "s": pl.BlockSpec(memory_space=pltpu.SMEM),
+    }
+    return pl.pallas_call(
+        body,
+        out_shape=[jax.ShapeDtypeStruct(*out) for out in outs],
+        in_specs=[spec[kind] for kind in kinds],
+        out_specs=[spec[kind] for kind in out_kinds],
+        scratch_shapes=scratch,
+        compiler_params=pltpu.CompilerParams(
+            collective_id=cid, has_side_effects=True, vmem_limit_bytes=62 * 2**20
+        ),
+        name=name,
+    )(*args)
+
+
+def mlp_forward(tokens, proj, attn_gain, w_gate, w_up, w_down, cid):
+    rows, width = tokens.shape
+    wide = w_gate.shape[1]
+    n_tp = lax.axis_size("tp")
+    line = LineSum(n_tp, rows, width)
+    n_line = len(line.scratch())
+    tile = 64
+    cut = 512
+    n_cut = wide // cut
+
+    def body(
+        tok_hbm, proj_hbm, again_ref, wg_hbm, wu_hbm, wd_hbm,
+        hidt_out, gate_out, up_out, inner_out, down_out,
+        tok, proj_v, hid, hidt, gate, up, inner, wg, wu, wd, first, loads, stores, *rest,
+    ):
+        line.bind(rest[:n_line])
+        start = load_list([(proj_hbm, proj_v), (tok_hbm, tok)], first)
+        pairs = []
+        for j in range(n_cut):
+            cols = pl.ds(j * cut, cut)
+            pairs += [(wg_hbm.at[:, cols], wg.at[j]), (wu_hbm.at[:, cols], wu.at[j])]
+        for j in range(n_tp):
+            cols = pl.ds(j * line.part, line.part)
+            pairs += [(wd_hbm.at[:, cols], wd.at[j])]
+        weights = load_list(pairs, loads)
+        bar = pltpu.get_barrier_semaphore()
+        peers = line.greet(bar)
+        for copy in start:
+            copy.wait()
+
+        def norm_rows(t, carry):
+            sl = pl.ds(pl.multiple_of(t * tile, tile), tile)
+            out = proj_v[sl].astype(f32)
+            inv = lax.rsqrt(jnp.mean(out * out, axis=1, keepdims=True) + norm_eps)
+            hid[sl] = (tok[sl].astype(f32) + out * inv * again_ref[...]).astype(bf16)
+            return carry
+
+        lax.fori_loop(0, rows // tile, norm_rows, 0)
+        for j in range(n_cut):
+            cols = slice(j * cut, (j + 1) * cut)
+            weights[2 * j].wait()
+            weights[2 * j + 1].wait()
+            for r in range(2):
+                sl = slice(r * rows // 2, (r + 1) * rows // 2)
+                g = jnp.dot(hid[sl], wg[j], preferred_element_type=f32)
+                u = jnp.dot(hid[sl], wu[j], preferred_element_type=f32)
+                gate[sl, cols] = g.astype(bf16)
+                up[sl, cols] = u.astype(bf16)
+                inner[sl, cols] = (g * jax.nn.sigmoid(g) * u).astype(bf16)
+        outs = load_list([(gate, gate_out), (up, up_out), (inner, inner_out)], stores)
+        for j in range(n_tp):
+            weights[2 * n_cut + j].wait()
+            line.own[j] = jnp.dot(inner[...], wd[j], preferred_element_type=f32).astype(bf16)
+        pl.semaphore_wait(bar, peers)
+
+        def one(t, carry):
+            line.step(t)
+
+            @pl.when(t == 2)
+            def _():
+                hidt[...] = jnp.transpose(hid[...])
+
+            return carry
+
+        lax.fori_loop(0, line.steps, one, 0)
+        last = pltpu.make_async_copy(hidt, hidt_out, stores.at[3])
+        last.start()
+        line.ship(down_out, stores, 4)
+        line.drain()
+        for copy in outs + [last]:
+            copy.wait()
+
+    sem = pltpu.SemaphoreType.DMA
+    return kernel_call(
+        body, [tokens, proj, attn_gain, w_gate, w_up, w_down], "hhvhhh",
+        [((width, rows), bf16), ((rows, wide), bf16), ((rows, wide), bf16), ((rows, wide), bf16),
+         ((rows, width), bf16)],
+        "hhhhh",
+        [
+            pltpu.VMEM((rows, width), bf16), pltpu.VMEM((rows, width), bf16),
+            pltpu.VMEM((rows, width), bf16), pltpu.VMEM((width, rows), bf16),
+            pltpu.VMEM((rows, wide), bf16), pltpu.VMEM((rows, wide), bf16),
+            pltpu.VMEM((rows, wide), bf16),
+            pltpu.VMEM((n_cut, width, cut), bf16), pltpu.VMEM((n_cut, width, cut), bf16),
+            pltpu.VMEM((n_tp, wide, line.part), bf16),
+            sem((2,)), sem((2 * n_cut + n_tp,)), sem((4 + n_tp,)),
+        ] + line.scratch(),
+        cid, "mlp_forward",
+    )
+
+
+def mlp_back(down, grad, mlp_gain, gate, up, inner, hid_t, w_gate, w_up, w_down, jobs, widths, cid):
+    rows, width = down.shape
+    wide = gate.shape[1]
+    n_tp = lax.axis_size("tp")
+    line = LineSum(n_tp, rows, width)
+    grads = GradScatter(lax.axis_size("ctx"), lax.axis_size("seq"), width, jobs)
+    n_line, n_grads, n_out = len(line.scratch()), len(grads.scratch()), len(widths)
+    tile = 64
+    cut = 512
+    n_cut = wide // cut
+    part = line.part
+
+    def body(
+        down_ref, grad_ref, mgain_ref, gate_hbm, up_hbm, inner_hbm, hidt_hbm, wg_hbm, wu_hbm, wd_hbm,
+        back_out, dgate_out, dup_out, dgain_out, *rest,
+    ):
+        grad_outs, rest = rest[:n_out], rest[n_out:]
+        (gate_v, up_v, inner_v, hidt, ddown, ddownt, dgate, dup, ring, loads, wsem, stores) = rest[:12]
+        line.bind(rest[12 : 12 + n_line])
+        grads.bind(rest[12 + n_line :], [ddownt, hidt], [inner_v, dgate, dup], grad_outs)
+
+        def fetch(src, index):
+            return pltpu.make_async_copy(src, ring.at[index], wsem.at[index])
+
+        def rows_of(ref, j, size):
+            return ref.at[pl.ds(pl.multiple_of(j * size, size), size)]
+
+        for j in range(4):
+            fetch(rows_of(wd_hbm, j, cut), j).start()
+        early = load_list(
+            [(inner_hbm, inner_v), (gate_hbm, gate_v), (up_hbm, up_v), (hidt_hbm, hidt)], loads
+        )
+        bar = pltpu.get_barrier_semaphore()
+        peers = line.greet(bar) + grads.greet(bar)
+        dgain_out[...] = jnp.zeros_like(dgain_out)
+
+        def norm_rows(t, carry):
+            sl = pl.ds(pl.multiple_of(t * tile, tile), tile)
+            out = down_ref[sl].astype(f32)
+            upstream = grad_ref[sl].astype(f32)
+            inv = lax.rsqrt(jnp.mean(out * out, axis=1, keepdims=True) + norm_eps)
+            norm = out * inv
+            dgain_out[...] += jnp.sum(upstream * norm, axis=0, keepdims=True)
+            dnorm = upstream * mgain_ref[...]
+            dot = jnp.mean(dnorm * norm, axis=1, keepdims=True)
+            ddown[sl] = (inv * (dnorm - norm * dot)).astype(bf16)
+            return carry
+
+        lax.fori_loop(0, rows // tile, norm_rows, 0)
+        ddownt[...] = jnp.transpose(ddown[...])
+        for copy in early:
+            copy.wait()
+        pl.semaphore_wait(bar, peers)
+
+        def inner_back(j, carry):
+            fetch(rows_of(wd_hbm, j, cut), j).wait()
+            cols = pl.ds(pl.multiple_of(j * cut, cut), cut)
+            for r in range(2):
+                sl = slice(r * rows // 2, (r + 1) * rows // 2)
+                dmix = dot_nt(ddown[sl], ring[j])
+                g, u = gate_v[sl, cols].astype(f32), up_v[sl, cols].astype(f32)
+                sig = jax.nn.sigmoid(g)
+                dgate[sl, cols] = (dmix * u * sig * (1.0 + g * (1.0 - sig))).astype(bf16)
+                dup[sl, cols] = (dmix * (g * sig)).astype(bf16)
+
+            @pl.when(lax.rem(j, 2) == 0)
+            def _():
+                fetch(rows_of(wg_hbm, j // 2, part), j).start()
+
+            @pl.when(lax.rem(j, 2) == 1)
+            def _():
+                fetch(rows_of(wu_hbm, j // 2, part), j).start()
+                grads.early(j // 2)
+                grads.late(j // 2)
+
+            return carry
+
+        lax.fori_loop(0, n_cut, inner_back, 0)
+        outs = load_list([(dgate, dgate_out), (dup, dup_out)], stores)
+
+        def hidden_back(j, carry):
+            slot = lax.rem(2 * j, 4)
+            fetch(rows_of(wg_hbm, j, part), slot).wait()
+            fetch(rows_of(wu_hbm, j, part), slot + 1).wait()
+            for r in range(2):
+                sl = slice(r * rows // 2, (r + 1) * rows // 2)
+                line.own[j, sl] = (
+                    dot_nt(dgate[sl], ring[slot]) + dot_nt(dup[sl], ring[slot + 1])
+                ).astype(bf16)
+
+            @pl.when(j + 2 < n_tp)
+            def _():
+                fetch(rows_of(wg_hbm, j + 2, part), slot).start()
+                fetch(rows_of(wu_hbm, j + 2, part), slot + 1).start()
+
+            @pl.when(lax.rem(j, 2) == 1)
+            def _():
+                grads.early(n_cut // 2 + j // 2)
+                grads.late(n_cut // 2 + j // 2)
+
+            return carry
+
+        lax.fori_loop(0, n_tp, hidden_back, 0)
+        done = n_cut // 2 + n_tp // 2
+
+        def one(it, carry):
+            grads.early(it)
+            for v in range(pace):
+                line.piece((it - done) * pace + v)
+            grads.late(it)
+            return carry
+
+        line_steps = -(-line.steps * row_chains // pace)
+        lax.fori_loop(done, max(done + line_steps, grads.steps), one, 0)
+        line.ship(back_out, stores, 2)
+        line.drain()
+        grads.drain()
+        for copy in outs:
+            copy.wait()
+
+    sem = pltpu.SemaphoreType.DMA
+    return kernel_call(
+        body, [down, grad, mlp_gain, gate, up, inner, hid_t, w_gate, w_up, w_down], "vvvhhhhhhh",
+        [((rows, width), bf16), ((rows, wide), bf16), ((rows, wide), bf16), ((1, width), f32)]
+        + [((grads.rows, w), f32) for w in widths],
+        "hhhv" + "v" * n_out,
+        [
+            pltpu.VMEM((rows, wide), bf16), pltpu.VMEM((rows, wide), bf16),
+            pltpu.VMEM((rows, wide), bf16), pltpu.VMEM((width, rows), bf16),
+            pltpu.VMEM((rows, width), bf16), pltpu.VMEM((width, rows), bf16),
+            pltpu.VMEM((rows, wide), bf16), pltpu.VMEM((rows, wide), bf16),
+            pltpu.VMEM((4, cut, width), bf16),
+            sem((4,)), sem((4,)), sem((2 + n_tp,)),
+        ] + line.scratch() + grads.scratch(),
+        cid, "mlp_back",
+    )
+
+
+def last_sums(dqkv, w_query, w_key, w_value, ats, bs, jobs, widths, gains, cid):
+    rows = dqkv.shape[0]
+    width, local = w_query.shape
+    n_ctx, n_seq = lax.axis_size("ctx"), lax.axis_size("seq")
+    n_tp = lax.axis_size("tp")
+    line = LineSum(n_tp, rows, width)
+    grads = GradScatter(n_ctx, n_seq, width, jobs)
+    small = GainSum(n_ctx, n_seq)
+    na, nb, n_out = len(ats), len(bs), len(widths)
+    n_line, n_grads = len(line.scratch()), len(grads.scratch())
+    part = line.part
+
+    def body(dqkv_ref, wq_ref, wk_ref, wv_ref, *refs):
+        at_refs, b_refs = refs[:na], refs[na : na + nb]
+        gain_ref, last_out = refs[na + nb], refs[na + nb + 1]
+        refs = refs[na + nb + 2 :]
+        grad_outs, gain_out, stores, scratch = refs[:n_out], refs[n_out], refs[n_out + 1], refs[n_out + 2 :]
+        line.bind(scratch[:n_line])
+        grads.bind(scratch[n_line : n_line + n_grads], at_refs, list(b_refs) + [dqkv_ref], grad_outs)
+        small.bind(scratch[n_line + n_grads :], gain_ref, gain_out)
+        bar = pltpu.get_barrier_semaphore()
+        peers = line.greet(bar) + small.greet(bar)
+        pl.semaphore_wait(bar, peers)
+        small.start()
+
+        def input_back(j, carry):
+            rs = pl.ds(pl.multiple_of(j * part, part), part)
+            line.own[j] = (
+                dot_nt(dqkv_ref[:, :local], wq_ref[rs])
+                + dot_nt(dqkv_ref[:, local : 2 * local], wk_ref[rs])
+                + dot_nt(dqkv_ref[:, 2 * local :], wv_ref[rs])
+            ).astype(bf16)
+
+            @pl.when(lax.rem(j, 2) == 0)
+            def _():
+                grads.early(j // 2)
+                grads.late(j // 2)
+
+            return carry
+
+        lax.fori_loop(0, n_tp, input_back, 0)
+        done = n_tp // 2
+
+        def one(it, carry):
+            grads.early(it)
+            for v in range(pace):
+                line.piece((it - done) * pace + v)
+            grads.late(it)
+            return carry
+
+        line_steps = -(-line.steps * row_chains // pace)
+        lax.fori_loop(done, max(done + line_steps, grads.steps), one, 0)
+        small.finish()
+        line.ship(last_out, stores, 0)
+        line.drain()
+        grads.drain()
+
+    sem = pltpu.SemaphoreType.DMA
+    return kernel_call(
+        body, [dqkv, w_query, w_key, w_value] + list(ats) + list(bs) + [gains],
+        "vvvv" + "v" * (na + nb + 1),
+        [((rows, width), bf16)] + [((grads.rows, w), f32) for w in widths] + [((8, lanes), f32)],
+        "h" + "v" * (n_out + 1),
+        [sem((n_tp,))] + line.scratch() + grads.scratch() + small.scratch(),
+        cid, "last_sums",
+    )
 
 
 def per_device(
@@ -1095,71 +1347,40 @@
     w_down,
     mlp_gain,
 ):
-    inputs_bf = tokens[0]
-    order = group_order[0]
-    row_count, width = inputs_bf.shape
+    inputs = tokens[0]
+    upstream = out_grad[0]
+    rows, width = inputs.shape
     heads, head_dim = query_gain.shape
     local = heads * head_dim
-    group = row_count // 2
-    query_pos = key_positions(order, lax.axis_index("ctx") * row_count, row_count, group)
-    cosine, sine = rope_tables(query_pos, head_dim)
-    inputs = inputs_bf.astype(jnp.float32)
-    qgain = query_gain.reshape(local)
-    kgain = key_gain.reshape(local)
+    wide = w_gate.shape[1]
+    positions = key_positions(group_order[0], lax.axis_index("ctx") * rows, rows, rows // 2)
+    cosine, sine = rope_tables(positions, head_dim)
     angle_cos = jnp.concatenate([cosine, cosine], axis=1)
     angle_sin = jnp.concatenate([-sine, sine], axis=1)
-    (query_rot, whole_keys, whole_values, query_norm, key_norm, attn_flat, scales, lse,
-     proj_sum) = front(
-        inputs_bf, w_query, w_key, w_value, w_output, qgain[None], kgain[None], angle_cos,
-        angle_sin, group_order, 1,
+    qgain = query_gain.reshape(1, local)
+    kgain = key_gain.reshape(1, local)
+    (query_rot, keys, values, query_norm, key_norm, attn, tokens_t, proj, scales, lse) = front(
+        inputs, w_query, w_key, w_value, w_output, qgain, kgain, angle_cos, angle_sin, group_order, 1
     )
-    proj = proj_sum.astype(f32)
-    attn_scale = lax.rsqrt(jnp.mean(proj * proj, axis=1) + norm_eps)
-    attn_norm = proj * attn_scale[:, None]
-    resid = inputs + attn_norm * attn_gain
-    hidden = resid.astype(jnp.bfloat16)
-    gate = matmul(hidden, w_gate)
-    up = matmul(hidden, w_up)
-    sigma = jax.nn.sigmoid(gate)
-    active = gate * sigma
-    inner = (active * up).astype(jnp.bfloat16)
-    down = tp_sum(matmul(inner, w_down), 2).astype(f32)
-    mlp_scale = lax.rsqrt(jnp.mean(down * down, axis=1) + norm_eps)
-    mlp_norm = down * mlp_scale[:, None]
-    block_out = resid + mlp_norm * mlp_gain
-    upstream = out_grad[0].astype(jnp.float32)
-    d_mlp_gain = jnp.sum(upstream * mlp_norm, axis=0)
-    d_mnorm = upstream * mlp_gain
-    d_down = (
-        mlp_scale[:, None]
-        * (d_mnorm - mlp_norm * jnp.mean(d_mnorm * mlp_norm, axis=1, keepdims=True))
-    ).astype(jnp.bfloat16)
-    d_inner = matmul(d_down, w_down.T)
-    d_gate = (d_inner * up * sigma * (1.0 + gate * (1.0 - sigma))).astype(jnp.bfloat16)
-    d_up = (d_inner * active).astype(jnp.bfloat16)
-    hidden_t = hidden.T
-    wide = inner.shape[1] // (2 * lanes)
-    half = wide // 2
-    back, (grad_down, grad_gate_a) = sum_and_scatter(
-        matmul(d_gate, w_gate.T) + matmul(d_up, w_up.T),
-        [d_down.T, hidden_t],
-        [inner, d_gate],
+    hidden_t, gate, up, inner, down = mlp_forward(
+        inputs, proj, attn_gain[None], w_gate, w_up, w_down, 2
+    )
+    chunks = wide // (2 * lanes)
+    chunk_cols = 2 * lanes
+    back, d_gate, d_up, d_mlp_gain, grad_down, grad_gate = mlp_back(
+        down, upstream, mlp_gain[None], gate, up, inner, hidden_t, w_gate, w_up, w_down,
         [
-            dict(a=0, b=0, first=0, count=wide, out=0, place=0),
-            dict(a=1, b=1, first=0, count=half, out=1, place=0),
+            dict(a=0, b=0, first=0, count=chunks, out=0, place=0),
+            dict(a=1, b=1, first=0, count=chunks, out=1, place=0),
         ],
-        [inner.shape[1], half * 2 * lanes],
+        [wide, wide],
         3,
     )
     d_qkv, d_proj_t, d_attn_gain, d_query_gain, d_key_gain = attention_back(
-        back, out_grad[0], proj_sum, attn_gain[None], w_output, query_rot,
-        whole_keys, whole_values, attn_flat, lse, query_pos[None], group_order,
-        query_norm, key_norm, scales, qgain[None], kgain[None], angle_cos, angle_sin, 5,
+        back, upstream, proj, attn_gain[None], w_output, query_rot, keys, values, attn, lse,
+        positions[None], group_order, query_norm, key_norm, scales, qgain, kgain, angle_cos,
+        angle_sin, 4,
     )
-    d_query_gain = d_query_gain.reshape(heads, head_dim)
-    d_key_gain = d_key_gain.reshape(heads, head_dim)
-    d_query, d_key, d_value = (d_qkv[:, i * local : (i + 1) * local] for i in range(3))
-    thin = local // (2 * lanes)
     owners = lax.axis_size("ctx") * lax.axis_size("seq")
     pieces = [
         d_attn_gain.reshape(owners, -1),
@@ -1170,28 +1391,33 @@
     cuts = [piece.shape[1] for piece in pieces]
     packed = jnp.concatenate(pieces, axis=1)
     packed = jnp.pad(packed, ((0, 0), (0, 8 * lanes - packed.shape[1]))).reshape(owners, 8, lanes)
-    last, (grad_gate_b, grad_up, grad_qkv, grad_output, small) = sum_and_scatter(
-        matmul(d_query, w_query.T) + matmul(d_key, w_key.T) + matmul(d_value, w_value.T),
-        [hidden_t, inputs_bf.T, d_proj_t],
-        [d_gate, d_up, d_qkv, attn_flat],
+    thin = local // chunk_cols
+    last, grad_up, grad_qkv, grad_output, small = last_sums(
+        d_qkv, w_query, w_key, w_value,
+        [hidden_t, tokens_t, d_proj_t],
+        [d_up, attn],
         [
-            dict(a=0, b=0, first=half, count=wide - half, out=0, place=0),
-            dict(a=0, b=1, first=0, count=wide, out=1, place=0),
-            dict(a=2, b=3, first=0, count=thin, out=3, place=0),
-            dict(a=1, b=2, first=0, count=3 * thin, out=2, place=0),
+            dict(a=0, b=0, first=0, count=chunks, out=0, place=0),
+            dict(a=2, b=1, first=0, count=thin, out=2, place=0),
+            dict(a=1, b=2, first=0, count=3 * thin, out=1, place=0),
         ],
-        [(wide - half) * 2 * lanes, inner.shape[1], 3 * local, local],
-        4,
+        [wide, 3 * local, local],
         packed,
+        5,
     )
     small = small.reshape(-1)
     g_attn, g_mlp, g_query, g_key = jnp.split(
         small[: sum(cuts)], [cuts[0], cuts[0] + cuts[1], cuts[0] + cuts[1] + cuts[2]]
     )
-    input_grad = upstream + back.astype(f32) + last.astype(f32)
     grad_query, grad_key, grad_value = jnp.split(grad_qkv, 3, axis=1)
-    grad_gate = jnp.concatenate([grad_gate_a, grad_gate_b], axis=1)
-    summed = (
+    proj, down = proj.astype(f32), down.astype(f32)
+    attn_norm = proj * lax.rsqrt(jnp.mean(proj * proj, axis=1) + norm_eps)[:, None]
+    mlp_norm = down * lax.rsqrt(jnp.mean(down * down, axis=1) + norm_eps)[:, None]
+    block_out = inputs.astype(f32) + attn_norm * attn_gain + mlp_norm * mlp_gain
+    input_grad = upstream.astype(f32) + back.astype(f32) + last.astype(f32)
+    return (
+        block_out[None],
+        input_grad[None],
         grad_query,
         grad_key,
         grad_value,
@@ -1203,21 +1429,6 @@
         grad_up,
         grad_down.T,
         g_mlp,
-    )
-    return (
-        block_out[None],
-        input_grad[None],
-        summed[0],
-        summed[1],
-        summed[2],
-        summed[3],
-        summed[4],
-        summed[5],
-        summed[6],
-        summed[7],
-        summed[8],
-        summed[9],
-        summed[10],
     )
 
 

time: 530 us -> 462 us (0.87)
  matrix products: 58.4 us -> 0 us
  Pallas kernels: 386 us -> 425 us
  local copies, waits for them, and re-layouts: 45.9 us -> 12.9 us
  other arithmetic: 28.5 us -> 18.7 us
    pallas_call x0 -> x3, Pallas kernels: none -> 274 us  [kernel_call(): pl.pallas_call(body, out_shape=[jax.ShapeDtypeStruct(*out) for out in out...]
    pallas_call x4 -> x1, Pallas kernels: 285 us -> 48.2 us  [comm_call(): pl.pallas_call(body, out_shape=outs, in_specs=[pl.BlockSpec(memory_space=...]
    dot_general x9 -> x0, matrix products: 58.4 us -> none  [matmul(): return jnp.dot(left, right, preferred_element_type=jnp.float32)]
    unnamed x60 -> x27, local copies, waits for them, and re-layouts: 26.3 us -> 9.65 us
    pallas_call x4 -> x1, local copies, waits for them, and re-layouts: 12.8 us -> 0.51 us  [comm_call(): pl.pallas_call(body, out_shape=outs, in_specs=[pl.BlockSpec(memory_space=...]
    reduce_sum x3 -> x2, other arithmetic: 7.21 us -> 0.97 us  [the longest x1 0.48 us: per_device(): jnp.mean(down * down, axis=1) + norm_eps]
    transpose x1 -> x0, other arithmetic: 5.3 us -> none  [per_device(): back, (grad_down, grad_gate_a) = sum_and_scatter(matmul(d_gate, w_gate.T)...]
where the time goes in v5:
time: 462 us; the launch traced here: 457 us
  Pallas kernels  425 us (92%)
  other arithmetic  18.7 us (4%)
  local copies, waits for them, and re-layouts  12.9 us (3%)
    pallas_call x3, Pallas kernels, kernel_call(): pl.pallas_call(body, out_shape=[jax.ShapeDtypeStruct(*out) for out in out...  274 us
    pallas_call x1, Pallas kernels, front(): pl.pallas_call(body, out_shape=[block((rows, local), bf16), block((count,...  102 us
    pallas_call x1, Pallas kernels, comm_call(): pl.pallas_call(body, out_shape=outs, in_specs=[pl.BlockSpec(memory_space=...  48.2 us
    unnamed x27, local copies, waits for them, and re-layouts  9.65 us

profile of v5, /device:TPU:0, one launch (start us, length us, event | category | flops | bytes accessed | tf_op | source)
XLA Modules:
  0.0 457.3 jit_solution(4523215793522615023)
XLA Ops:
  0.7 0.7 select_reduce_fusion
  1.4 1.0 fusion.7
  2.4 1.0 pad_maximum_fusion
  3.4 102.1 %front.1 = (bf16[512,512]{1,0:T(8,128)(2,1)}, bf16[2048,512]{1,0:T(8,128)(2,1)}, bf16[2048,512]{1,0:T(8,128)(2,1)}, f32[512,512]{1,0:T(8,128)}, f32[512,512]{1,0...) custom-call(bf16[512,2048]{1,0:T(8,128)(2,1)} %bitcast.30, ...), custom_call_target="tpu_custom_call" | custom-call | tf_op jit(solution)/shard_map/front/pallas_call | solution.py:982
  105.5 84.0 %mlp_forward.1 = (bf16[2048,512]{1,0:T(8,128)(2,1)}, bf16[512,2048]{1,0:T(8,128)(2,1)}, bf16[512,2048]{1,0:T(8,128)(2,1)}, bf16[512,2048]{1,0:T(8,128)(2,1)}, bf16[512,2048]{1,0:T(8,128)(2,1)}) custom-call(bf16[512,2048]{1,0:T(8,128)(2,1)} %bitcast.31, bf16[512,2048]{1,0:T(8,128)(2,1)} %get-tuple-element.43.proj_hbm.proj_ref, f32[1,2048]{1,0:T(1,128)} %bitcast.35, ...), custom_call_target="tpu_custom_call" | custom-call | tf_op jit(solution)/shard_map/mlp_forward/pallas_call | solution.py:1024
  189.6 100.5 %mlp_back.1 = (bf16[512,2048]{1,0:T(8,128)(2,1)}, bf16[512,2048]{1,0:T(8,128)(2,1)}, bf16[512,2048]{1,0:T(8,128)(2,1)}, f32[1,2048]{1,0:T(1,128)}, f32[256,2048]{1,0:T(8,128)}, /*index=5*/f32[256,2048]{1,0:T(8,128)}) custom-call(bf16[512,2048]{1,0:T(8,128)(2,1)} %get-tuple-element.44.down_ref, bf16[512,2048]{1,0:T(8,128)(2,1)} %bitcast.28, ...), custom_call_target="tpu_custom_call" | custom-call | tf_op jit(solution)/shard_map/mlp_back/pallas_call | solution.py:1024
  290.1 0.6 fusion.9.prow_ref
  290.7 48.2 %attention_back.1 = (bf16[512,1536]{1,0:T(8,128)(2,1)}, bf16[2048,512]{1,0:T(8,128)(2,1)}, f32[1,2048]{1,0:T(1,128)}, f32[1,512]{1,0:T(1,128)}, f32[1,512]{1,0:T(1,128)}) custom-call(bf16[512,2048]{1,0:T(8,128)(2,1)} %get-tuple-element.49.back_ref, bf16[512,2048]{1,0:T(8,128)(2,1)} %bitcast.29, bf16[512,2048]{1,0:T(8,128)(2,1)} %get-tuple-element.43.proj_hbm.proj_ref, ...), custom_call_target="tpu_custom_call" | custom-call | tf_op jit(solution)/shard_map/attention_back/pallas_call | solution.py:495
  339.4 1.3 reduce.13
  340.9 1.3 reduce.12
  342.4 1.4 reduce.15
  343.8 0.7 reduce.14
  344.6 0.6 copy.41
  345.2 89.9 %last_sums.1 = (bf16[512,2048]{1,0:T(8,128)(2,1)}, f32[256,2048]{1,0:T(8,128)}, f32[256,1536]{1,0:T(8,128)}, f32[256,512]{1,0:T(8,128)}, f32[8,128]{1,0:T(8,128)}) custom-call(bf16[512,1536]{1,0:T(8,128)(2,1)} %get-tuple-element.58.dqkv_ref, bf16[2048,512]{1,0:T(8,128)(2,1)} %wq_ref.1, bf16[2048,512]{1,0:T(8,128)(2,1)} %wk_ref.1, bf16[2048,512]{1,0:T(8,128)(2,1)} %wv_ref.1, ...), custom_call_target="tpu_custom_call" | custom-call | tf_op jit(solution)/shard_map/last_sums/pallas_call | solution.py:1024
  435.1 6.2 %add_bitcast_fusion = f32[1,512,2048]{2,1,0:T(8,128)} fusion(bf16[512,2048]{1,0:T(8,128)(2,1)} %get-tuple-element.66, bf16[512,2048]{1,0:T(8,128)(2,1)} %get-tuple-element.49.back_ref, bf16[1,512,2048]{2,1,0:T(8,128)(2,1)} %param.15), kind=kLoop, calls=%fused_computation.11 | loop fusion | flops 5242880 | bytes 10485760 | tf_op jit(solution)/shard_map/broadcast_in_dim | solution.py:1420
  441.3 1.2 fusion.16
  442.6 1.0 copy.37
  443.7 0.6 fusion.17
  444.8 3.0 copy.38
  448.4 1.1 copy-done
  450.1 3.4 fusion.4
  453.5 1.3 copy.44
  454.8 1.0 copy-done.4
  455.8 1.3 copy.45
  (39 shorter events, 2.9 us)
Async XLA Ops:
  290.7 53.1 %copy-start.10 = (f32[1,2048]{1,0:T(1,128)S(1)}, f32[1,2048]{1,0:T(1,128)}, u32[]{:S(2)}) copy-start(f32[1,2048]{1,0:T(1,128)} %get-tuple-element.63) | copy-start | bytes 24580
  435.1 6.2 %copy-start.5 = (f32[256,1536]{1,0:T(8,128)S(1)}, f32[256,1536]{1,0:T(8,128)}, u32[]{:S(2)}) copy-start(f32[256,1536]{1,0:T(8,128)} %get-tuple-element.67) | copy-start | bytes 4718596
  441.3 1.3 copy-start.6
  441.3 2.3 copy-start.9
  444.8 3.0 copy-start.1
  444.8 5.1 %copy-start.8 = (f32[2048]{0:T(1024)S(1)}, f32[2048]{0:T(1024)}, u32[]{:S(2)}) copy-start(f32[2048]{0:T(1024)} %param.27) | copy-start | bytes 24580
  447.9 1.6 copy-start
  447.9 2.2 copy-start.2
  447.9 2.2 copy-start.7
  450.1 3.4 copy-start.3
  453.5 2.3 copy-start.4

commit v6 on v5

--- a/solution.py
+++ b/solution.py
@@ -40,11 +40,11 @@
 
 
 class LineSum:
-    def __init__(self, n, rows, width):
+    def __init__(self, n, rows, width, blocks=row_blocks):
         self.n, self.rows, self.width = n, rows, width
         self.part = width // n
-        self.rc = rows // row_blocks
-        self.total = row_blocks // row_chains * n
+        self.rc = rows // blocks
+        self.total = blocks // row_chains * n
         self.steps = self.total + n - 1
 
     def scratch(self):
@@ -197,26 +197,24 @@
 
         lax.fori_loop(0, self.total, one, 0)
 
-    def ship(self, out_ref, sems, base):
-        copies = []
-        for j in range(self.n):
-            cols = pl.ds(j * self.part, self.part)
-            copy = pltpu.make_async_copy(self.res.at[j], out_ref.at[:, cols], sems.at[base + j])
-            copy.start()
-            copies.append(copy)
-        for copy in copies:
-            copy.wait()
-
-    def store(self, out_ref):
-        for j in range(self.n):
-            out_ref[:, j * self.part : (j + 1) * self.part] = self.res[j]
+    def ship(self, out_ref, sems, base, start, count):
+        return load_list(
+            [
+                (
+                    self.res.at[j, pl.ds(start, count)],
+                    out_ref.at[:, pl.ds(j * self.part, self.part)],
+                )
+                for j in range(self.n)
+            ],
+            sems, base,
+        )
 
 
 class GradScatter:
-    def __init__(self, n_ctx, n_seq, width, jobs):
+    def __init__(self, n_ctx, n_seq, width, jobs, orders=("xy", "yx")):
         self.nx, self.ny = n_ctx // 2, n_seq
         self.rows = width // (n_ctx * n_seq)
-        self.jobs = jobs
+        self.jobs, self.orders = jobs, orders
         start = 0
         self.spans = []
         for job in jobs:
@@ -225,78 +223,72 @@
         self.total = start
         self.steps = start + 5
 
+    def sizes(self, order):
+        return (self.nx, self.ny) if order == "xy" else (self.ny, self.nx)
+
     def scratch(self):
-        nx, ny, r, t = self.nx, self.ny, self.rows, self.total
-        tile = (r, lanes)
+        nx, ny, t = self.nx, self.ny, self.total
+        tile = (self.rows, lanes)
         sem = pltpu.SemaphoreType.DMA
-        return [
+        out = [
             pltpu.VMEM((2, nx, ny, 2) + tile, bf16),
             pltpu.VMEM((2, nx, ny, 2) + tile, f32),
             pltpu.VMEM((t, nx, ny, 2) + tile, bf16),
-            pltpu.VMEM((3, nx, ny) + tile, bf16),
-            pltpu.VMEM((3, ny, nx) + tile, bf16),
-            pltpu.VMEM((t, nx - 1, ny) + tile, bf16),
-            pltpu.VMEM((t, ny - 1, nx) + tile, bf16),
-            pltpu.VMEM((3, ny) + tile, bf16),
-            pltpu.VMEM((3, nx) + tile, bf16),
-            pltpu.VMEM((t, ny - 1) + tile, bf16),
-            pltpu.VMEM((t, nx - 1) + tile, bf16),
             sem((2,)), sem((t,)),
-            sem((3, nx - 1)), sem((t, nx - 1)), sem((3, ny - 1)), sem((t, ny - 1)),
-            sem((3, ny - 1)), sem((t, ny - 1)), sem((3, nx - 1)), sem((t, nx - 1)),
         ]
+        for order in self.orders:
+            n1, n2 = self.sizes(order)
+            out += [
+                pltpu.VMEM((3, n1, n2) + tile, bf16),
+                pltpu.VMEM((t, n1 - 1, n2) + tile, bf16),
+                pltpu.VMEM((3, n2) + tile, bf16),
+                pltpu.VMEM((t, n2 - 1) + tile, bf16),
+                sem((3, n1 - 1)), sem((t, n1 - 1)), sem((3, n2 - 1)), sem((t, n2 - 1)),
+            ]
+        return out
 
     def bind(self, refs, at_refs, b_refs, out_refs):
-        (self.send0, self.keep, self.recv0, self.pa, self.pb, self.r1a, self.r1b, self.qa, self.qb,
-         self.r2a, self.r2b, self.s0, self.d0, self.s1a, self.d1a, self.s1b, self.d1b,
-         self.s2a, self.d2a, self.s2b, self.d2b) = refs
+        self.send0, self.keep, self.recv0, self.s0, self.d0 = refs[:5]
+        self.half = [refs[5 + 8 * h : 13 + 8 * h] for h in range(2)]
         self.at_refs, self.b_refs, self.out_refs = at_refs, b_refs, out_refs
         ctx = lax.axis_index("ctx")
         self.mx, self.core, self.my = ctx // 2, lax.rem(ctx, 2), lax.axis_index("seq")
 
-    def at_x(self, d):
-        return {"ctx": lax.rem(self.mx + d, self.nx) * 2 + self.core}
-
-    def at_y(self, d):
-        return {"seq": lax.rem(self.my + d, self.ny)}
+    def axis(self, name, d):
+        if name == "x":
+            to = lax.rem(self.mx + d, self.nx)
+            return to, {"ctx": to * 2 + self.core}
+        to = lax.rem(self.my + d, self.ny)
+        return to, {"seq": to}
 
     def at_mate(self):
         return {"ctx": self.mx * 2 + 1 - self.core}
 
     def greet(self, bar):
         places = [self.at_mate()]
-        places += [self.at_x(d) for d in range(1, self.nx)]
-        places += [self.at_y(d) for d in range(1, self.ny)]
+        places += [self.axis("x", d)[1] for d in range(1, self.nx)]
+        places += [self.axis("y", d)[1] for d in range(1, self.ny)]
         for place in places:
             pl.semaphore_signal(bar, inc=1, device_id=place, device_id_type=MESH)
         return len(places)
 
-    def c0(self, c, slot):
-        return remote(self.send0.at[slot], self.recv0.at[c], self.s0.at[slot], self.d0.at[c], self.at_mate())
-
-    def c1a(self, c, slot, d):
+    def c0(self, c):
+        slot = lax.rem(c, 2)
         return remote(
-            self.pa.at[slot, lax.rem(self.mx + d, self.nx)], self.r1a.at[c, d - 1],
-            self.s1a.at[slot, d - 1], self.d1a.at[c, d - 1], self.at_x(d),
+            self.send0.at[slot], self.recv0.at[c], self.s0.at[slot], self.d0.at[c], self.at_mate()
         )
 
-    def c1b(self, c, slot, d):
-        return remote(
-            self.pb.at[slot, lax.rem(self.my + d, self.ny)], self.r1b.at[c, d - 1],
-            self.s1b.at[slot, d - 1], self.d1b.at[c, d - 1], self.at_y(d),
-        )
-
-    def c2a(self, c, slot, d):
-        return remote(
-            self.qa.at[slot, lax.rem(self.my + d, self.ny)], self.r2a.at[c, d - 1],
-            self.s2a.at[slot, d - 1], self.d2a.at[c, d - 1], self.at_y(d),
-        )
-
-    def c2b(self, c, slot, d):
-        return remote(
-            self.qb.at[slot, lax.rem(self.mx + d, self.nx)], self.r2b.at[c, d - 1],
-            self.s2b.at[slot, d - 1], self.d2b.at[c, d - 1], self.at_x(d),
-        )
+    def c1(self, h, c, d):
+        p, r1, _, _, sent, done, _, _ = self.half[h]
+        to, where = self.axis(self.orders[h][0], d)
+        slot = lax.rem(c, 3)
+        return remote(p.at[slot, to], r1.at[c, d - 1], sent.at[slot, d - 1], done.at[c, d - 1], where)
+
+    def c2(self, h, c, d):
+        _, _, q, r2, _, _, sent, done = self.half[h]
+        to, where = self.axis(self.orders[h][1], d)
+        slot = lax.rem(c, 3)
+        return remote(q.at[slot, to], r2.at[c, d - 1], sent.at[slot, d - 1], done.at[c, d - 1], where)
 
     def make(self, c):
         slot = lax.rem(c, 2)
@@ -304,7 +296,7 @@
 
         @pl.when(c >= 2)
         def _():
-            self.c0(c, slot).wait_send()
+            self.c0(c).wait_send()
 
         def products(at_ref, b_ref, col, parity, write):
             def tile(e, carry):
@@ -334,89 +326,77 @@
                 at_ref, b_ref = self.at_refs[job["a"]], self.b_refs[job["b"]]
                 col = pl.multiple_of((c - lo + job["first"]) * (2 * lanes), 2 * lanes)
                 products(at_ref, b_ref, col, 1 - self.core, to_send)
-                self.c0(c, slot).start()
+                self.c0(c).start()
                 products(at_ref, b_ref, col, self.core, to_keep)
 
     def pair(self, c):
-        slot = lax.rem(c, 3)
-        nx, ny = self.nx, self.ny
+        slot, two = lax.rem(c, 3), lax.rem(c, 2)
 
         @pl.when(c >= 3)
         def _():
-            for d in range(1, nx):
-                self.c1a(c, slot, d).wait_send()
-            for d in range(1, ny):
-                self.c1b(c, slot, d).wait_send()
-
-        self.c0(c, lax.rem(c, 2)).wait_recv()
-        for x in range(nx):
-            for y in range(ny):
-                self.pa[slot, x, y] = (
-                    self.keep[lax.rem(c, 2), x, y, 0] + self.recv0[c, x, y, 0].astype(f32)
-                ).astype(bf16)
-        for d in range(1, nx):
-            self.c1a(c, slot, d).start()
-        for x in range(nx):
-            for y in range(ny):
-                self.pb[slot, y, x] = (
-                    self.keep[lax.rem(c, 2), x, y, 1] + self.recv0[c, x, y, 1].astype(f32)
-                ).astype(bf16)
-        for d in range(1, ny):
-            self.c1b(c, slot, d).start()
+            for h in range(2):
+                for d in range(1, self.sizes(self.orders[h])[0]):
+                    self.c1(h, c, d).wait_send()
+
+        self.c0(c).wait_recv()
+        for h, order in enumerate(self.orders):
+            p = self.half[h][0]
+            for x in range(self.nx):
+                for y in range(self.ny):
+                    spot = (x, y) if order == "xy" else (y, x)
+                    p[(slot,) + spot] = (
+                        self.keep[two, x, y, h] + self.recv0[c, x, y, h].astype(f32)
+                    ).astype(bf16)
+            for d in range(1, self.sizes(order)[0]):
+                self.c1(h, c, d).start()
+
+    def own(self, name):
+        return self.mx if name == "x" else self.my
 
     def cross(self, c):
         slot = lax.rem(c, 3)
-        nx, ny = self.nx, self.ny
 
         @pl.when(c >= 3)
         def _():
-            for d in range(1, ny):
-                self.c2a(c, slot, d).wait_send()
-            for d in range(1, nx):
-                self.c2b(c, slot, d).wait_send()
-
-        for d in range(1, nx):
-            self.c1a(c, slot, d).wait_recv()
-        for y in range(ny):
-            acc = self.pa[slot, self.mx, y].astype(f32)
-            for d in range(1, nx):
-                acc = acc + self.r1a[c, d - 1, y].astype(f32)
-            self.qa[slot, y] = acc.astype(bf16)
-        for d in range(1, ny):
-            self.c2a(c, slot, d).start()
-        for d in range(1, ny):
-            self.c1b(c, slot, d).wait_recv()
-        for x in range(nx):
-            acc = self.pb[slot, self.my, x].astype(f32)
-            for d in range(1, ny):
-                acc = acc + self.r1b[c, d - 1, x].astype(f32)
-            self.qb[slot, x] = acc.astype(bf16)
-        for d in range(1, nx):
-            self.c2b(c, slot, d).start()
+            for h in range(2):
+                for d in range(1, self.sizes(self.orders[h])[1]):
+                    self.c2(h, c, d).wait_send()
+
+        for h, order in enumerate(self.orders):
+            n1, n2 = self.sizes(order)
+            p, r1, q = self.half[h][:3]
+            for d in range(1, n1):
+                self.c1(h, c, d).wait_recv()
+            for e in range(n2):
+                acc = p[slot, self.own(order[0]), e].astype(f32)
+                for d in range(1, n1):
+                    acc = acc + r1[c, d - 1, e].astype(f32)
+                q[slot, e] = acc.astype(bf16)
+            for d in range(1, n2):
+                self.c2(h, c, d).start()
 
     def finish(self, c):
         slot = lax.rem(c, 3)
-        nx, ny = self.nx, self.ny
-        for d in range(1, ny):
-            self.c2a(c, slot, d).wait_recv()
-        for d in range(1, nx):
-            self.c2b(c, slot, d).wait_recv()
+        totals = []
+        for h, order in enumerate(self.orders):
+            n2 = self.sizes(order)[1]
+            q, r2 = self.half[h][2:4]
+            for d in range(1, n2):
+                self.c2(h, c, d).wait_recv()
+            acc = q[slot, self.own(order[1])].astype(f32)
+            for d in range(1, n2):
+                acc = acc + r2[c, d - 1].astype(f32)
+            totals.append(acc)
         for job, (lo, hi) in zip(self.jobs, self.spans):
 
             @pl.when((c >= lo) & (c < hi))
             def _():
                 out_ref = self.out_refs[job["out"]]
                 col = pl.multiple_of((c - lo + job["place"]) * (2 * lanes), 2 * lanes)
-                acc = self.qa[slot, self.my].astype(f32)
-                for d in range(1, ny):
-                    acc = acc + self.r2a[c, d - 1].astype(f32)
-                out_ref[:, pl.ds(col, lanes)] = acc
-                acc = self.qb[slot, self.mx].astype(f32)
-                for d in range(1, nx):
-                    acc = acc + self.r2b[c, d - 1].astype(f32)
-                out_ref[:, pl.ds(col + lanes, lanes)] = acc
-
-    def early(self, it):
+                out_ref[:, pl.ds(col, lanes)] = totals[0]
+                out_ref[:, pl.ds(col + lanes, lanes)] = totals[1]
+
+    def tick(self, it):
         @pl.when((it >= 5) & (it < self.total + 5))
         def _():
             self.finish(it - 5)
@@ -429,22 +409,20 @@
         def _():
             self.pair(it - 1)
 
-    def late(self, it):
         @pl.when(it < self.total)
         def _():
             self.make(it)
 
     def drain(self):
         for c in range(max(self.total - 2, 0), self.total):
-            self.c0(c, c % 2).wait_send()
+            self.c0(c).wait_send()
         for c in range(max(self.total - 3, 0), self.total):
-            slot = c % 3
-            for d in range(1, self.nx):
-                self.c1a(c, slot, d).wait_send()
-                self.c2b(c, slot, d).wait_send()
-            for d in range(1, self.ny):
-                self.c1b(c, slot, d).wait_send()
-                self.c2a(c, slot, d).wait_send()
+            for h, order in enumerate(self.orders):
+                n1, n2 = self.sizes(order)
+                for d in range(1, n1):
+                    self.c1(h, c, d).wait_send()
+                for d in range(1, n2):
+                    self.c2(h, c, d).wait_send()
 
 
 class GainSum:
@@ -564,7 +542,7 @@
 
 def attention_back(
     back, grad, proj, attn_gain, w_output, query_rot, keys, values, attn, lse, pos_row, order,
-    query_norm, key_norm, scales, qgain, kgain, cosine, sine, cid,
+    query_norm, key_norm, scales, qgain, kgain, cosine, sine, ats, bs, jobs, widths, cid,
 ):
     rows, width = back.shape
     local = w_output.shape[0]
@@ -577,25 +555,43 @@
     scale = head_dim ** (-0.5)
     tile = 64
     sub = rows // 2
+    na, nb, n_out = len(ats), len(bs), len(widths)
+    grads = None
+    if jobs:
+        grads = GradScatter(2 * nx, lax.axis_size("seq"), width, jobs, ("yx", "yx"))
 
     def body(
         back_ref, grad_ref, proj_ref, again_ref, w_ref, q_ref, k_ref, v_ref, attn_ref, lse_ref,
-        prow_ref, order_ref, qn_ref, kn_ref, sc_ref, qg_ref, kg_ref, cos_ref, sin_ref,
-        dqkv_ref, dprojt_ref, dagain_ref, dqg_ref, dkg_ref,
-        dproj, dout, columns, delta, dqs, dks, send0, keep, recv0, recv1,
-        s0, d0, s1, d1, *small_refs,
+        prow_ref, order_ref, qn_ref, kn_ref, sc_ref, qg_ref, kg_ref, cos_ref, sin_ref, *rest,
     ):
-        small.bind(small_refs)
+        at_refs, b_refs, rest = rest[:na], rest[na : na + nb], rest[na + nb :]
+        dqkv_ref, dprojt_ref, dagain_ref, dqg_ref, dkg_ref = rest[:5]
+        grad_outs, rest = rest[5 : 5 + n_out], rest[5 + n_out :]
+        (dproj, dout, columns, delta, dqs, dks, send0, keep, recv0, recv1, s0, d0, s1, d1) = rest[:14]
+        small.bind(rest[14 : 14 + n_small])
+        if jobs:
+            grads.bind(rest[14 + n_small :], at_refs, b_refs, grad_outs)
+
+        def tick(it):
+            if jobs:
+                grads.tick(it)
+
         ctx = lax.axis_index("ctx")
         mx, core = ctx // 2, lax.rem(ctx, 2)
         bar = pltpu.get_barrier_semaphore()
         mate = {"ctx": mx * 2 + 1 - core}
-        peers = small.greet(bar) + nx
-        pl.semaphore_signal(bar, inc=1, device_id=mate, device_id_type=MESH)
-        for d in range(1, nx):
-            pl.semaphore_signal(
-                bar, inc=1, device_id={"ctx": lax.rem(mx + d, nx) * 2 + core}, device_id_type=MESH
-            )
+        if jobs:
+            peers = small.greet(bar) + grads.greet(bar)
+        else:
+            peers = small.greet(bar) + nx
+            pl.semaphore_signal(bar, inc=1, device_id=mate, device_id_type=MESH)
+            for d in range(1, nx):
+                pl.semaphore_signal(
+                    bar, inc=1, device_id={"ctx": lax.rem(mx + d, nx) * 2 + core},
+                    device_id_type=MESH,
+                )
+        pl.semaphore_wait(bar, peers)
+        tick(jnp.int32(0))
 
         dagain_ref[...] = jnp.zeros_like(dagain_ref)
 
@@ -627,7 +623,6 @@
         columns[...] = acc
         delta[...] = jnp.transpose(columns[...])[:8]
         dqs[...] = jnp.zeros_like(dqs)
-        pl.semaphore_wait(bar, peers)
 
         def c0(h):
             slot = lax.rem(h, 2)
@@ -651,11 +646,14 @@
                 seen = place + lax.broadcasted_iota(jnp.int32, (sub, rows), 0) <= prow_ref[...]
                 share = jnp.where(seen, jnp.exp(score - lse_ref[pl.ds(h, 1), :]), 0.0)
                 dshare = dot_nt(value, dhead)
-                dscore = (share * (dshare - delta[pl.ds(h, 1), :]) * scale).astype(bf16)
-                dqs[:, hs] += dot_tn(dscore, key)
+                dscore = share * (dshare - delta[pl.ds(h, 1), :]) * scale
+                high = dscore.astype(bf16)
+                low = (dscore - high.astype(f32)).astype(bf16)
+                dqs[:, hs] += dot_tn(high, key) + dot_tn(low, key)
                 write(
                     x, slice(part * sub, (part + 1) * sub),
-                    jnp.dot(dscore, query, preferred_element_type=f32),
+                    jnp.dot(high, query, preferred_element_type=f32)
+                    + jnp.dot(low, query, preferred_element_type=f32),
                     jnp.dot(share.astype(bf16), dhead, preferred_element_type=f32),
                 )
 
@@ -681,6 +679,7 @@
 
             lax.fori_loop(0, nx, mates, 0)
             c0(h).start()
+            tick(2 * h + 1)
 
             def owns(e, carry):
                 one_block(h, hs, lax.rem(mx + 1 + e, nx), core, to_keep)
@@ -696,12 +695,20 @@
             lax.fori_loop(0, nx, add, 0)
             for d in range(1, nx):
                 c1(h, d).start()
+            tick(2 * h + 2)
 
         def heads_loop(h, carry):
             one_head(h)
             return carry
 
         lax.fori_loop(0, heads, heads_loop, 0)
+        if jobs:
+
+            def more(it, carry):
+                grads.tick(it)
+                return carry
+
+            lax.fori_loop(2 * heads + 1, grads.steps, more, 0)
 
         dot_q = jnp.zeros((rows, 1), f32)
         for h in range(heads):
@@ -745,20 +752,22 @@
                 c0(h).wait_send()
             for d in range(1, nx):
                 c1(h, d).wait_send()
+        if jobs:
+            grads.drain()
 
     sem = pltpu.SemaphoreType.DMA
     pair = (rows, 2 * lanes)
     return comm_call(
         body,
         [back, grad, proj, attn_gain, w_output, query_rot, keys, values, attn, lse, pos_row,
-         order, query_norm, key_norm, scales, qgain, kgain, cosine, sine],
+         order, query_norm, key_norm, scales, qgain, kgain, cosine, sine] + ats + bs,
         [
             jax.ShapeDtypeStruct((rows, 3 * local), bf16),
             jax.ShapeDtypeStruct((width, rows), bf16),
             jax.ShapeDtypeStruct((1, width), f32),
             jax.ShapeDtypeStruct((1, local), f32),
             jax.ShapeDtypeStruct((1, local), f32),
-        ],
+        ] + [jax.ShapeDtypeStruct((grads.rows, w), f32) for w in widths],
         [
             pltpu.VMEM((rows, width), bf16), pltpu.VMEM((rows, local), bf16),
             pltpu.VMEM((rows, lanes), f32), pltpu.VMEM((8, rows), f32),
@@ -766,12 +775,12 @@
             pltpu.VMEM((2, nx) + pair, bf16), pltpu.VMEM((2, nx) + pair, bf16),
             pltpu.VMEM((heads, nx) + pair, bf16), pltpu.VMEM((heads, nx - 1) + pair, bf16),
             sem((2,)), sem((heads,)), sem((heads, nx - 1)), sem((heads, nx - 1)),
-        ] + small.scratch(),
+        ] + small.scratch() + (grads.scratch() if jobs else []),
         cid, "attention_back", {11},
     )
 
 
-def front(tokens, w_query, w_key, w_value, w_output, qgain, kgain, cosine, sine, order, cid):
+def front(tokens, w_query, w_key, w_value, qgain, kgain, cosine, sine, order, cid):
     rows, width = tokens.shape
     local = w_query.shape[1]
     head_dim = lanes
@@ -780,24 +789,21 @@
     count = nx * 2 * rows
     n_tp = lax.axis_size("tp")
     small = LineSmall(n_tp, rows)
-    line = LineSum(n_tp, rows, width)
-    n_small, n_line = len(small.scratch()), len(line.scratch())
+    n_small = len(small.scratch())
     scale = head_dim ** (-0.5)
     group = rows // 2
 
     def body(
-        tok_hbm, wq_hbm, wk_hbm, wv_hbm, wo_hbm, qg_ref, kg_ref, cos_ref, sin_ref, order_ref,
-        qrot_out, key_out, value_out, qn_out, kn_out, attn_out, tokt_out, proj_out, sc_out, lse_out,
-        tok, tokt, w3, wo, qn, kn, qrot, keys, values, peak, total, acc, attn, loads, stores,
+        tok_hbm, wq_hbm, wk_hbm, wv_hbm, qg_ref, kg_ref, cos_ref, sin_ref, order_ref,
+        qrot_out, key_out, value_out, qn_out, kn_out, attn_out, tokt_out, sc_out, lse_out,
+        tok, tokt, w3, qn, kn, qrot, keys, values, peak, total, acc, attn, loads, stores,
         sx, dx, sm, dm, sf, df, *rest,
     ):
         small.bind(rest[:n_small])
-        line.bind(rest[n_small : n_small + n_line])
         copies = [
             pltpu.make_async_copy(src, dst, loads.at[i])
             for i, (src, dst) in enumerate(
-                [(tok_hbm, tok), (wv_hbm, w3.at[2]), (wq_hbm, w3.at[0]), (wk_hbm, w3.at[1]),
-                 (wo_hbm, wo)]
+                [(tok_hbm, tok), (wv_hbm, w3.at[2]), (wq_hbm, w3.at[0]), (wk_hbm, w3.at[1])]
             )
         ]
         for copy in copies:
@@ -955,19 +961,6 @@
         ]
         for copy in outs:
             copy.start()
-        copies[4].wait()
-        for j in range(n_tp):
-            line.own[j] = jnp.dot(
-                attn[...], wo[:, j * line.part : (j + 1) * line.part], preferred_element_type=f32
-            ).astype(bf16)
-
-        def one(t, carry):
-            line.step(t)
-            return carry
-
-        lax.fori_loop(0, line.steps, one, 0)
-        line.ship(proj_out, stores, 7)
-        line.drain()
         for copy in outs:
             copy.wait()
         for b in range(2):
@@ -984,32 +977,34 @@
         out_shape=[
             block((rows, local), bf16), block((count, local), bf16), block((count, local), bf16),
             block((rows, local), f32), block((rows, local), f32), block((rows, local), bf16),
-            block((width, rows), bf16), block((rows, width), bf16),
+            block((width, rows), bf16),
             block((rows, lanes), f32), block((8, rows), f32),
         ],
-        in_specs=[hbm] * 5 + [vmem_spec()] * 4 + [pl.BlockSpec(memory_space=pltpu.SMEM)],
-        out_specs=[hbm] * 8 + [vmem_spec()] * 2,
+        in_specs=[hbm] * 4 + [vmem_spec()] * 4 + [pl.BlockSpec(memory_space=pltpu.SMEM)],
+        out_specs=[hbm] * 7 + [vmem_spec()] * 2,
         scratch_shapes=[
             pltpu.VMEM((rows, width), bf16), pltpu.VMEM((width, rows), bf16),
             pltpu.VMEM((3, width, local), bf16),
-            pltpu.VMEM((local, width), bf16), pltpu.VMEM((rows, local), f32),
+            pltpu.VMEM((rows, local), f32),
             pltpu.VMEM((rows, local), f32), pltpu.VMEM((rows, local), bf16),
             pltpu.VMEM((count, local), bf16), pltpu.VMEM((count, local), bf16),
             pltpu.VMEM((heads, rows, 1), f32), pltpu.VMEM((heads, rows, 1), f32),
             pltpu.VMEM((rows, local), f32), pltpu.VMEM((rows, local), bf16),
-            sem((5,)), sem((7 + n_tp,)),
+            sem((4,)), sem((7,)),
             sem((2, nx - 1)), sem((2, nx - 1)), sem((2,)), sem((2,)),
             sem((2, nx - 1)), sem((2, nx - 1)),
-        ] + small.scratch() + line.scratch(),
+        ] + small.scratch(),
         compiler_params=pltpu.CompilerParams(
             collective_id=cid, has_side_effects=True, vmem_limit_bytes=62 * 2**20
         ),
         name="front",
-    )(tokens, w_query, w_key, w_value, w_output, qgain, kgain, cosine, sine, order)
-
-
-def load_list(pairs, sems):
-    copies = [pltpu.make_async_copy(src, dst, sems.at[i]) for i, (src, dst) in enumerate(pairs)]
+    )(tokens, w_query, w_key, w_value, qgain, kgain, cosine, sine, order)
+
+
+def load_list(pairs, sems, base=0):
+    copies = [
+        pltpu.make_async_copy(src, dst, sems.at[base + i]) for i, (src, dst) in enumerate(pairs)
+    ]
     for copy in copies:
         copy.start()
     return copies
@@ -1034,94 +1029,124 @@
     )(*args)
 
 
-def mlp_forward(tokens, proj, attn_gain, w_gate, w_up, w_down, cid):
+def middle(attn, tokens, attn_gain, w_output, w_gate, w_up, w_down, cid):
     rows, width = tokens.shape
-    wide = w_gate.shape[1]
+    local, wide = w_output.shape[0], w_gate.shape[1]
     n_tp = lax.axis_size("tp")
-    line = LineSum(n_tp, rows, width)
+    line = LineSum(n_tp, 2 * rows, width, 4 * row_chains)
     n_line = len(line.scratch())
+    half = rows // 2
     tile = 64
     cut = 512
     n_cut = wide // cut
+    part = line.part
 
     def body(
-        tok_hbm, proj_hbm, again_ref, wg_hbm, wu_hbm, wd_hbm,
-        hidt_out, gate_out, up_out, inner_out, down_out,
-        tok, proj_v, hid, hidt, gate, up, inner, wg, wu, wd, first, loads, stores, *rest,
+        attn_hbm, tok_hbm, again_ref, wo_hbm, wg_hbm, wu_hbm, wd_hbm,
+        proj_out, hidt_out, gate_out, up_out, inner_out, down_out,
+        attn_v, tok, wo, hid, hidt, gate, up, inner, wg, wu, wd, first, loads, stores, *rest,
     ):
         line.bind(rest[:n_line])
-        start = load_list([(proj_hbm, proj_v), (tok_hbm, tok)], first)
+        start = load_list([(attn_hbm, attn_v), (wo_hbm, wo), (tok_hbm, tok)], first)
         pairs = []
         for j in range(n_cut):
             cols = pl.ds(j * cut, cut)
             pairs += [(wg_hbm.at[:, cols], wg.at[j]), (wu_hbm.at[:, cols], wu.at[j])]
         for j in range(n_tp):
-            cols = pl.ds(j * line.part, line.part)
+            cols = pl.ds(j * part, part)
             pairs += [(wd_hbm.at[:, cols], wd.at[j])]
         weights = load_list(pairs, loads)
         bar = pltpu.get_barrier_semaphore()
         peers = line.greet(bar)
         for copy in start:
             copy.wait()
-
-        def norm_rows(t, carry):
-            sl = pl.ds(pl.multiple_of(t * tile, tile), tile)
-            out = proj_v[sl].astype(f32)
-            inv = lax.rsqrt(jnp.mean(out * out, axis=1, keepdims=True) + norm_eps)
-            hid[sl] = (tok[sl].astype(f32) + out * inv * again_ref[...]).astype(bf16)
+        for j in range(n_tp):
+            line.own[j, :rows] = jnp.dot(
+                attn_v[...], wo[:, j * part : (j + 1) * part], preferred_element_type=f32
+            ).astype(bf16)
+        pl.semaphore_wait(bar, peers)
+
+        def step(t, carry):
+            line.step(t)
+
+            @pl.when(t == 3 * n_tp + 1)
+            def _():
+                hidt[...] = jnp.transpose(hid[...])
+
             return carry
 
-        lax.fori_loop(0, rows // tile, norm_rows, 0)
-        for j in range(n_cut):
-            cols = slice(j * cut, (j + 1) * cut)
-            weights[2 * j].wait()
-            weights[2 * j + 1].wait()
-            for r in range(2):
-                sl = slice(r * rows // 2, (r + 1) * rows // 2)
+        def row_half(c, carry):
+            base = pl.multiple_of(c * half, half)
+            sl = pl.ds(base, half)
+            lax.fori_loop(c * 2 * n_tp, c * n_tp + 2 * n_tp - 1, step, 0)
+
+            def norm_rows(t, carry):
+                rs = pl.ds(pl.multiple_of(base + t * tile, tile), tile)
+                outs = [line.res[j, rs].astype(f32) for j in range(n_tp)]
+                square = sum(jnp.sum(out * out, axis=1, keepdims=True) for out in outs)
+                inv = lax.rsqrt(square * (1.0 / width) + norm_eps)
+                for j, out in enumerate(outs):
+                    cols = slice(j * part, (j + 1) * part)
+                    hid[rs, cols] = (
+                        tok[rs, cols].astype(f32) + out * inv * again_ref[:, cols]
+                    ).astype(bf16)
+                return carry
+
+            lax.fori_loop(0, half // tile, norm_rows, 0)
+            for j in range(n_cut):
+                cols = slice(j * cut, (j + 1) * cut)
+
+                @pl.when(c == 0)
+                def _():
+                    weights[2 * j].wait()
+                    weights[2 * j + 1].wait()
+
                 g = jnp.dot(hid[sl], wg[j], preferred_element_type=f32)
                 u = jnp.dot(hid[sl], wu[j], preferred_element_type=f32)
                 gate[sl, cols] = g.astype(bf16)
                 up[sl, cols] = u.astype(bf16)
                 inner[sl, cols] = (g * jax.nn.sigmoid(g) * u).astype(bf16)
+                for v in range(j * row_chains // n_cut, (j + 1) * row_chains // n_cut):
+                    line.piece(((c + 2) * n_tp - 1) * row_chains + v)
+            for j in range(n_tp):
+
+                @pl.when(c == 0)
+                def _():
+                    weights[2 * n_cut + j].wait()
+
+                line.own[j, pl.ds(rows + base, half)] = jnp.dot(
+                    inner[sl], wd[j], preferred_element_type=f32
+                ).astype(bf16)
+            return carry
+
+        lax.fori_loop(0, 2, row_half, 0)
         outs = load_list([(gate, gate_out), (up, up_out), (inner, inner_out)], stores)
-        for j in range(n_tp):
-            weights[2 * n_cut + j].wait()
-            line.own[j] = jnp.dot(inner[...], wd[j], preferred_element_type=f32).astype(bf16)
-        pl.semaphore_wait(bar, peers)
-
-        def one(t, carry):
-            line.step(t)
-
-            @pl.when(t == 2)
-            def _():
-                hidt[...] = jnp.transpose(hid[...])
-
-            return carry
-
-        lax.fori_loop(0, line.steps, one, 0)
+        ready = line.ship(proj_out, stores, 4, 0, rows)
+        lax.fori_loop(3 * n_tp, line.steps, step, 0)
         last = pltpu.make_async_copy(hidt, hidt_out, stores.at[3])
         last.start()
-        line.ship(down_out, stores, 4)
+        ready = ready + line.ship(down_out, stores, 4 + n_tp, rows, rows)
         line.drain()
-        for copy in outs + [last]:
+        for copy in outs + [last] + ready:
             copy.wait()
 
     sem = pltpu.SemaphoreType.DMA
     return kernel_call(
-        body, [tokens, proj, attn_gain, w_gate, w_up, w_down], "hhvhhh",
-        [((width, rows), bf16), ((rows, wide), bf16), ((rows, wide), bf16), ((rows, wide), bf16),
-         ((rows, width), bf16)],
-        "hhhhh",
+        body, [attn, tokens, attn_gain, w_output, w_gate, w_up, w_down], "hhvhhhh",
+        [((rows, width), bf16), ((width, rows), bf16), ((rows, wide), bf16), ((rows, wide), bf16),
+         ((rows, wide), bf16), ((rows, width), bf16)],
+        "hhhhhh",
         [
-            pltpu.VMEM((rows, width), bf16), pltpu.VMEM((rows, width), bf16),
+            pltpu.VMEM((rows, local), bf16), pltpu.VMEM((rows, width), bf16),
+            pltpu.VMEM((local, width), bf16),
             pltpu.VMEM((rows, width), bf16), pltpu.VMEM((width, rows), bf16),
             pltpu.VMEM((rows, wide), bf16), pltpu.VMEM((rows, wide), bf16),
             pltpu.VMEM((rows, wide), bf16),
             pltpu.VMEM((n_cut, width, cut), bf16), pltpu.VMEM((n_cut, width, cut), bf16),
-            pltpu.VMEM((n_tp, wide, line.part), bf16),
-            sem((2,)), sem((2 * n_cut + n_tp,)), sem((4 + n_tp,)),
+            pltpu.VMEM((n_tp, wide, part), bf16),
+            sem((3,)), sem((2 * n_cut + n_tp,)), sem((4 + 2 * n_tp,)),
         ] + line.scratch(),
-        cid, "mlp_forward",
+        cid, "middle",
     )
 
 
@@ -1136,6 +1161,8 @@
     cut = 512
     n_cut = wide // cut
     part = line.part
+    lead = row_chains * n_tp // (n_cut + n_tp)
+    ticks = 3
 
     def body(
         down_ref, grad_ref, mgain_ref, gate_hbm, up_hbm, inner_hbm, hidt_hbm, wg_hbm, wu_hbm, wd_hbm,
@@ -1179,67 +1206,85 @@
             copy.wait()
         pl.semaphore_wait(bar, peers)
 
-        def inner_back(j, carry):
-            fetch(rows_of(wd_hbm, j, cut), j).wait()
-            cols = pl.ds(pl.multiple_of(j * cut, cut), cut)
-            for r in range(2):
-                sl = slice(r * rows // 2, (r + 1) * rows // 2)
+        half = rows // 2
+
+        def row_half(c, carry):
+            sl = pl.ds(pl.multiple_of(c * half, half), half)
+
+            def beside(i, t):
+                @pl.when(c == 1)
+                def _():
+                    for v in range(lead):
+                        line.piece(i * lead + v)
+
+                if t is not None:
+                    grads.tick(t)
+
+            def inner_back(j, carry):
+                fetch(rows_of(wd_hbm, j, cut), j).wait()
+                cols = pl.ds(pl.multiple_of(j * cut, cut), cut)
                 dmix = dot_nt(ddown[sl], ring[j])
                 g, u = gate_v[sl, cols].astype(f32), up_v[sl, cols].astype(f32)
                 sig = jax.nn.sigmoid(g)
                 dgate[sl, cols] = (dmix * u * sig * (1.0 + g * (1.0 - sig))).astype(bf16)
                 dup[sl, cols] = (dmix * (g * sig)).astype(bf16)
 
-            @pl.when(lax.rem(j, 2) == 0)
-            def _():
-                fetch(rows_of(wg_hbm, j // 2, part), j).start()
-
-            @pl.when(lax.rem(j, 2) == 1)
-            def _():
-                fetch(rows_of(wu_hbm, j // 2, part), j).start()
-                grads.early(j // 2)
-                grads.late(j // 2)
-
-            return carry
-
-        lax.fori_loop(0, n_cut, inner_back, 0)
-        outs = load_list([(dgate, dgate_out), (dup, dup_out)], stores)
-
-        def hidden_back(j, carry):
-            slot = lax.rem(2 * j, 4)
-            fetch(rows_of(wg_hbm, j, part), slot).wait()
-            fetch(rows_of(wu_hbm, j, part), slot + 1).wait()
-            for r in range(2):
-                sl = slice(r * rows // 2, (r + 1) * rows // 2)
+                @pl.when(lax.rem(j, 2) == 0)
+                def _():
+                    fetch(rows_of(wg_hbm, j // 2, part), j).start()
+
+                @pl.when(lax.rem(j, 2) == 1)
+                def _():
+                    fetch(rows_of(wu_hbm, j // 2, part), j).start()
+
+                beside(j, None)
+                return carry
+
+            lax.fori_loop(0, n_cut, inner_back, 0)
+            grads.tick(c * ticks)
+
+            def hidden_back(j, carry):
+                slot = lax.rem(2 * j, 4)
+                fetch(rows_of(wg_hbm, j, part), slot).wait()
+                fetch(rows_of(wu_hbm, j, part), slot + 1).wait()
                 line.own[j, sl] = (
                     dot_nt(dgate[sl], ring[slot]) + dot_nt(dup[sl], ring[slot + 1])
                 ).astype(bf16)
 
-            @pl.when(j + 2 < n_tp)
-            def _():
-                fetch(rows_of(wg_hbm, j + 2, part), slot).start()
-                fetch(rows_of(wu_hbm, j + 2, part), slot + 1).start()
-
-            @pl.when(lax.rem(j, 2) == 1)
-            def _():
-                grads.early(n_cut // 2 + j // 2)
-                grads.late(n_cut // 2 + j // 2)
-
+                @pl.when(j + 2 < n_tp)
+                def _():
+                    fetch(rows_of(wg_hbm, j + 2, part), slot).start()
+                    fetch(rows_of(wu_hbm, j + 2, part), slot + 1).start()
+
+                @pl.when((j + 2 >= n_tp) & (c == 0))
+                def _():
+                    fetch(rows_of(wd_hbm, slot, cut), slot).start()
+                    fetch(rows_of(wd_hbm, slot + 1, cut), slot + 1).start()
+
+                beside(n_cut + j, None)
+
+                @pl.when((lax.rem(j, 2) == 1) & (c * ticks + 1 + j // 2 < (c + 1) * ticks))
+                def _():
+                    grads.tick(c * ticks + 1 + j // 2)
+
+                return carry
+
+            lax.fori_loop(0, n_tp, hidden_back, 0)
             return carry
 
-        lax.fori_loop(0, n_tp, hidden_back, 0)
-        done = n_cut // 2 + n_tp // 2
+        lax.fori_loop(0, 2, row_half, 0)
+        outs = load_list([(dgate, dgate_out), (dup, dup_out)], stores)
+        done, used = 2 * ticks, (n_cut + n_tp) * lead
 
         def one(it, carry):
-            grads.early(it)
             for v in range(pace):
-                line.piece((it - done) * pace + v)
-            grads.late(it)
+                line.piece(used + (it - done) * pace + v)
+            grads.tick(it)
             return carry
 
-        line_steps = -(-line.steps * row_chains // pace)
-        lax.fori_loop(done, max(done + line_steps, grads.steps), one, 0)
-        line.ship(back_out, stores, 2)
+        line_its = -(-(line.steps * row_chains - used) // pace)
+        lax.fori_loop(done, max(done + line_its, grads.steps), one, 0)
+        outs += line.ship(back_out, stores, 2, 0, rows)
         line.drain()
         grads.drain()
         for copy in outs:
@@ -1298,8 +1343,7 @@
 
             @pl.when(lax.rem(j, 2) == 0)
             def _():
-                grads.early(j // 2)
-                grads.late(j // 2)
+                grads.tick(j // 2)
 
             return carry
 
@@ -1307,18 +1351,19 @@
         done = n_tp // 2
 
         def one(it, carry):
-            grads.early(it)
+            grads.tick(it)
             for v in range(pace):
                 line.piece((it - done) * pace + v)
-            grads.late(it)
             return carry
 
         line_steps = -(-line.steps * row_chains // pace)
         lax.fori_loop(done, max(done + line_steps, grads.steps), one, 0)
         small.finish()
-        line.ship(last_out, stores, 0)
+        outs = line.ship(last_out, stores, 0, 0, rows)
         line.drain()
         grads.drain()
+        for copy in outs:
+            copy.wait()
 
     sem = pltpu.SemaphoreType.DMA
     return kernel_call(
@@ -1359,27 +1404,38 @@
     angle_sin = jnp.concatenate([-sine, sine], axis=1)
     qgain = query_gain.reshape(1, local)
     kgain = key_gain.reshape(1, local)
-    (query_rot, keys, values, query_norm, key_norm, attn, tokens_t, proj, scales, lse) = front(
-        inputs, w_query, w_key, w_value, w_output, qgain, kgain, angle_cos, angle_sin, group_order, 1
+    (query_rot, keys, values, query_norm, key_norm, attn, tokens_t, scales, lse) = front(
+        inputs, w_query, w_key, w_value, qgain, kgain, angle_cos, angle_sin, group_order, 1
     )
-    hidden_t, gate, up, inner, down = mlp_forward(
-        inputs, proj, attn_gain[None], w_gate, w_up, w_down, 2
+    proj, hidden_t, gate, up, inner, down = middle(
+        attn, inputs, attn_gain[None], w_output, w_gate, w_up, w_down, 2
     )
-    chunks = wide // (2 * lanes)
     chunk_cols = 2 * lanes
+    chunks = wide // chunk_cols
+    thin = local // chunk_cols
+    n_first = chunks * 5 // 8 if keys.shape[0] <= 8 * rows else chunks
+    n_mid = chunks * 5 // 8 if keys.shape[0] <= 8 * rows else 0
     back, d_gate, d_up, d_mlp_gain, grad_down, grad_gate = mlp_back(
         down, upstream, mlp_gain[None], gate, up, inner, hidden_t, w_gate, w_up, w_down,
         [
             dict(a=0, b=0, first=0, count=chunks, out=0, place=0),
-            dict(a=1, b=1, first=0, count=chunks, out=1, place=0),
+            dict(a=1, b=1, first=0, count=n_first, out=1, place=0),
         ],
-        [wide, wide],
+        [wide, n_first * chunk_cols],
         3,
     )
-    d_qkv, d_proj_t, d_attn_gain, d_query_gain, d_key_gain = attention_back(
+    mid_jobs, mid_widths = [], []
+    if n_mid:
+        mid_jobs = [
+            dict(a=0, b=0, first=n_first, count=chunks - n_first, out=0, place=0),
+            dict(a=0, b=1, first=0, count=n_mid, out=1, place=0),
+        ]
+        mid_widths = [(chunks - n_first) * chunk_cols, n_mid * chunk_cols]
+    d_qkv, d_proj_t, d_attn_gain, d_query_gain, d_key_gain, *mid = attention_back(
         back, upstream, proj, attn_gain[None], w_output, query_rot, keys, values, attn, lse,
         positions[None], group_order, query_norm, key_norm, scales, qgain, kgain, angle_cos,
-        angle_sin, 4,
+        angle_sin, [hidden_t] if n_mid else [], [d_gate, d_up] if n_mid else [], mid_jobs,
+        mid_widths, 4,
     )
     owners = lax.axis_size("ctx") * lax.axis_size("seq")
     pieces = [
@@ -1391,20 +1447,22 @@
     cuts = [piece.shape[1] for piece in pieces]
     packed = jnp.concatenate(pieces, axis=1)
     packed = jnp.pad(packed, ((0, 0), (0, 8 * lanes - packed.shape[1]))).reshape(owners, 8, lanes)
-    thin = local // chunk_cols
     last, grad_up, grad_qkv, grad_output, small = last_sums(
         d_qkv, w_query, w_key, w_value,
         [hidden_t, tokens_t, d_proj_t],
         [d_up, attn],
         [
-            dict(a=0, b=0, first=0, count=chunks, out=0, place=0),
+            dict(a=0, b=0, first=n_mid, count=chunks - n_mid, out=0, place=0),
             dict(a=2, b=1, first=0, count=thin, out=2, place=0),
             dict(a=1, b=2, first=0, count=3 * thin, out=1, place=0),
         ],
-        [wide, 3 * local, local],
+        [(chunks - n_mid) * chunk_cols, 3 * local, local],
         packed,
         5,
     )
+    if n_mid:
+        grad_gate = jnp.concatenate([grad_gate, mid[0]], axis=1)
+        grad_up = jnp.concatenate([mid[1], grad_up], axis=1)
     small = small.reshape(-1)
     g_attn, g_mlp, g_query, g_key = jnp.split(
         small[: sum(cuts)], [cuts[0], cuts[0] + cuts[1], cuts[0] + cuts[1] + cuts[2]]

time: 462 us -> 461 us (level)
    pallas_call x1, Pallas kernels: 102 us -> 44.3 us  [front(): pl.pallas_call(body, out_shape=[block((rows, local), bf16), block((count,...]
    pallas_call x1, Pallas kernels: 48.2 us -> 83.9 us  [comm_call(): pl.pallas_call(body, out_shape=outs, in_specs=[pl.BlockSpec(memory_space=...]
    pallas_call x3, Pallas kernels: 274 us -> 293 us  [kernel_call(): pl.pallas_call(body, out_shape=[jax.ShapeDtypeStruct(*out) for out in out...]
    unnamed x27 -> x33, local copies, waits for them, and re-layouts: 9.65 us -> 7.37 us
where the time goes in v6:
time: 461 us; the launch traced here: 454 us
  Pallas kernels  421 us (91%)
  other arithmetic  20.2 us (4%)
  local copies, waits for them, and re-layouts  10.6 us (2%)
    pallas_call x3, Pallas kernels, kernel_call(): pl.pallas_call(body, out_shape=[jax.ShapeDtypeStruct(*out) for out in out...  293 us
    pallas_call x1, Pallas kernels, comm_call(): pl.pallas_call(body, out_shape=outs, in_specs=[pl.BlockSpec(memory_space=...  83.9 us
    pallas_call x1, Pallas kernels, front(): pl.pallas_call(body, out_shape=[block((rows, local), bf16), block((count,...  44.3 us

profile of v6, /device:TPU:0, one launch (start us, length us, event | category | flops | bytes accessed | tf_op | source)
XLA Modules:
  0.0 453.5 jit_solution(15007806090421307955)
XLA Ops:
  0.7 0.7 select_reduce_fusion
  1.4 1.0 fusion.7
  2.4 1.0 pad_maximum_fusion.2
  3.4 44.3 %front.1 = (bf16[512,512]{1,0:T(8,128)(2,1)}, bf16[2048,512]{1,0:T(8,128)(2,1)}, bf16[2048,512]{1,0:T(8,128)(2,1)}, f32[512,512]{1,0:T(8,128)}, f32[512,512]{1,0...) custom-call(bf16[512,2048]{1,0:T(8,128)(2,1)} %bitcast.30, ...), custom_call_target="tpu_custom_call" | custom-call | tf_op jit(solution)/shard_map/front/pallas_call | solution.py:975
  47.8 121.2 %middle.1 = (bf16[512,2048]{1,0:T(8,128)(2,1)}, bf16[2048,512]{1,0:T(8,128)(2,1)}, bf16[512,2048]{1,0:T(8,128)(2,1)}, bf16[512,2048]{1,0:T(8,128)(2,1)}, bf16[51...) custom-call(bf16[512,512]{1,0:T(8,128)(2,1)} %get-tuple-element.46.attn_hbm.attn_ref.refs_4_, bf16[512,2048]{1,0:T(8,128)(2,1)} %bitcast.31, ...), custom_call_target="tpu_custom_call" | custom-call | tf_op jit(solution)/shard_map/middle/pallas_call | solution.py:1019
  169.0 91.8 %mlp_back.1 = (bf16[512,2048]{1,0:T(8,128)(2,1)}, bf16[512,2048]{1,0:T(8,128)(2,1)}, bf16[512,2048]{1,0:T(8,128)(2,1)}, f32[1,2048]{1,0:T(1,128)}, f32[256,2048]{1,0:T(8,128)}, /*index=5*/f32[256,1280]{1,0:T(8,128)}) custom-call(bf16[512,2048]{1,0:T(8,128)(2,1)} %get-tuple-element.48.down_ref, bf16[512,2048]{1,0:T(8,128)(2,1)} %bitcast.28, ...), custom_call_target="tpu_custom_call" | custom-call | tf_op jit(solution)/shard_map/mlp_back/pallas_call | solution.py:1019
  261.4 83.9 %attention_back.1 = (bf16[512,1536]{1,0:T(8,128)(2,1)}, bf16[2048,512]{1,0:T(8,128)(2,1)}, f32[1,2048]{1,0:T(1,128)}, f32[1,512]{1,0:T(1,128)}, f32[1,512]{1,0:T...) custom-call(bf16[512,2048]{1,0:T(8,128)(2,1)} %get-tuple-element.53.back_ref, bf16[512,2048]{1,0:T(8,128)(2,1)} %bitcast.29, ...), custom_call_target="tpu_custom_call" | custom-call | tf_op jit(solution)/shard_map/attention_back/pallas_call | solution.py:473
  345.8 1.3 reduce.13
  347.3 1.3 reduce.12
  348.9 1.4 reduce.15
  350.2 0.7 reduce.14
  351.0 0.6 copy.41
  351.6 80.2 %last_sums.1 = (bf16[512,2048]{1,0:T(8,128)(2,1)}, f32[256,768]{1,0:T(8,128)}, f32[256,1536]{1,0:T(8,128)}, f32[256,512]{1,0:T(8,128)}, f32[8,128]{1,0:T(8,128)}) custom-call(bf16[512,1536]{1,0:T(8,128)(2,1)} %get-tuple-element.63.dqkv_ref, bf16[2048,512]{1,0:T(8,128)(2,1)} %wq_ref.1, bf16[2048,512]{1,0:T(8,128)(2,1)} %wk_ref.1, bf16[2048,512]{1,0:T(8,128)(2,1)} %wv_ref.1, ...), custom_call_target="tpu_custom_call" | custom-call | tf_op jit(solution)/shard_map/last_sums/pallas_call | solution.py:1019
  431.9 2.9 pad_maximum_fusion.1
  434.7 1.6 pad_maximum_fusion
  436.3 0.7 copy-done
  437.1 0.6 copy-done.4
  437.7 3.2 add_bitcast_fusion
  440.9 1.2 fusion.16
  442.2 1.0 copy.37
  443.3 0.6 fusion.17
  444.4 3.0 copy.38
  448.0 1.1 copy-done.1
  449.7 3.4 fusion.4
  (47 shorter events, 3.5 us)
Async XLA Ops:
  261.4 88.8 %copy-start.14 = (f32[1,2048]{1,0:T(1,128)S(1)}, f32[1,2048]{1,0:T(1,128)}, u32[]{:S(2)}) copy-start(f32[1,2048]{1,0:T(1,128)} %get-tuple-element.67) | copy-start | bytes 24580
  351.6 80.2 %copy-start.8 = (f32[256,1280]{1,0:T(8,128)S(1)}, f32[256,1280]{1,0:T(8,128)}, u32[]{:S(2)}) copy-start(f32[256,1280]{1,0:T(8,128)} %get-tuple-element.76) | copy-start | bytes 3932164
  431.8 2.9 copy-start.7
  431.8 2.9 copy-start.9
  431.8 4.5 copy-start.5
  434.7 2.3 copy-start
  434.7 3.0 copy-start.4
  437.7 3.2 copy-start.6
  440.9 1.3 copy-start.10
  440.9 2.3 copy-start.13
  444.4 3.0 copy-start.2
  444.4 5.1 %copy-start.12 = (f32[2048]{0:T(1024)S(1)}, f32[2048]{0:T(1024)}, u32[]{:S(2)}) copy-start(f32[2048]{0:T(1024)} %param.27) | copy-start | bytes 24580
  447.5 1.6 copy-start.1
  447.5 2.2 copy-start.3
  447.5 2.2 copy-start.11

commit v7 on v6

--- a/solution.py
+++ b/solution.py
@@ -49,9 +49,11 @@
 
     def scratch(self):
         shape = (self.n, self.rows, self.part)
-        return [pltpu.VMEM(shape, bf16)] * 4 + [
-            pltpu.SemaphoreType.DMA((row_chains, self.total))
-        ] * 4
+        return (
+            [pltpu.VMEM(shape, bf16)] * 4
+            + [pltpu.SemaphoreType.DMA] * 2
+            + [pltpu.SemaphoreType.DMA((row_chains, self.total))] * 2
+        )
 
     def bind(self, refs):
         self.own, self.from_l, self.from_r, self.res = refs[:4]
@@ -81,34 +83,40 @@
     def right(self, src, dst, g, p, j):
         sl = self.rows_of(g, p)
         return remote(
-            src.at[j, sl], dst.at[j, sl], self.send_r.at[g, p], self.recv_l.at[g, p],
+            src.at[j, sl], dst.at[j, sl], self.send_r, self.recv_l.at[g, p],
             {"tp": self.i + 1},
         )
 
     def left(self, src, dst, g, q, j):
         sl = self.rows_of(g, q)
         return remote(
-            src.at[j, sl], dst.at[j, sl], self.send_l.at[g, q], self.recv_r.at[g, q],
+            src.at[j, sl], dst.at[j, sl], self.send_l, self.recv_r.at[g, q],
             {"tp": self.i - 1},
         )
 
     def wait_l(self, g, p, j):
         sl = self.rows_of(g, p)
         remote(
-            self.own.at[j, sl], self.from_l.at[j, sl], self.send_r.at[g, p], self.recv_l.at[g, p],
+            self.own.at[j, sl], self.from_l.at[j, sl], self.send_r, self.recv_l.at[g, p],
             {"tp": self.i - 1},
         ).wait_recv()
 
     def wait_r(self, g, q, j):
         sl = self.rows_of(g, q)
         remote(
-            self.own.at[j, sl], self.from_r.at[j, sl], self.send_l.at[g, q], self.recv_r.at[g, q],
+            self.own.at[j, sl], self.from_r.at[j, sl], self.send_l, self.recv_r.at[g, q],
             {"tp": self.i + 1},
         ).wait_recv()
 
     def step(self, t):
-        for g in range(row_chains):
-            self.sub_step(t, g)
+        self.pieces(t * row_chains, row_chains)
+
+    def pieces(self, first, count):
+        def one(v, carry):
+            self.piece(first + v)
+            return carry
+
+        lax.fori_loop(0, count, one, 0)
 
     def piece(self, e):
         t = e // row_chains
@@ -182,20 +190,17 @@
             self.left(res, res, g, q, jl).start()
 
     def drain(self):
-        def one(p, carry):
-            for g in range(row_chains):
-
-                @pl.when(self.has_r)
-                def _():
-                    self.right(self.own, self.from_l, g, p, 0).wait_send()
-
-                @pl.when(self.has_l)
-                def _():
-                    self.left(self.own, self.from_r, g, p, 0).wait_send()
-
-            return carry
-
-        lax.fori_loop(0, self.total, one, 0)
+        @pl.when(self.has_r)
+        def _():
+            remote(
+                self.own, self.from_l, self.send_r, self.recv_l.at[0, 0], {"tp": self.i + 1}
+            ).wait_send()
+
+        @pl.when(self.has_l)
+        def _():
+            remote(
+                self.own, self.from_r, self.send_l, self.recv_r.at[0, 0], {"tp": self.i - 1}
+            ).wait_send()
 
     def ship(self, out_ref, sems, base, start, count):
         return load_list(
@@ -222,6 +227,12 @@
             start += job["count"]
         self.total = start
         self.steps = start + 5
+
+    def out_shapes(self, widths):
+        flips = {job["out"] for job in self.jobs if job["flip"]}
+        return [
+            ((w, self.rows) if i in flips else (self.rows, w), f32) for i, w in enumerate(widths)
+        ]
 
     def sizes(self, order):
         return (self.nx, self.ny) if order == "xy" else (self.ny, self.nx)
@@ -393,8 +404,12 @@
             def _():
                 out_ref = self.out_refs[job["out"]]
                 col = pl.multiple_of((c - lo + job["place"]) * (2 * lanes), 2 * lanes)
-                out_ref[:, pl.ds(col, lanes)] = totals[0]
-                out_ref[:, pl.ds(col + lanes, lanes)] = totals[1]
+                for h in range(2):
+                    place = pl.ds(col + h * lanes, lanes)
+                    if job["flip"]:
+                        out_ref[place, :] = jnp.transpose(totals[h])
+                    else:
+                        out_ref[:, place] = totals[h]
 
     def tick(self, it):
         @pl.when((it >= 5) & (it < self.total + 5))
@@ -426,12 +441,12 @@
 
 
 class GainSum:
-    def __init__(self, n_ctx, n_seq):
-        self.ny, self.n = n_seq, n_ctx * n_seq
+    def __init__(self, n_ctx, n_seq, rows):
+        self.ny, self.n, self.rows = n_seq, n_ctx * n_seq, rows
 
     def scratch(self):
         sem = pltpu.SemaphoreType.DMA
-        return [pltpu.VMEM((self.n - 1, 8, lanes), f32), sem((self.n - 1,)), sem((self.n - 1,))]
+        return [pltpu.VMEM((self.n - 1, self.rows, lanes), f32), sem((self.n - 1,)), sem((self.n - 1,))]
 
     def bind(self, refs, in_ref, out_ref):
         self.got, self.sent, self.done = refs
@@ -440,15 +455,16 @@
 
     def place(self, d):
         to = lax.rem(self.me + d, self.n)
-        return to, {"ctx": to // self.ny, "seq": lax.rem(to, self.ny)}
+        return {"ctx": to // self.ny, "seq": lax.rem(to, self.ny)}
 
     def copy(self, d):
-        to, where = self.place(d)
-        return remote(self.in_ref.at[to], self.got.at[d - 1], self.sent.at[d - 1], self.done.at[d - 1], where)
+        return remote(
+            self.in_ref, self.got.at[d - 1], self.sent.at[d - 1], self.done.at[d - 1], self.place(d)
+        )
 
     def greet(self, bar):
         for d in range(1, self.n):
-            pl.semaphore_signal(bar, inc=1, device_id=self.place(d)[1], device_id_type=MESH)
+            pl.semaphore_signal(bar, inc=1, device_id=self.place(d), device_id_type=MESH)
         return self.n - 1
 
     def start(self):
@@ -456,7 +472,7 @@
             self.copy(d).start()
 
     def finish(self):
-        acc = self.in_ref[self.me]
+        acc = self.in_ref[...]
         for d in range(1, self.n):
             self.copy(d).wait_recv()
             acc = acc + self.got[d - 1]
@@ -767,7 +783,7 @@
             jax.ShapeDtypeStruct((1, width), f32),
             jax.ShapeDtypeStruct((1, local), f32),
             jax.ShapeDtypeStruct((1, local), f32),
-        ] + [jax.ShapeDtypeStruct((grads.rows, w), f32) for w in widths],
+        ] + [jax.ShapeDtypeStruct(*out) for out in (grads.out_shapes(widths) if jobs else [])],
         [
             pltpu.VMEM((rows, width), bf16), pltpu.VMEM((rows, local), bf16),
             pltpu.VMEM((rows, lanes), f32), pltpu.VMEM((8, rows), f32),
@@ -825,45 +841,47 @@
             return pl.ds(pl.multiple_of((x * 2 + owner) * rows, rows), rows)
 
         mine = at(mx, core)
-        boxes = [keys, values]
-
-        def to_peer(b, d):
-            box = boxes[b]
-            return remote(
-                box.at[mine], box.at[mine], sx.at[b, d - 1], dx.at[b, d - 1], peer(d)
-            )
-
-        def from_peer(b, d):
-            box = boxes[b]
+        side = local // 2
+        boxes = [(keys, pl.ds(0, side)), (keys, pl.ds(side, side)), (values, pl.ds(0, local))]
+
+        def move(t, rs, sent, done, where):
+            box, cols = boxes[t]
+            return remote(box.at[rs, cols], box.at[rs, cols], sent, done, where)
+
+        def to_peer(t, d):
+            return move(t, mine, sx.at[t, d - 1], dx.at[t, d - 1], peer(d))
+
+        def from_peer(t, d):
             rs = at(lax.rem(mx + nx - d, nx), core)
-            return remote(box.at[rs], box.at[rs], sx.at[b, d - 1], dx.at[b, d - 1], peer(d))
-
-        def to_mate(b):
-            box = boxes[b]
-            return remote(box.at[mine], box.at[mine], sm.at[b], dm.at[b], mate)
-
-        def from_mate(b):
-            box = boxes[b]
-            rs = at(mx, 1 - core)
-            return remote(box.at[rs], box.at[rs], sm.at[b], dm.at[b], mate)
-
-        def pass_on(b, d):
-            box = boxes[b]
+            return move(t, rs, sx.at[t, d - 1], dx.at[t, d - 1], peer(d))
+
+        def to_mate(t):
+            return move(t, mine, sm.at[t], dm.at[t], mate)
+
+        def from_mate(t):
+            return move(t, at(mx, 1 - core), sm.at[t], dm.at[t], mate)
+
+        def pass_on(t, d):
             rs = at(lax.rem(mx + nx - d, nx), core)
-            return remote(box.at[rs], box.at[rs], sf.at[b, d - 1], df.at[b, d - 1], mate)
-
-        def passed(b, d):
-            box = boxes[b]
+            return move(t, rs, sf.at[t, d - 1], df.at[t, d - 1], mate)
+
+        def passed(t, d):
             rs = at(lax.rem(mx + nx - d, nx), 1 - core)
-            return remote(box.at[rs], box.at[rs], sf.at[b, d - 1], df.at[b, d - 1], mate)
+            return move(t, rs, sf.at[t, d - 1], df.at[t, d - 1], mate)
+
+        def each_peer(act):
+            def one(d, carry):
+                act(d)
+                return carry
+
+            lax.fori_loop(1, nx, one, 0)
 
         copies[0].wait()
         copies[1].wait()
         values[mine] = jnp.dot(tok[...], w3[2], preferred_element_type=f32).astype(bf16)
         pl.semaphore_wait(bar, peers)
-        for d in range(1, nx):
-            to_peer(1, d).start()
-        to_mate(1).start()
+        each_peer(lambda d: to_peer(2, d).start())
+        to_mate(2).start()
         copies[2].wait()
         qn[...] = jnp.dot(tok[...], w3[0], preferred_element_type=f32)
         copies[3].wait()
@@ -891,9 +909,10 @@
 
         for h in range(heads):
             keys[mine, h * head_dim : (h + 1) * head_dim] = rotated(kn, 1, kg_ref, h)
-        for d in range(1, nx):
-            to_peer(0, d).start()
-        to_mate(0).start()
+            if (h + 1) * head_dim in (side, local):
+                t = (h + 1) * head_dim // side - 1
+                each_peer(lambda d: to_peer(t, d).start())
+                to_mate(t).start()
         for h in range(heads):
             qrot[:, h * head_dim : (h + 1) * head_dim] = rotated(qn, 0, qg_ref, h)
         peak[...] = jnp.full_like(peak, masked_score)
@@ -905,7 +924,7 @@
             first, second = order_ref[0, block * 2], order_ref[0, block * 2 + 1]
             return jnp.where(spot < group, first * group + spot, (second - 1) * group + spot)
 
-        def attend(x, owner):
+        def attend(x, owner, low, high):
             block = x * 2 + owner
             rs = at(x, owner)
 
@@ -926,24 +945,49 @@
                 )
                 return carry
 
-            lax.fori_loop(0, heads, one, 0)
-
-        attend(mx, core)
-        for d in range(1, nx):
-            from_peer(1, d).wait_recv()
-            pass_on(1, d).start()
-        from_mate(1).wait_recv()
-        from_mate(0).wait_recv()
-        attend(mx, 1 - core)
+            lax.fori_loop(low, high, one, 0)
+
+        attend(mx, core, 0, heads)
+
+        def hand_on(t, d):
+            from_peer(t, d).wait_recv()
+            pass_on(t, d).start()
+
+        each_peer(lambda d: hand_on(2, d))
+        for t in range(3):
+            from_mate(t).wait_recv()
+        attend(mx, 1 - core, 0, heads)
         tokt[...] = jnp.transpose(tok[...])
-        for d in range(1, nx):
-            from_peer(0, d).wait_recv()
-            pass_on(0, d).start()
-            attend(lax.rem(mx + nx - d, nx), core)
-        for d in range(1, nx):
-            passed(1, d).wait_recv()
-            passed(0, d).wait_recv()
-            attend(lax.rem(mx + nx - d, nx), 1 - core)
+
+        def half_heads(t, carry):
+            low, high = t * heads // 2, (t + 1) * heads // 2
+
+            def near(d):
+                for v in range(2):
+
+                    @pl.when(t == v)
+                    def _():
+                        hand_on(v, d)
+
+                attend(lax.rem(mx + nx - d, nx), core, low, high)
+
+            def far(d):
+                @pl.when(t == 0)
+                def _():
+                    passed(2, d).wait_recv()
+                    passed(0, d).wait_recv()
+
+                @pl.when(t == 1)
+                def _():
+                    passed(1, d).wait_recv()
+
+                attend(lax.rem(mx + nx - d, nx), 1 - core, low, high)
+
+            each_peer(near)
+            each_peer(far)
+            return carry
+
+        lax.fori_loop(0, 2, half_heads, 0)
 
         lane = lax.broadcasted_iota(jnp.int32, (rows, lanes), 1)
         logs = jnp.zeros((rows, lanes), f32)
@@ -963,11 +1007,14 @@
             copy.start()
         for copy in outs:
             copy.wait()
-        for b in range(2):
-            to_mate(b).wait_send()
-            for d in range(1, nx):
-                to_peer(b, d).wait_send()
-                pass_on(b, d).wait_send()
+        for t in range(3):
+            to_mate(t).wait_send()
+
+            def sent(d):
+                to_peer(t, d).wait_send()
+                pass_on(t, d).wait_send()
+
+            each_peer(sent)
 
     sem = pltpu.SemaphoreType.DMA
     hbm = pl.BlockSpec(memory_space=pl.ANY)
@@ -991,8 +1038,8 @@
             pltpu.VMEM((heads, rows, 1), f32), pltpu.VMEM((heads, rows, 1), f32),
             pltpu.VMEM((rows, local), f32), pltpu.VMEM((rows, local), bf16),
             sem((4,)), sem((7,)),
-            sem((2, nx - 1)), sem((2, nx - 1)), sem((2,)), sem((2,)),
-            sem((2, nx - 1)), sem((2, nx - 1)),
+            sem((3, nx - 1)), sem((3, nx - 1)), sem((3,)), sem((3,)),
+            sem((3, nx - 1)), sem((3, nx - 1)),
         ] + small.scratch(),
         compiler_params=pltpu.CompilerParams(
             collective_id=cid, has_side_effects=True, vmem_limit_bytes=62 * 2**20
@@ -1043,7 +1090,7 @@
 
     def body(
         attn_hbm, tok_hbm, again_ref, wo_hbm, wg_hbm, wu_hbm, wd_hbm,
-        proj_out, hidt_out, gate_out, up_out, inner_out, down_out,
+        proj_out, hidt_out, gate_out, up_out, inner_out, down_out, inv_out,
         attn_v, tok, wo, hid, hidt, gate, up, inner, wg, wu, wd, first, loads, stores, *rest,
     ):
         line.bind(rest[:n_line])
@@ -1085,6 +1132,7 @@
                 outs = [line.res[j, rs].astype(f32) for j in range(n_tp)]
                 square = sum(jnp.sum(out * out, axis=1, keepdims=True) for out in outs)
                 inv = lax.rsqrt(square * (1.0 / width) + norm_eps)
+                inv_out[rs, :] = inv
                 for j, out in enumerate(outs):
                     cols = slice(j * part, (j + 1) * part)
                     hid[rs, cols] = (
@@ -1106,8 +1154,8 @@
                 gate[sl, cols] = g.astype(bf16)
                 up[sl, cols] = u.astype(bf16)
                 inner[sl, cols] = (g * jax.nn.sigmoid(g) * u).astype(bf16)
-                for v in range(j * row_chains // n_cut, (j + 1) * row_chains // n_cut):
-                    line.piece(((c + 2) * n_tp - 1) * row_chains + v)
+                low, high = j * row_chains // n_cut, (j + 1) * row_chains // n_cut
+                line.pieces(((c + 2) * n_tp - 1) * row_chains + low, high - low)
             for j in range(n_tp):
 
                 @pl.when(c == 0)
@@ -1134,8 +1182,8 @@
     return kernel_call(
         body, [attn, tokens, attn_gain, w_output, w_gate, w_up, w_down], "hhvhhhh",
         [((rows, width), bf16), ((width, rows), bf16), ((rows, wide), bf16), ((rows, wide), bf16),
-         ((rows, wide), bf16), ((rows, width), bf16)],
-        "hhhhhh",
+         ((rows, wide), bf16), ((rows, width), bf16), ((rows, 1), f32)],
+        "hhhhhhv",
         [
             pltpu.VMEM((rows, local), bf16), pltpu.VMEM((rows, width), bf16),
             pltpu.VMEM((local, width), bf16),
@@ -1162,11 +1210,11 @@
     n_cut = wide // cut
     part = line.part
     lead = row_chains * n_tp // (n_cut + n_tp)
-    ticks = 3
+    ticks = n_cut // 2 + n_tp // 2
 
     def body(
-        down_ref, grad_ref, mgain_ref, gate_hbm, up_hbm, inner_hbm, hidt_hbm, wg_hbm, wu_hbm, wd_hbm,
-        back_out, dgate_out, dup_out, dgain_out, *rest,
+        down_hbm, grad_hbm, mgain_ref, gate_hbm, up_hbm, inner_hbm, hidt_hbm, wg_hbm, wu_hbm, wd_hbm,
+        back_out, dgate_out, dup_out, dgain_out, inv_out, *rest,
     ):
         grad_outs, rest = rest[:n_out], rest[n_out:]
         (gate_v, up_v, inner_v, hidt, ddown, ddownt, dgate, dup, ring, loads, wsem, stores) = rest[:12]
@@ -1181,12 +1229,16 @@
 
         for j in range(4):
             fetch(rows_of(wd_hbm, j, cut), j).start()
+        down_ref, grad_ref = dgate.at[:, pl.ds(0, width)], dup.at[:, pl.ds(0, width)]
+        first = load_list([(down_hbm, down_ref), (grad_hbm, grad_ref)], loads, 4)
         early = load_list(
             [(inner_hbm, inner_v), (gate_hbm, gate_v), (up_hbm, up_v), (hidt_hbm, hidt)], loads
         )
         bar = pltpu.get_barrier_semaphore()
         peers = line.greet(bar) + grads.greet(bar)
         dgain_out[...] = jnp.zeros_like(dgain_out)
+        for copy in first:
+            copy.wait()
 
         def norm_rows(t, carry):
             sl = pl.ds(pl.multiple_of(t * tile, tile), tile)
@@ -1194,6 +1246,7 @@
             upstream = grad_ref[sl].astype(f32)
             inv = lax.rsqrt(jnp.mean(out * out, axis=1, keepdims=True) + norm_eps)
             norm = out * inv
+            inv_out[sl, :] = inv
             dgain_out[...] += jnp.sum(upstream * norm, axis=0, keepdims=True)
             dnorm = upstream * mgain_ref[...]
             dot = jnp.mean(dnorm * norm, axis=1, keepdims=True)
@@ -1211,14 +1264,14 @@
         def row_half(c, carry):
             sl = pl.ds(pl.multiple_of(c * half, half), half)
 
-            def beside(i, t):
+            def beside(i, j, first):
                 @pl.when(c == 1)
                 def _():
-                    for v in range(lead):
-                        line.piece(i * lead + v)
-
-                if t is not None:
-                    grads.tick(t)
+                    line.pieces(i * lead, lead)
+
+                @pl.when(lax.rem(j, 2) == 1)
+                def _():
+                    grads.tick(first + j // 2)
 
             def inner_back(j, carry):
                 fetch(rows_of(wd_hbm, j, cut), j).wait()
@@ -1237,11 +1290,10 @@
                 def _():
                     fetch(rows_of(wu_hbm, j // 2, part), j).start()
 
-                beside(j, None)
+                beside(j, j, c * ticks)
                 return carry
 
             lax.fori_loop(0, n_cut, inner_back, 0)
-            grads.tick(c * ticks)
 
             def hidden_back(j, carry):
                 slot = lax.rem(2 * j, 4)
@@ -1261,12 +1313,7 @@
                     fetch(rows_of(wd_hbm, slot, cut), slot).start()
                     fetch(rows_of(wd_hbm, slot + 1, cut), slot + 1).start()
 
-                beside(n_cut + j, None)
-
-                @pl.when((lax.rem(j, 2) == 1) & (c * ticks + 1 + j // 2 < (c + 1) * ticks))
-                def _():
-                    grads.tick(c * ticks + 1 + j // 2)
-
+                beside(n_cut + j, j, c * ticks + n_cut // 2)
                 return carry
 
             lax.fori_loop(0, n_tp, hidden_back, 0)
@@ -1277,8 +1324,7 @@
         done, used = 2 * ticks, (n_cut + n_tp) * lead
 
         def one(it, carry):
-            for v in range(pace):
-                line.piece(used + (it - done) * pace + v)
+            line.pieces(used + (it - done) * pace, pace)
             grads.tick(it)
             return carry
 
@@ -1292,17 +1338,18 @@
 
     sem = pltpu.SemaphoreType.DMA
     return kernel_call(
-        body, [down, grad, mlp_gain, gate, up, inner, hid_t, w_gate, w_up, w_down], "vvvhhhhhhh",
-        [((rows, width), bf16), ((rows, wide), bf16), ((rows, wide), bf16), ((1, width), f32)]
-        + [((grads.rows, w), f32) for w in widths],
-        "hhhv" + "v" * n_out,
+        body, [down, grad, mlp_gain, gate, up, inner, hid_t, w_gate, w_up, w_down], "hhvhhhhhhh",
+        [((rows, width), bf16), ((rows, wide), bf16), ((rows, wide), bf16), ((1, width), f32),
+         ((rows, 1), f32)]
+        + grads.out_shapes(widths),
+        "hhhvv" + "v" * n_out,
         [
             pltpu.VMEM((rows, wide), bf16), pltpu.VMEM((rows, wide), bf16),
             pltpu.VMEM((rows, wide), bf16), pltpu.VMEM((width, rows), bf16),
             pltpu.VMEM((rows, width), bf16), pltpu.VMEM((width, rows), bf16),
             pltpu.VMEM((rows, wide), bf16), pltpu.VMEM((rows, wide), bf16),
             pltpu.VMEM((4, cut, width), bf16),
-            sem((4,)), sem((4,)), sem((2 + n_tp,)),
+            sem((6,)), sem((4,)), sem((2 + n_tp,)),
         ] + line.scratch() + grads.scratch(),
         cid, "mlp_back",
     )
@@ -1315,7 +1362,7 @@
     n_tp = lax.axis_size("tp")
     line = LineSum(n_tp, rows, width)
     grads = GradScatter(n_ctx, n_seq, width, jobs)
-    small = GainSum(n_ctx, n_seq)
+    small = GainSum(n_ctx, n_seq, gains.shape[0])
     na, nb, n_out = len(ats), len(bs), len(widths)
     n_line, n_grads = len(line.scratch()), len(grads.scratch())
     part = line.part
@@ -1352,8 +1399,7 @@
 
         def one(it, carry):
             grads.tick(it)
-            for v in range(pace):
-                line.piece((it - done) * pace + v)
+            line.pieces((it - done) * pace, pace)
             return carry
 
         line_steps = -(-line.steps * row_chains // pace)
@@ -1369,7 +1415,7 @@
     return kernel_call(
         body, [dqkv, w_query, w_key, w_value] + list(ats) + list(bs) + [gains],
         "vvvv" + "v" * (na + nb + 1),
-        [((rows, width), bf16)] + [((grads.rows, w), f32) for w in widths] + [((8, lanes), f32)],
+        [((rows, width), bf16)] + grads.out_shapes(widths) + [(gains.shape, f32)],
         "h" + "v" * (n_out + 1),
         [sem((n_tp,))] + line.scratch() + grads.scratch() + small.scratch(),
         cid, "last_sums",
@@ -1407,70 +1453,59 @@
     (query_rot, keys, values, query_norm, key_norm, attn, tokens_t, scales, lse) = front(
         inputs, w_query, w_key, w_value, qgain, kgain, angle_cos, angle_sin, group_order, 1
     )
-    proj, hidden_t, gate, up, inner, down = middle(
+    proj, hidden_t, gate, up, inner, down, proj_scale = middle(
         attn, inputs, attn_gain[None], w_output, w_gate, w_up, w_down, 2
     )
     chunk_cols = 2 * lanes
     chunks = wide // chunk_cols
     thin = local // chunk_cols
-    n_first = chunks * 5 // 8 if keys.shape[0] <= 8 * rows else chunks
-    n_mid = chunks * 5 // 8 if keys.shape[0] <= 8 * rows else 0
-    back, d_gate, d_up, d_mlp_gain, grad_down, grad_gate = mlp_back(
+    back, d_gate, d_up, d_mlp_gain, down_scale, grad_down, grad_gate = mlp_back(
         down, upstream, mlp_gain[None], gate, up, inner, hidden_t, w_gate, w_up, w_down,
         [
-            dict(a=0, b=0, first=0, count=chunks, out=0, place=0),
-            dict(a=1, b=1, first=0, count=n_first, out=1, place=0),
+            dict(a=0, b=0, first=0, count=chunks, out=0, place=0, flip=True),
+            dict(a=1, b=1, first=0, count=chunks, out=1, place=0, flip=False),
         ],
-        [wide, n_first * chunk_cols],
+        [wide, wide],
         3,
     )
-    mid_jobs, mid_widths = [], []
-    if n_mid:
-        mid_jobs = [
-            dict(a=0, b=0, first=n_first, count=chunks - n_first, out=0, place=0),
-            dict(a=0, b=1, first=0, count=n_mid, out=1, place=0),
-        ]
-        mid_widths = [(chunks - n_first) * chunk_cols, n_mid * chunk_cols]
-    d_qkv, d_proj_t, d_attn_gain, d_query_gain, d_key_gain, *mid = attention_back(
+    d_qkv, d_proj_t, d_attn_gain, d_query_gain, d_key_gain = attention_back(
         back, upstream, proj, attn_gain[None], w_output, query_rot, keys, values, attn, lse,
         positions[None], group_order, query_norm, key_norm, scales, qgain, kgain, angle_cos,
-        angle_sin, [hidden_t] if n_mid else [], [d_gate, d_up] if n_mid else [], mid_jobs,
-        mid_widths, 4,
+        angle_sin, [], [], [], [], 4,
     )
     owners = lax.axis_size("ctx") * lax.axis_size("seq")
-    pieces = [
-        d_attn_gain.reshape(owners, -1),
-        d_mlp_gain.reshape(owners, -1),
-        d_query_gain.reshape(heads, owners, -1).transpose(1, 0, 2).reshape(owners, -1),
-        d_key_gain.reshape(heads, owners, -1).transpose(1, 0, 2).reshape(owners, -1),
-    ]
-    cuts = [piece.shape[1] for piece in pieces]
-    packed = jnp.concatenate(pieces, axis=1)
-    packed = jnp.pad(packed, ((0, 0), (0, 8 * lanes - packed.shape[1]))).reshape(owners, 8, lanes)
+    gains = [d_attn_gain, d_mlp_gain, d_query_gain, d_key_gain]
+    ends = [gain.shape[1] for gain in gains]
+    ends = [sum(ends[: i + 1]) for i in range(4)]
+    packed = jnp.concatenate(gains, axis=1).reshape(-1, lanes)
     last, grad_up, grad_qkv, grad_output, small = last_sums(
         d_qkv, w_query, w_key, w_value,
         [hidden_t, tokens_t, d_proj_t],
         [d_up, attn],
         [
-            dict(a=0, b=0, first=n_mid, count=chunks - n_mid, out=0, place=0),
-            dict(a=2, b=1, first=0, count=thin, out=2, place=0),
-            dict(a=1, b=2, first=0, count=3 * thin, out=1, place=0),
+            dict(a=0, b=0, first=0, count=chunks, out=0, place=0, flip=False),
+            dict(a=2, b=1, first=0, count=thin, out=2, place=0, flip=True),
+            dict(a=1, b=2, first=0, count=3 * thin, out=1, place=0, flip=False),
         ],
-        [(chunks - n_mid) * chunk_cols, 3 * local, local],
+        [wide, 3 * local, local],
         packed,
         5,
     )
-    if n_mid:
-        grad_gate = jnp.concatenate([grad_gate, mid[0]], axis=1)
-        grad_up = jnp.concatenate([mid[1], grad_up], axis=1)
     small = small.reshape(-1)
-    g_attn, g_mlp, g_query, g_key = jnp.split(
-        small[: sum(cuts)], [cuts[0], cuts[0] + cuts[1], cuts[0] + cuts[1] + cuts[2]]
-    )
+    me = lax.axis_index("ctx") * lax.axis_size("seq") + lax.axis_index("seq")
+
+    def my_part(start, end, lead):
+        whole = small[start:end].reshape(lead, -1)
+        size = whole.shape[1] // owners
+        return lax.dynamic_slice_in_dim(whole, me * size, size, 1)
+
+    g_attn = my_part(0, ends[0], 1)[0]
+    g_mlp = my_part(ends[0], ends[1], 1)[0]
+    g_query = my_part(ends[1], ends[2], heads)
+    g_key = my_part(ends[2], ends[3], heads)
     grad_query, grad_key, grad_value = jnp.split(grad_qkv, 3, axis=1)
-    proj, down = proj.astype(f32), down.astype(f32)
-    attn_norm = proj * lax.rsqrt(jnp.mean(proj * proj, axis=1) + norm_eps)[:, None]
-    mlp_norm = down * lax.rsqrt(jnp.mean(down * down, axis=1) + norm_eps)[:, None]
+    attn_norm = proj.astype(f32) * proj_scale
+    mlp_norm = down.astype(f32) * down_scale
     block_out = inputs.astype(f32) + attn_norm * attn_gain + mlp_norm * mlp_gain
     input_grad = upstream.astype(f32) + back.astype(f32) + last.astype(f32)
     return (
@@ -1479,13 +1514,13 @@
         grad_query,
         grad_key,
         grad_value,
-        g_query.reshape(heads, -1),
-        g_key.reshape(heads, -1),
-        grad_output.T,
+        g_query,
+        g_key,
+        grad_output,
         g_attn,
         grad_gate,
         grad_up,
-        grad_down.T,
+        grad_down,
         g_mlp,
     )
 

time: 461 us -> 437 us (0.948)
  Pallas kernels: 421 us -> 399 us
    pallas_call x1, Pallas kernels: 83.9 us -> 52.3 us  [comm_call(): pl.pallas_call(body, out_shape=outs, in_specs=[pl.BlockSpec(memory_space=...]
    pallas_call x3, Pallas kernels: 293 us -> 305 us  [kernel_call(): pl.pallas_call(body, out_shape=[jax.ShapeDtypeStruct(*out) for out in out...]
where the time goes in v7:
time: 437 us; the launch traced here: 429 us
  Pallas kernels  399 us (91%)
  other arithmetic  17.6 us (4%)
  local copies, waits for them, and re-layouts  10.6 us (2%)
    pallas_call x3, Pallas kernels, kernel_call(): pl.pallas_call(body, out_shape=[jax.ShapeDtypeStruct(*out) for out in out...  305 us
    pallas_call x1, Pallas kernels, comm_call(): pl.pallas_call(body, out_shape=outs, in_specs=[pl.BlockSpec(memory_space=...  52.3 us
    pallas_call x1, Pallas kernels, front(): pl.pallas_call(body, out_shape=[block((rows, local), bf16), block((count,...  41.5 us

profile of v7, /device:TPU:0, one launch (start us, length us, event | category | flops | bytes accessed | tf_op | source)
XLA Modules:
  0.0 428.7 jit_solution(9041352047872312243)
XLA Ops:
  0.7 0.7 select_reduce_fusion
  1.4 0.6 fusion.1.prow_ref
  2.0 1.0 fusion
  3.0 1.0 pad_maximum_fusion
  4.0 41.5 %front.1 = (bf16[512,512]{1,0:T(8,128)(2,1)}, bf16[2048,512]{1,0:T(8,128)(2,1)}, bf16[2048,512]{1,0:T(8,128)(2,1)}, f32[512,512]{1,0:T(8,128)}, f32[512,512]{1,0...) custom-call(bf16[512,2048]{1,0:T(8,128)(2,1)} %bitcast.21, ...), custom_call_target="tpu_custom_call" | custom-call | tf_op jit(solution)/shard_map/front/pallas_call | solution.py:1022
  45.6 119.1 %middle.1 = (bf16[512,2048]{1,0:T(8,128)(2,1)}, bf16[2048,512]{1,0:T(8,128)(2,1)}, bf16[512,2048]{1,0:T(8,128)(2,1)}, bf16[512,2048]{1,0:T(8,128)(2,1)}, bf16[51...) custom-call(bf16[512,512]{1,0:T(8,128)(2,1)} %get-tuple-element.45.attn_hbm.attn_ref.refs_4_, ...), custom_call_target="tpu_custom_call" | custom-call | tf_op jit(solution)/shard_map/middle/pallas_call | solution.py:1066
  164.6 1.1 reduce
  165.7 97.6 %mlp_back.1 = (bf16[512,2048]{1,0:T(8,128)(2,1)}, bf16[512,2048]{1,0:T(8,128)(2,1)}, bf16[512,2048]{1,0:T(8,128)(2,1)}, f32[1,2048]{1,0:T(1,128)}, f32[512,1]{1,...) custom-call(bf16[512,2048]{1,0:T(8,128)(2,1)} %get-tuple-element.48.down_hbm, bf16[512,2048]{1,0:T(8,128)(2,1)} %bitcast.19, ...), custom_call_target="tpu_custom_call" | custom-call | tf_op jit(solution)/shard_map/mlp_back/pallas_call | solution.py:1066
  263.4 52.3 %attention_back.1 = (bf16[512,1536]{1,0:T(8,128)(2,1)}, bf16[2048,512]{1,0:T(8,128)(2,1)}, f32[1,2048]{1,0:T(1,128)}, f32[1,512]{1,0:T(1,128)}, f32[1,512]{1,0:T(1,128)}) custom-call(bf16[512,2048]{1,0:T(8,128)(2,1)} %get-tuple-element.54.back_ref, bf16[512,2048]{1,0:T(8,128)(2,1)} %bitcast.20, bf16[512,2048]{1,0:T(8,128)(2,1)} %get-tuple-element.46.proj_ref, ...), custom_call_target="tpu_custom_call" | custom-call | tf_op jit(solution)/shard_map/attention_back/pallas_call | solution.py:489
  316.0 6.2 %add_bitcast_fusion.1 = f32[1,512,2048]{2,1,0:T(8,128)} fusion(bf16[512,2048]{1,0:T(8,128)(2,1)} %get-tuple-element.48.down_hbm, bf16[512,2048]{1,0:T(8,128)(2,1)} %get-tuple-element.46.proj_ref, f32[2048]{0:T(1024)S(1)} %copy-done.7, f32[512]{0:T(512)S(1)} %reduce.1, f32[2048]{0:T(1024)S(1)} %copy-done.6, f32[512]{0:T(512)S(1)} %reduce, ...), kind=kLoop, calls=%fused_computation.1 | loop fusion | flops 9437184 | bytes 10506240 | tf_op jit(solution)/shard_map/broadcast_in_dim | solution.py:1512
  322.2 0.6 pad_maximum_fusion.2
  322.8 88.6 %last_sums.1 = (bf16[512,2048]{1,0:T(8,128)(2,1)}, f32[256,2048]{1,0:T(8,128)}, f32[256,1536]{1,0:T(8,128)}, f32[512,256]{1,0:T(8,128)}, f32[40,128]{1,0:T(8,128)}) custom-call(bf16[512,1536]{1,0:T(8,128)(2,1)} %get-tuple-element.62.dqkv_ref, bf16[2048,512]{1,0:T(8,128)(2,1)} %wq_ref.1, bf16[2048,512]{1,0:T(8,128)(2,1)} %wk_ref.1, bf16[2048,512]{1,0:T(8,128)(2,1)} %wv_ref.1, ...), custom_call_target="tpu_custom_call" | custom-call | tf_op jit(solution)/shard_map/last_sums/pallas_call | solution.py:1066
  411.4 6.2 %add_bitcast_fusion = f32[1,512,2048]{2,1,0:T(8,128)} fusion(bf16[512,2048]{1,0:T(8,128)(2,1)} %get-tuple-element.70, bf16[512,2048]{1,0:T(8,128)(2,1)} %get-tuple-element.54.back_ref, bf16[1,512,2048]{2,1,0:T(8,128)(2,1)} %param.15), kind=kLoop, calls=%fused_computation | loop fusion | flops 5242880 | bytes 10485760 | tf_op jit(solution)/shard_map/broadcast_in_dim | solution.py:1513
  417.6 0.6 constant_dynamic-slice_fusion.3
  418.2 0.6 constant_dynamic-slice_fusion
  418.8 0.6 constant_dynamic-slice_fusion.1
  419.4 0.6 constant_dynamic-slice_fusion.2
  420.1 1.2 fusion.8
  421.2 0.8 copy.31
  422.2 1.3 copy.32
  423.5 1.0 copy-done.2
  424.6 1.3 copy.33
  425.9 1.0 copy-done
  426.9 1.3 copy.34
  (30 shorter events, 0.4 us)
Async XLA Ops:
  263.4 52.4 %copy-start.5 = (f32[512,1]{1,0:T(8,128)S(1)}, f32[512,1]{1,0:T(8,128)}, u32[]{:S(2)}) copy-start(f32[512,1]{1,0:T(8,128)} %get-tuple-element.53) | copy-start | bytes 6148
  263.4 52.5 %copy-start.6 = (f32[2048]{0:T(1024)S(1)}, f32[2048]{0:T(1024)}, u32[]{:S(2)}) copy-start(f32[2048]{0:T(1024)} %param.23) | copy-start | bytes 24580
  263.4 52.5 %copy-start.7 = (f32[2048]{0:T(1024)S(1)}, f32[2048]{0:T(1024)}, u32[]{:S(2)}) copy-start(f32[2048]{0:T(1024)} %param.27) | copy-start | bytes 24580
  315.9 6.2 %copy-start.9 = (f32[1,2048]{1,0:T(1,128)S(1)}, f32[1,2048]{1,0:T(1,128)}, u32[]{:S(2)}) copy-start(f32[1,2048]{1,0:T(1,128)} %get-tuple-element.67) | copy-start | bytes 24580
  315.9 6.2 %copy-start.10 = (f32[1,2048]{1,0:T(1,128)S(1)}, f32[1,2048]{1,0:T(1,128)}, u32[]{:S(2)}) copy-start(f32[1,2048]{1,0:T(1,128)} %get-tuple-element.66) | copy-start | bytes 24580
  315.9 6.2 %copy-start.11 = (f32[1,512]{1,0:T(1,128)S(1)}, f32[1,512]{1,0:T(1,128)}, u32[]{:S(2)}) copy-start(f32[1,512]{1,0:T(1,128)} %get-tuple-element.68) | copy-start | bytes 6148
  315.9 6.2 %copy-start.12 = (f32[1,512]{1,0:T(1,128)S(1)}, f32[1,512]{1,0:T(1,128)}, u32[]{:S(2)}) copy-start(f32[1,512]{1,0:T(1,128)} %get-tuple-element.69) | copy-start | bytes 6148
  411.4 6.2 %copy-start.8 = (f32[40,128]{1,0:T(8,128)S(1)}, f32[40,128]{1,0:T(8,128)}, u32[]{:S(2)}) copy-start(f32[40,128]{1,0:T(8,128)} %get-tuple-element.72) | copy-start | bytes 61444
  411.4 8.7 %copy-start.3 = (f32[256,1536]{1,0:T(8,128)S(1)}, f32[256,1536]{1,0:T(8,128)}, u32[]{:S(2)}) copy-start(f32[256,1536]{1,0:T(8,128)} %get-tuple-element.71) | copy-start | bytes 4718596
  417.6 3.6 copy-start.4
  420.1 2.2 copy-start.1
  422.2 2.3 copy-start.2
  424.6 2.3 copy-start

commit v8 on v7

--- a/solution.py
+++ b/solution.py
@@ -12,9 +12,10 @@
 
 def rope_tables(positions, head_dim):
     half = head_dim // 2
-    rates = rope_base ** (-(jnp.arange(half, dtype=jnp.float32) * 2.0 / head_dim))
+    channel = jnp.arange(head_dim, dtype=jnp.int32)
+    rates = rope_base ** (-((channel % half).astype(jnp.float32) * 2.0 / head_dim))
     angle = positions.astype(jnp.float32)[:, None] * rates[None, :]
-    return (jnp.cos(angle), jnp.sin(angle))
+    return jnp.cos(angle), jnp.where(channel[None, :] < half, -jnp.sin(angle), jnp.sin(angle))
 
 
 def key_positions(order, first_row, count, group):
@@ -1422,6 +1423,29 @@
     )
 
 
+def row_tiles(body, args, out_shape, name):
+    rows, width = out_shape
+    tile = rows // 4
+
+    def spec(arg):
+        if arg.shape[0] == 1:
+            return pl.BlockSpec((1, arg.shape[1]), lambda i: (0, 0))
+        return pl.BlockSpec((tile, arg.shape[1]), lambda i: (i, 0))
+
+    def whole(*refs):
+        refs[-1][...] = body(*[ref[...].astype(f32) for ref in refs[:-1]])
+
+    return pl.pallas_call(
+        whole,
+        grid=(4,),
+        out_shape=jax.ShapeDtypeStruct(out_shape, f32),
+        in_specs=[spec(arg) for arg in args],
+        out_specs=pl.BlockSpec((tile, width), lambda i: (i, 0)),
+        compiler_params=pltpu.CompilerParams(vmem_limit_bytes=32 * 2**20),
+        name=name,
+    )(*args)
+
+
 def per_device(
     tokens,
     out_grad,
@@ -1445,9 +1469,7 @@
     local = heads * head_dim
     wide = w_gate.shape[1]
     positions = key_positions(group_order[0], lax.axis_index("ctx") * rows, rows, rows // 2)
-    cosine, sine = rope_tables(positions, head_dim)
-    angle_cos = jnp.concatenate([cosine, cosine], axis=1)
-    angle_sin = jnp.concatenate([-sine, sine], axis=1)
+    angle_cos, angle_sin = rope_tables(positions, head_dim)
     qgain = query_gain.reshape(1, local)
     kgain = key_gain.reshape(1, local)
     (query_rot, keys, values, query_norm, key_norm, attn, tokens_t, scales, lse) = front(
@@ -1504,10 +1526,14 @@
     g_query = my_part(ends[1], ends[2], heads)
     g_key = my_part(ends[2], ends[3], heads)
     grad_query, grad_key, grad_value = jnp.split(grad_qkv, 3, axis=1)
-    attn_norm = proj.astype(f32) * proj_scale
-    mlp_norm = down.astype(f32) * down_scale
-    block_out = inputs.astype(f32) + attn_norm * attn_gain + mlp_norm * mlp_gain
-    input_grad = upstream.astype(f32) + back.astype(f32) + last.astype(f32)
+    block_out = row_tiles(
+        lambda x, a, ra, ga, d, rd, gd: x + (a * ra) * ga + (d * rd) * gd,
+        [inputs, proj, proj_scale, attn_gain[None], down, down_scale, mlp_gain[None]],
+        inputs.shape, "block_out",
+    )
+    input_grad = row_tiles(
+        lambda g, a, b: g + a + b, [upstream, back, last], inputs.shape, "input_grad"
+    )
     return (
         block_out[None],
         input_grad[None],

time: 437 us -> 437 us (level)
  other arithmetic: 17.6 us -> 3.8 us
  local copies, waits for them, and re-layouts: 10.6 us -> 19 us
  Pallas kernels: 399 us -> 405 us
    broadcast_in_dim x2 -> x0, other arithmetic: 12.4 us -> none  [the longest x1 6.2 us: per_device(): block_out[None]]
    unnamed x30 -> x44, local copies, waits for them, and re-layouts: 7.04 us -> 16.6 us
    pallas_call x0 -> x2, Pallas kernels: none -> 5.83 us  [row_tiles(): pl.pallas_call(whole, grid=(4,), out_shape=jax.ShapeDtypeStruct(out_shape...]
where the time goes in v8:
time: 437 us; the launch traced here: 429 us
  Pallas kernels  405 us (93%)
  local copies, waits for them, and re-layouts  19 us (4%)
    pallas_call x3, Pallas kernels, kernel_call(): pl.pallas_call(body, out_shape=[jax.ShapeDtypeStruct(*out) for out in out...  305 us
    pallas_call x1, Pallas kernels, comm_call(): pl.pallas_call(body, out_shape=outs, in_specs=[pl.BlockSpec(memory_space=...  52.4 us
    pallas_call x1, Pallas kernels, front(): pl.pallas_call(body, out_shape=[block((rows, local), bf16), block((count,...  41.5 us
    unnamed x44, local copies, waits for them, and re-layouts  16.6 us

profile of v8, /device:TPU:0, one launch (start us, length us, event | category | flops | bytes accessed | tf_op | source)
XLA Modules:
  0.0 429.1 jit_solution(5442212801013111681)
XLA Ops:
  0.7 0.7 select_reduce_fusion
  2.0 1.8 negate_select_fusion
  3.9 41.5 %front.1 = (bf16[512,512]{1,0:T(8,128)(2,1)}, bf16[2048,512]{1,0:T(8,128)(2,1)}, bf16[2048,512]{1,0:T(8,128)(2,1)}, f32[512,512]{1,0:T(8,128)}, f32[512,512]{1,0...) custom-call(bf16[512,2048]{1,0:T(8,128)(2,1)} %bitcast.18, ...), custom_call_target="tpu_custom_call" | custom-call | tf_op jit(solution)/shard_map/front/pallas_call | solution.py:1023
  45.4 119.2 %middle.1 = (bf16[512,2048]{1,0:T(8,128)(2,1)}, bf16[2048,512]{1,0:T(8,128)(2,1)}, bf16[512,2048]{1,0:T(8,128)(2,1)}, bf16[512,2048]{1,0:T(8,128)(2,1)}, bf16[51...) custom-call(bf16[512,512]{1,0:T(8,128)(2,1)} %get-tuple-element.45.attn_hbm.attn_ref.refs_4_, ...), custom_call_target="tpu_custom_call" | custom-call | tf_op jit(solution)/shard_map/middle/pallas_call | solution.py:1067
  164.6 97.6 %mlp_back.1 = (bf16[512,2048]{1,0:T(8,128)(2,1)}, bf16[512,2048]{1,0:T(8,128)(2,1)}, bf16[512,2048]{1,0:T(8,128)(2,1)}, f32[1,2048]{1,0:T(1,128)}, f32[512,1]{1,...) custom-call(bf16[512,2048]{1,0:T(8,128)(2,1)} %get-tuple-element.48.down_hbm.refs_4_, bf16[512,2048]{1,0:T(8,128)(2,1)} %bitcast.15, ...), custom_call_target="tpu_custom_call" | custom-call | tf_op jit(solution)/shard_map/mlp_back/pallas_call | solution.py:1067
  262.2 52.4 %attention_back.1 = (bf16[512,1536]{1,0:T(8,128)(2,1)}, bf16[2048,512]{1,0:T(8,128)(2,1)}, f32[1,2048]{1,0:T(1,128)}, f32[1,512]{1,0:T(1,128)}, f32[1,512]{1,0:T(1,128)}) custom-call(bf16[512,2048]{1,0:T(8,128)(2,1)} %get-tuple-element.54.back_ref.refs_1_, bf16[512,2048]{1,0:T(8,128)(2,1)} %bitcast.16, bf16[512,2048]{1,0:T(8,128)(2,1)} %get-tuple-element.46.refs_1_.proj_ref, ...), custom_call_target="tpu_custom_call" | custom-call | tf_op jit(solution)/shard_map/attention_back/pallas_call | solution.py:490
  314.7 1.6 copy-done.1
  316.3 1.6 copy-done.3
  317.9 1.6 copy-done.4
  319.5 3.2 block_out.1
  322.7 0.6 pad_maximum_fusion
  323.3 88.5 %last_sums.1 = (bf16[512,2048]{1,0:T(8,128)(2,1)}, f32[256,2048]{1,0:T(8,128)}, f32[256,1536]{1,0:T(8,128)}, f32[512,256]{1,0:T(8,128)}, f32[40,128]{1,0:T(8,128)}) custom-call(bf16[512,1536]{1,0:T(8,128)(2,1)} %get-tuple-element.62.dqkv_ref, bf16[2048,512]{1,0:T(8,128)(2,1)} %wq_ref.1, bf16[2048,512]{1,0:T(8,128)(2,1)} %wk_ref.1, bf16[2048,512]{1,0:T(8,128)(2,1)} %wv_ref.1, ...), custom_call_target="tpu_custom_call" | custom-call | tf_op jit(solution)/shard_map/last_sums/pallas_call | solution.py:1067
  411.9 1.6 copy-done
  413.5 1.6 copy-done.2
  415.1 1.6 copy-done.5
  416.6 2.6 input_grad.1
  419.9 0.7 constant_dynamic-slice_fusion.1
  420.5 1.2 fusion.11
  421.7 0.8 copy.31
  422.7 1.3 copy.32
  424.0 1.0 copy-done.12
  425.0 1.3 copy.33
  426.4 1.0 copy-done.10
  427.4 1.3 copy.34
  (40 shorter events, 1.5 us)
Async XLA Ops:
  262.2 52.4 %copy-start.6 = (f32[512,1]{1,0:T(8,128)S(1)}, f32[512,1]{1,0:T(8,128)}, u32[]{:S(2)}) copy-start(f32[512,1]{1,0:T(8,128)} %get-tuple-element.47.refs_2_) | copy-start | bytes 6148
  262.2 52.4 %copy-start.7 = (f32[512,1]{1,0:T(8,128)S(1)}, f32[512,1]{1,0:T(8,128)}, u32[]{:S(2)}) copy-start(f32[512,1]{1,0:T(8,128)} %get-tuple-element.53.refs_5_) | copy-start | bytes 6148
  262.2 52.4 %copy-start.8 = (f32[2048]{0:T(1024)S(1)}, f32[2048]{0:T(1024)}, u32[]{:S(2)}) copy-start(f32[2048]{0:T(1024)} %param.23) | copy-start | bytes 24580
  262.2 52.4 %copy-start.9 = (f32[2048]{0:T(1024)S(1)}, f32[2048]{0:T(1024)}, u32[]{:S(2)}) copy-start(f32[2048]{0:T(1024)} %param.27) | copy-start | bytes 24580
  314.7 1.6 copy-start.1
  316.3 1.6 copy-start.3
  317.9 1.6 copy-start.4
  319.4 3.2 copy-start.16
  319.5 3.2 copy-start.17
  319.5 3.2 copy-start.18
  319.5 3.2 copy-start.19
  411.9 1.6 copy-start
  413.5 1.6 copy-start.2
  415.0 1.6 copy-start.5
  416.6 2.6 copy-start.15
  416.6 3.9 copy-start.13
  419.3 2.4 copy-start.14
  420.5 2.2 copy-start.11
  422.7 2.3 copy-start.12
  425.0 2.3 copy-start.10

commit v9 on v8

--- a/solution.py
+++ b/solution.py
@@ -1423,27 +1423,42 @@
     )
 
 
-def row_tiles(body, args, out_shape, name):
-    rows, width = out_shape
-    tile = rows // 4
-
-    def spec(arg):
-        if arg.shape[0] == 1:
-            return pl.BlockSpec((1, arg.shape[1]), lambda i: (0, 0))
-        return pl.BlockSpec((tile, arg.shape[1]), lambda i: (i, 0))
+def row_tiles(body, args, outs, name):
+    count = 4
+
+    def spec(shape):
+        if shape[0] == 1:
+            return pl.BlockSpec(shape, lambda i: (0, 0))
+        return pl.BlockSpec((shape[0] // count, shape[1]), lambda i: (i, 0))
 
     def whole(*refs):
-        refs[-1][...] = body(*[ref[...].astype(f32) for ref in refs[:-1]])
+        body(refs[: len(args)], refs[len(args) :])
 
     return pl.pallas_call(
         whole,
-        grid=(4,),
-        out_shape=jax.ShapeDtypeStruct(out_shape, f32),
-        in_specs=[spec(arg) for arg in args],
-        out_specs=pl.BlockSpec((tile, width), lambda i: (i, 0)),
-        compiler_params=pltpu.CompilerParams(vmem_limit_bytes=32 * 2**20),
+        grid=(count,),
+        out_shape=[jax.ShapeDtypeStruct(shape, f32) for shape in outs],
+        in_specs=[spec(arg.shape) for arg in args],
+        out_specs=[spec(shape) for shape in outs],
+        compiler_params=pltpu.CompilerParams(vmem_limit_bytes=62 * 2**20),
         name=name,
     )(*args)
+
+
+def block_tile(ins, outs):
+    x, a, ra, ga, d, rd, gd = [ref[...].astype(f32) for ref in ins[:7]]
+    outs[0][...] = x + (a * ra) * ga + (d * rd) * gd
+    for src, dst in zip(ins[7:], outs[1:]):
+        dst[...] = src[...]
+
+
+def input_tile(ins, outs):
+    outs[0][...] = ins[0][...].astype(f32) + ins[1][...].astype(f32) + ins[2][...].astype(f32)
+    outs[1][...] = ins[3][...]
+    outs[2][...] = ins[4][...]
+    size = outs[3].shape[1]
+    for i in range(3):
+        outs[3 + i][...] = ins[5][:, i * size : (i + 1) * size]
 
 
 def per_device(
@@ -1525,14 +1540,16 @@
     g_mlp = my_part(ends[0], ends[1], 1)[0]
     g_query = my_part(ends[1], ends[2], heads)
     g_key = my_part(ends[2], ends[3], heads)
-    grad_query, grad_key, grad_value = jnp.split(grad_qkv, 3, axis=1)
-    block_out = row_tiles(
-        lambda x, a, ra, ga, d, rd, gd: x + (a * ra) * ga + (d * rd) * gd,
-        [inputs, proj, proj_scale, attn_gain[None], down, down_scale, mlp_gain[None]],
-        inputs.shape, "block_out",
+    block_out, grad_down, grad_gate = row_tiles(
+        block_tile,
+        [inputs, proj, proj_scale, attn_gain[None], down, down_scale, mlp_gain[None], grad_down,
+         grad_gate],
+        [inputs.shape, grad_down.shape, grad_gate.shape], "block_out",
     )
-    input_grad = row_tiles(
-        lambda g, a, b: g + a + b, [upstream, back, last], inputs.shape, "input_grad"
+    own = grad_qkv.shape[0]
+    input_grad, grad_up, grad_output, grad_query, grad_key, grad_value = row_tiles(
+        input_tile, [upstream, back, last, grad_up, grad_output, grad_qkv],
+        [inputs.shape, grad_up.shape, grad_output.shape] + [(own, local)] * 3, "input_grad",
     )
     return (
         block_out[None],

time: 437 us -> 429 us (0.982)
  local copies, waits for them, and re-layouts: 19 us -> 1.26 us
  Pallas kernels: 405 us -> 415 us
    unnamed x44 -> x10, local copies, waits for them, and re-layouts: 16.6 us -> 0.02 us
    pallas_call x2, Pallas kernels: 5.83 us -> 15.8 us  [row_tiles(): pl.pallas_call(whole, grid=(count,), out_shape=[jax.ShapeDtypeStruct(shap...]
where the time goes in v9:
time: 429 us; the launch traced here: 421 us
  Pallas kernels  415 us (97%)
    pallas_call x3, Pallas kernels, kernel_call(): pl.pallas_call(body, out_shape=[jax.ShapeDtypeStruct(*out) for out in out...  305 us
    pallas_call x1, Pallas kernels, comm_call(): pl.pallas_call(body, out_shape=outs, in_specs=[pl.BlockSpec(memory_space=...  52.4 us
    pallas_call x1, Pallas kernels, front(): pl.pallas_call(body, out_shape=[block((rows, local), bf16), block((count,...  41.6 us
    pallas_call x2, Pallas kernels, row_tiles(): pl.pallas_call(whole, grid=(count,), out_shape=[jax.ShapeDtypeStruct(shap...  15.8 us

profile of v9, /device:TPU:0, one launch (start us, length us, event | category | flops | bytes accessed | tf_op | source)
XLA Modules:
  0.0 421.3 jit_solution(15052971252819875852)
XLA Ops:
  0.7 0.7 select_reduce_fusion
  1.5 0.6 fusion.prow_ref
  2.0 1.8 negate_select_fusion
  3.9 41.6 %front.1 = (bf16[512,512]{1,0:T(8,128)(2,1)}, bf16[2048,512]{1,0:T(8,128)(2,1)}, bf16[2048,512]{1,0:T(8,128)(2,1)}, f32[512,512]{1,0:T(8,128)}, f32[512,512]{1,0...) custom-call(bf16[512,2048]{1,0:T(8,128)(2,1)} %bitcast.18, ...), custom_call_target="tpu_custom_call" | custom-call | tf_op jit(solution)/shard_map/front/pallas_call | solution.py:1023
  45.4 119.1 %middle.1 = (bf16[512,2048]{1,0:T(8,128)(2,1)}, bf16[2048,512]{1,0:T(8,128)(2,1)}, bf16[512,2048]{1,0:T(8,128)(2,1)}, bf16[512,2048]{1,0:T(8,128)(2,1)}, bf16[51...) custom-call(bf16[512,512]{1,0:T(8,128)(2,1)} %get-tuple-element.54.attn_hbm.attn_ref.refs_4_, ...), custom_call_target="tpu_custom_call" | custom-call | tf_op jit(solution)/shard_map/middle/pallas_call | solution.py:1067
  164.5 97.6 %mlp_back.1 = (bf16[512,2048]{1,0:T(8,128)(2,1)}, bf16[512,2048]{1,0:T(8,128)(2,1)}, bf16[512,2048]{1,0:T(8,128)(2,1)}, f32[1,2048]{1,0:T(1,128)}, f32[512,1]{1,...) custom-call(bf16[512,2048]{1,0:T(8,128)(2,1)} %get-tuple-element.57.down_hbm.refs_4_, bf16[512,2048]{1,0:T(8,128)(2,1)} %bitcast.15, ...), custom_call_target="tpu_custom_call" | custom-call | tf_op jit(solution)/shard_map/mlp_back/pallas_call | solution.py:1067
  262.1 52.4 %attention_back.1 = (bf16[512,1536]{1,0:T(8,128)(2,1)}, bf16[2048,512]{1,0:T(8,128)(2,1)}, f32[1,2048]{1,0:T(1,128)}, f32[1,512]{1,0:T(1,128)}, f32[1,512]{1,0:T(1,128)}) custom-call(bf16[512,2048]{1,0:T(8,128)(2,1)} %get-tuple-element.66.back_ref.refs_1_, bf16[512,2048]{1,0:T(8,128)(2,1)} %bitcast.16, bf16[512,2048]{1,0:T(8,128)(2,1)} %get-tuple-element.55.refs_1_.proj_ref, ...), custom_call_target="tpu_custom_call" | custom-call | tf_op jit(solution)/shard_map/attention_back/pallas_call | solution.py:490
  314.5 0.0 copy-start.1
  314.5 0.0 copy-start.2
  314.5 0.0 copy-start.3
  314.6 0.0 copy-start.4
  314.6 8.4 %block_out.1 = (f32[512,2048]{1,0:T(8,128)}, f32[2048,256]{1,0:T(8,128)}, f32[256,2048]{1,0:T(8,128)}) custom-call(bf16[512,2048]{1,0:T(8,128)(2,1)} %bitcast.20, bf16[512,2048]{1,0:T(8,128)(2,1)} %get-tuple-element.55.refs_1_.proj_ref, f32[512,1]{1,0:T(8,128)} %get-tuple-element.56.refs_2_, f32[1,2048]{1,0:T(1,128)} %bitcast.24, ...), custom_call_target="tpu_custom_call" | custom-call | tf_op jit(solution)/shard_map/block_out/pallas_call | solution.py:1437
  322.9 0.0 copy-done.1
  322.9 0.0 copy-done.2
  323.0 0.0 copy-done.3
  323.0 0.0 copy-done.4
  323.0 0.6 pad_maximum_fusion
  323.6 88.6 %last_sums.1 = (bf16[512,2048]{1,0:T(8,128)(2,1)}, f32[256,2048]{1,0:T(8,128)}, f32[256,1536]{1,0:T(8,128)}, f32[512,256]{1,0:T(8,128)}, f32[40,128]{1,0:T(8,128)}) custom-call(bf16[512,1536]{1,0:T(8,128)(2,1)} %get-tuple-element.74.dqkv_ref, bf16[2048,512]{1,0:T(8,128)(2,1)} %wq_ref.1, bf16[2048,512]{1,0:T(8,128)(2,1)} %wk_ref.1, bf16[2048,512]{1,0:T(8,128)(2,1)} %wv_ref.1, ...), custom_call_target="tpu_custom_call" | custom-call | tf_op jit(solution)/shard_map/last_sums/pallas_call | solution.py:1067
  412.2 0.0 copy-start
  412.2 7.4 %input_grad.1 = (f32[512,2048]{1,0:T(8,128)}, f32[256,2048]{1,0:T(8,128)}, f32[512,256]{1,0:T(8,128)}, f32[256,512]{1,0:T(8,128)}, f32[256,512]{1,0:T(8,128)}, /*index=5*/f32[256,512]{1,0:T(8,128)}) custom-call(bf16[512,2048]{1,0:T(8,128)(2,1)} %bitcast.17, bf16[512,2048]{1,0:T(8,128)(2,1)} %get-tuple-element.66.back_ref.refs_1_, ...), custom_call_target="tpu_custom_call" | custom-call | tf_op jit(solution)/shard_map/input_grad/pallas_call | solution.py:1437
  419.6 0.0 copy-done
  419.7 0.6 constant_dynamic-slice_fusion
  420.2 0.7 constant_dynamic-slice_fusion.1
  (6 shorter events, 0.0 us)
Async XLA Ops:
  314.5 8.4 %copy-start.1 = (f32[1,2048]{1,0:T(1,128)S(1)}, f32[1,2048]{1,0:T(1,128)}, u32[]{:S(2)}) copy-start(f32[1,2048]{1,0:T(1,128)} %get-tuple-element.79) | copy-start | bytes 24580
  314.5 8.4 %copy-start.2 = (f32[1,2048]{1,0:T(1,128)S(1)}, f32[1,2048]{1,0:T(1,128)}, u32[]{:S(2)}) copy-start(f32[1,2048]{1,0:T(1,128)} %get-tuple-element.78) | copy-start | bytes 24580
  314.5 8.4 %copy-start.3 = (f32[1,512]{1,0:T(1,128)S(1)}, f32[1,512]{1,0:T(1,128)}, u32[]{:S(2)}) copy-start(f32[1,512]{1,0:T(1,128)} %get-tuple-element.80) | copy-start | bytes 6148
  314.6 8.4 %copy-start.4 = (f32[1,512]{1,0:T(1,128)S(1)}, f32[1,512]{1,0:T(1,128)}, u32[]{:S(2)}) copy-start(f32[1,512]{1,0:T(1,128)} %get-tuple-element.81) | copy-start | bytes 6148
  412.2 7.4 %copy-start = (f32[40,128]{1,0:T(8,128)S(1)}, f32[40,128]{1,0:T(8,128)}, u32[]{:S(2)}) copy-start(f32[40,128]{1,0:T(8,128)} %get-tuple-element.90) | copy-start | bytes 61444

commit v10 on v9

--- a/solution.py
+++ b/solution.py
@@ -654,7 +654,8 @@
 
         def one_block(h, hs, x, owner, write):
             start = (x * 2 + owner) * rows
-            for part in range(rows // sub):
+
+            def one_part(part, carry):
                 ks = pl.ds(pl.multiple_of(start + part * sub, sub), sub)
                 key, value = k_ref[ks, hs], v_ref[ks, hs]
                 query, dhead = q_ref[:, hs], dout[:, hs]
@@ -668,11 +669,14 @@
                 low = (dscore - high.astype(f32)).astype(bf16)
                 dqs[:, hs] += dot_tn(high, key) + dot_tn(low, key)
                 write(
-                    x, slice(part * sub, (part + 1) * sub),
+                    x, pl.ds(pl.multiple_of(part * sub, sub), sub),
                     jnp.dot(high, query, preferred_element_type=f32)
                     + jnp.dot(low, query, preferred_element_type=f32),
                     jnp.dot(share.astype(bf16), dhead, preferred_element_type=f32),
                 )
+                return carry
+
+            lax.fori_loop(0, rows // sub, one_part, 0)
 
         def one_head(h):
             hs = pl.ds(pl.multiple_of(h * head_dim, head_dim), head_dim)
@@ -1096,22 +1100,38 @@
     ):
         line.bind(rest[:n_line])
         start = load_list([(attn_hbm, attn_v), (wo_hbm, wo), (tok_hbm, tok)], first)
-        pairs = []
+
+        def load(src, dst, j, size, spot):
+            cols = pl.ds(pl.multiple_of(j * size, size), size)
+            return pltpu.make_async_copy(src.at[:, cols], dst.at[j], loads.at[spot])
+
+        def gate_load(j):
+            return load(wg_hbm, wg, j, cut, 2 * j)
+
+        def up_load(j):
+            return load(wu_hbm, wu, j, cut, 2 * j + 1)
+
+        def down_load(j):
+            return load(wd_hbm, wd, j, part, 2 * n_cut + j)
+
         for j in range(n_cut):
-            cols = pl.ds(j * cut, cut)
-            pairs += [(wg_hbm.at[:, cols], wg.at[j]), (wu_hbm.at[:, cols], wu.at[j])]
+            gate_load(j).start()
+            up_load(j).start()
         for j in range(n_tp):
-            cols = pl.ds(j * part, part)
-            pairs += [(wd_hbm.at[:, cols], wd.at[j])]
-        weights = load_list(pairs, loads)
+            down_load(j).start()
         bar = pltpu.get_barrier_semaphore()
         peers = line.greet(bar)
         for copy in start:
             copy.wait()
-        for j in range(n_tp):
+
+        def project(j, carry):
+            cols = pl.ds(pl.multiple_of(j * part, part), part)
             line.own[j, :rows] = jnp.dot(
-                attn_v[...], wo[:, j * part : (j + 1) * part], preferred_element_type=f32
+                attn_v[...], wo[:, cols], preferred_element_type=f32
             ).astype(bf16)
+            return carry
+
+        lax.fori_loop(0, n_tp, project, 0)
         pl.semaphore_wait(bar, peers)
 
         def step(t, carry):
@@ -1142,30 +1162,38 @@
                 return carry
 
             lax.fori_loop(0, half // tile, norm_rows, 0)
-            for j in range(n_cut):
-                cols = slice(j * cut, (j + 1) * cut)
+            per = row_chains // n_cut
+
+            def widen(j, carry):
+                cols = pl.ds(pl.multiple_of(j * cut, cut), cut)
 
                 @pl.when(c == 0)
                 def _():
-                    weights[2 * j].wait()
-                    weights[2 * j + 1].wait()
+                    gate_load(j).wait()
+                    up_load(j).wait()
 
                 g = jnp.dot(hid[sl], wg[j], preferred_element_type=f32)
                 u = jnp.dot(hid[sl], wu[j], preferred_element_type=f32)
                 gate[sl, cols] = g.astype(bf16)
                 up[sl, cols] = u.astype(bf16)
                 inner[sl, cols] = (g * jax.nn.sigmoid(g) * u).astype(bf16)
-                low, high = j * row_chains // n_cut, (j + 1) * row_chains // n_cut
-                line.pieces(((c + 2) * n_tp - 1) * row_chains + low, high - low)
-            for j in range(n_tp):
-
+                line.pieces(((c + 2) * n_tp - 1) * row_chains + j * per, per)
+                return carry
+
+            lax.fori_loop(0, n_cut, widen, 0)
+            line.pieces(((c + 2) * n_tp - 1) * row_chains + n_cut * per, row_chains - n_cut * per)
+
+            def narrow(j, carry):
                 @pl.when(c == 0)
                 def _():
-                    weights[2 * n_cut + j].wait()
+                    down_load(j).wait()
 
                 line.own[j, pl.ds(rows + base, half)] = jnp.dot(
                     inner[sl], wd[j], preferred_element_type=f32
                 ).astype(bf16)
+                return carry
+
+            lax.fori_loop(0, n_tp, narrow, 0)
             return carry
 
         lax.fori_loop(0, 2, row_half, 0)
@@ -1424,7 +1452,7 @@
 
 
 def row_tiles(body, args, outs, name):
-    count = 4
+    count = 8
 
     def spec(shape):
         if shape[0] == 1:

time: 429 us -> 428 us (level); the launches traced: 421 us -> 428 us
  Pallas kernels: 415 us -> 422 us
where the time goes in v10:
time: 428 us
  Pallas kernels  422 us (99%)
    pallas_call x3, Pallas kernels, kernel_call(): pl.pallas_call(body, out_shape=[jax.ShapeDtypeStruct(*out) for out in out...  306 us
    pallas_call x1, Pallas kernels, comm_call(): pl.pallas_call(body, out_shape=outs, in_specs=[pl.BlockSpec(memory_space=...  55.5 us
    pallas_call x1, Pallas kernels, front(): pl.pallas_call(body, out_shape=[block((rows, local), bf16), block((count,...  41.6 us
    pallas_call x2, Pallas kernels, row_tiles(): pl.pallas_call(whole, grid=(count,), out_shape=[jax.ShapeDtypeStruct(shap...  19 us

profile of v10, /device:TPU:0, one launch (start us, length us, event | category | flops | bytes accessed | tf_op | source)
XLA Modules:
  0.0 427.8 jit_solution(9505175186425083883)
XLA Ops:
  0.7 0.7 select_reduce_fusion
  1.5 0.6 fusion.prow_ref
  2.0 1.8 negate_select_fusion
  3.9 41.6 %front.1 = (bf16[512,512]{1,0:T(8,128)(2,1)}, bf16[2048,512]{1,0:T(8,128)(2,1)}, bf16[2048,512]{1,0:T(8,128)(2,1)}, f32[512,512]{1,0:T(8,128)}, f32[512,512]{1,0...) custom-call(bf16[512,2048]{1,0:T(8,128)(2,1)} %bitcast.18, ...), custom_call_target="tpu_custom_call" | custom-call | tf_op jit(solution)/shard_map/front/pallas_call | solution.py:1027
  45.4 119.6 %middle.1 = (bf16[512,2048]{1,0:T(8,128)(2,1)}, bf16[2048,512]{1,0:T(8,128)(2,1)}, bf16[512,2048]{1,0:T(8,128)(2,1)}, bf16[512,2048]{1,0:T(8,128)(2,1)}, bf16[51...) custom-call(bf16[512,512]{1,0:T(8,128)(2,1)} %get-tuple-element.54.attn_hbm.attn_ref.refs_4_, ...), custom_call_target="tpu_custom_call" | custom-call | tf_op jit(solution)/shard_map/middle/pallas_call | solution.py:1071
  165.1 97.6 %mlp_back.1 = (bf16[512,2048]{1,0:T(8,128)(2,1)}, bf16[512,2048]{1,0:T(8,128)(2,1)}, bf16[512,2048]{1,0:T(8,128)(2,1)}, f32[1,2048]{1,0:T(1,128)}, f32[512,1]{1,...) custom-call(bf16[512,2048]{1,0:T(8,128)(2,1)} %get-tuple-element.57.down_hbm.refs_4_, bf16[512,2048]{1,0:T(8,128)(2,1)} %bitcast.15, ...), custom_call_target="tpu_custom_call" | custom-call | tf_op jit(solution)/shard_map/mlp_back/pallas_call | solution.py:1071
  262.7 55.5 %attention_back.1 = (bf16[512,1536]{1,0:T(8,128)(2,1)}, bf16[2048,512]{1,0:T(8,128)(2,1)}, f32[1,2048]{1,0:T(1,128)}, f32[1,512]{1,0:T(1,128)}, f32[1,512]{1,0:T(1,128)}) custom-call(bf16[512,2048]{1,0:T(8,128)(2,1)} %get-tuple-element.66.back_ref.refs_1_, bf16[512,2048]{1,0:T(8,128)(2,1)} %bitcast.16, bf16[512,2048]{1,0:T(8,128)(2,1)} %get-tuple-element.55.refs_1_.proj_ref, ...), custom_call_target="tpu_custom_call" | custom-call | tf_op jit(solution)/shard_map/attention_back/pallas_call | solution.py:490
  318.2 0.0 copy-start.1
  318.2 0.0 copy-start.2
  318.2 0.0 copy-start.3
  318.2 0.0 copy-start.4
  318.2 9.8 %block_out.1 = (f32[512,2048]{1,0:T(8,128)}, f32[2048,256]{1,0:T(8,128)}, f32[256,2048]{1,0:T(8,128)}) custom-call(bf16[512,2048]{1,0:T(8,128)(2,1)} %bitcast.20, bf16[512,2048]{1,0:T(8,128)(2,1)} %get-tuple-element.55.refs_1_.proj_ref, f32[512,1]{1,0:T(8,128)} %get-tuple-element.56.refs_2_, f32[1,2048]{1,0:T(1,128)} %bitcast.24, ...), custom_call_target="tpu_custom_call" | custom-call | tf_op jit(solution)/shard_map/block_out/pallas_call | solution.py:1465
  328.1 0.0 copy-done.1
  328.1 0.0 copy-done.2
  328.1 0.0 copy-done.3
  328.1 0.0 copy-done.4
  328.1 0.6 pad_maximum_fusion
  328.7 88.6 %last_sums.1 = (bf16[512,2048]{1,0:T(8,128)(2,1)}, f32[256,2048]{1,0:T(8,128)}, f32[256,1536]{1,0:T(8,128)}, f32[512,256]{1,0:T(8,128)}, f32[40,128]{1,0:T(8,128)}) custom-call(bf16[512,1536]{1,0:T(8,128)(2,1)} %get-tuple-element.74.dqkv_ref, bf16[2048,512]{1,0:T(8,128)(2,1)} %wq_ref.1, bf16[2048,512]{1,0:T(8,128)(2,1)} %wk_ref.1, bf16[2048,512]{1,0:T(8,128)(2,1)} %wv_ref.1, ...), custom_call_target="tpu_custom_call" | custom-call | tf_op jit(solution)/shard_map/last_sums/pallas_call | solution.py:1071
  417.3 0.0 copy-start
  417.3 9.2 %input_grad.1 = (f32[512,2048]{1,0:T(8,128)}, f32[256,2048]{1,0:T(8,128)}, f32[512,256]{1,0:T(8,128)}, f32[256,512]{1,0:T(8,128)}, f32[256,512]{1,0:T(8,128)}, /*index=5*/f32[256,512]{1,0:T(8,128)}) custom-call(bf16[512,2048]{1,0:T(8,128)(2,1)} %bitcast.17, bf16[512,2048]{1,0:T(8,128)(2,1)} %get-tuple-element.66.back_ref.refs_1_, ...), custom_call_target="tpu_custom_call" | custom-call | tf_op jit(solution)/shard_map/input_grad/pallas_call | solution.py:1465
  426.5 0.0 copy-done
  426.6 0.6 constant_dynamic-slice_fusion
  427.1 0.7 constant_dynamic-slice_fusion.1
  (6 shorter events, 0.0 us)
Async XLA Ops:
  318.2 9.9 %copy-start.1 = (f32[1,2048]{1,0:T(1,128)S(1)}, f32[1,2048]{1,0:T(1,128)}, u32[]{:S(2)}) copy-start(f32[1,2048]{1,0:T(1,128)} %get-tuple-element.79) | copy-start | bytes 24580
  318.2 9.9 %copy-start.2 = (f32[1,2048]{1,0:T(1,128)S(1)}, f32[1,2048]{1,0:T(1,128)}, u32[]{:S(2)}) copy-start(f32[1,2048]{1,0:T(1,128)} %get-tuple-element.78) | copy-start | bytes 24580
  318.2 9.9 %copy-start.3 = (f32[1,512]{1,0:T(1,128)S(1)}, f32[1,512]{1,0:T(1,128)}, u32[]{:S(2)}) copy-start(f32[1,512]{1,0:T(1,128)} %get-tuple-element.80) | copy-start | bytes 6148
  318.2 9.9 %copy-start.4 = (f32[1,512]{1,0:T(1,128)S(1)}, f32[1,512]{1,0:T(1,128)}, u32[]{:S(2)}) copy-start(f32[1,512]{1,0:T(1,128)} %get-tuple-element.81) | copy-start | bytes 6148
  417.3 9.2 %copy-start = (f32[40,128]{1,0:T(8,128)S(1)}, f32[40,128]{1,0:T(8,128)}, u32[]{:S(2)}) copy-start(f32[40,128]{1,0:T(8,128)} %get-tuple-element.90) | copy-start | bytes 61444

commit v11 on v10

--- a/solution.py
+++ b/solution.py
@@ -654,8 +654,7 @@
 
         def one_block(h, hs, x, owner, write):
             start = (x * 2 + owner) * rows
-
-            def one_part(part, carry):
+            for part in range(rows // sub):
                 ks = pl.ds(pl.multiple_of(start + part * sub, sub), sub)
                 key, value = k_ref[ks, hs], v_ref[ks, hs]
                 query, dhead = q_ref[:, hs], dout[:, hs]
@@ -669,14 +668,11 @@
                 low = (dscore - high.astype(f32)).astype(bf16)
                 dqs[:, hs] += dot_tn(high, key) + dot_tn(low, key)
                 write(
-                    x, pl.ds(pl.multiple_of(part * sub, sub), sub),
+                    x, slice(part * sub, (part + 1) * sub),
                     jnp.dot(high, query, preferred_element_type=f32)
                     + jnp.dot(low, query, preferred_element_type=f32),
                     jnp.dot(share.astype(bf16), dhead, preferred_element_type=f32),
                 )
-                return carry
-
-            lax.fori_loop(0, rows // sub, one_part, 0)
 
         def one_head(h):
             hs = pl.ds(pl.multiple_of(h * head_dim, head_dim), head_dim)
@@ -1452,7 +1448,7 @@
 
 
 def row_tiles(body, args, outs, name):
-    count = 8
+    count = 4
 
     def spec(shape):
         if shape[0] == 1:

time: 428 us -> 422 us (0.986)
  Pallas kernels: 422 us -> 416 us
where the time goes in v11:
time: 422 us; the launch traced here: 421 us
  Pallas kernels  416 us (99%)
    pallas_call x3, Pallas kernels, kernel_call(): pl.pallas_call(body, out_shape=[jax.ShapeDtypeStruct(*out) for out in out...  306 us
    pallas_call x1, Pallas kernels, comm_call(): pl.pallas_call(body, out_shape=outs, in_specs=[pl.BlockSpec(memory_space=...  52.4 us
    pallas_call x1, Pallas kernels, front(): pl.pallas_call(body, out_shape=[block((rows, local), bf16), block((count,...  41.6 us
    pallas_call x2, Pallas kernels, row_tiles(): pl.pallas_call(whole, grid=(count,), out_shape=[jax.ShapeDtypeStruct(shap...  15.8 us

profile of v11, /device:TPU:0, one launch (start us, length us, event | category | flops | bytes accessed | tf_op | source)
XLA Modules:
  0.0 421.4 jit_solution(8072006344859828263)
XLA Ops:
  0.7 0.7 select_reduce_fusion
  1.5 0.6 fusion.prow_ref
  2.0 1.8 negate_select_fusion
  3.9 41.6 %front.1 = (bf16[512,512]{1,0:T(8,128)(2,1)}, bf16[2048,512]{1,0:T(8,128)(2,1)}, bf16[2048,512]{1,0:T(8,128)(2,1)}, f32[512,512]{1,0:T(8,128)}, f32[512,512]{1,0...) custom-call(bf16[512,2048]{1,0:T(8,128)(2,1)} %bitcast.18, ...), custom_call_target="tpu_custom_call" | custom-call | tf_op jit(solution)/shard_map/front/pallas_call | solution.py:1023
  45.4 119.6 %middle.1 = (bf16[512,2048]{1,0:T(8,128)(2,1)}, bf16[2048,512]{1,0:T(8,128)(2,1)}, bf16[512,2048]{1,0:T(8,128)(2,1)}, bf16[512,2048]{1,0:T(8,128)(2,1)}, bf16[51...) custom-call(bf16[512,512]{1,0:T(8,128)(2,1)} %get-tuple-element.54.attn_hbm.attn_ref.refs_4_, ...), custom_call_target="tpu_custom_call" | custom-call | tf_op jit(solution)/shard_map/middle/pallas_call | solution.py:1067
  165.1 97.6 %mlp_back.1 = (bf16[512,2048]{1,0:T(8,128)(2,1)}, bf16[512,2048]{1,0:T(8,128)(2,1)}, bf16[512,2048]{1,0:T(8,128)(2,1)}, f32[1,2048]{1,0:T(1,128)}, f32[512,1]{1,...) custom-call(bf16[512,2048]{1,0:T(8,128)(2,1)} %get-tuple-element.57.down_hbm.refs_4_, bf16[512,2048]{1,0:T(8,128)(2,1)} %bitcast.15, ...), custom_call_target="tpu_custom_call" | custom-call | tf_op jit(solution)/shard_map/mlp_back/pallas_call | solution.py:1067
  262.7 52.4 %attention_back.1 = (bf16[512,1536]{1,0:T(8,128)(2,1)}, bf16[2048,512]{1,0:T(8,128)(2,1)}, f32[1,2048]{1,0:T(1,128)}, f32[1,512]{1,0:T(1,128)}, f32[1,512]{1,0:T(1,128)}) custom-call(bf16[512,2048]{1,0:T(8,128)(2,1)} %get-tuple-element.66.back_ref.refs_1_, bf16[512,2048]{1,0:T(8,128)(2,1)} %bitcast.16, bf16[512,2048]{1,0:T(8,128)(2,1)} %get-tuple-element.55.refs_1_.proj_ref, ...), custom_call_target="tpu_custom_call" | custom-call | tf_op jit(solution)/shard_map/attention_back/pallas_call | solution.py:490
  315.0 0.0 copy-start.1
  315.0 0.0 copy-start.2
  315.1 0.0 copy-start.3
  315.1 0.0 copy-start.4
  315.1 8.4 %block_out.1 = (f32[512,2048]{1,0:T(8,128)}, f32[2048,256]{1,0:T(8,128)}, f32[256,2048]{1,0:T(8,128)}) custom-call(bf16[512,2048]{1,0:T(8,128)(2,1)} %bitcast.20, bf16[512,2048]{1,0:T(8,128)(2,1)} %get-tuple-element.55.refs_1_.proj_ref, f32[512,1]{1,0:T(8,128)} %get-tuple-element.56.refs_2_, f32[1,2048]{1,0:T(1,128)} %bitcast.24, ...), custom_call_target="tpu_custom_call" | custom-call | tf_op jit(solution)/shard_map/block_out/pallas_call | solution.py:1461
  323.4 0.0 copy-done.1
  323.5 0.0 copy-done.2
  323.5 0.0 copy-done.3
  323.5 0.0 copy-done.4
  323.5 0.6 pad_maximum_fusion
  324.1 88.6 %last_sums.1 = (bf16[512,2048]{1,0:T(8,128)(2,1)}, f32[256,2048]{1,0:T(8,128)}, f32[256,1536]{1,0:T(8,128)}, f32[512,256]{1,0:T(8,128)}, f32[40,128]{1,0:T(8,128)}) custom-call(bf16[512,1536]{1,0:T(8,128)(2,1)} %get-tuple-element.74.dqkv_ref, bf16[2048,512]{1,0:T(8,128)(2,1)} %wq_ref.1, bf16[2048,512]{1,0:T(8,128)(2,1)} %wk_ref.1, bf16[2048,512]{1,0:T(8,128)(2,1)} %wv_ref.1, ...), custom_call_target="tpu_custom_call" | custom-call | tf_op jit(solution)/shard_map/last_sums/pallas_call | solution.py:1067
  412.7 0.0 copy-start
  412.7 7.4 %input_grad.1 = (f32[512,2048]{1,0:T(8,128)}, f32[256,2048]{1,0:T(8,128)}, f32[512,256]{1,0:T(8,128)}, f32[256,512]{1,0:T(8,128)}, f32[256,512]{1,0:T(8,128)}, /*index=5*/f32[256,512]{1,0:T(8,128)}) custom-call(bf16[512,2048]{1,0:T(8,128)(2,1)} %bitcast.17, bf16[512,2048]{1,0:T(8,128)(2,1)} %get-tuple-element.66.back_ref.refs_1_, ...), custom_call_target="tpu_custom_call" | custom-call | tf_op jit(solution)/shard_map/input_grad/pallas_call | solution.py:1461
  420.1 0.0 copy-done
  420.2 0.6 constant_dynamic-slice_fusion
  420.8 0.7 constant_dynamic-slice_fusion.1
  (6 shorter events, 0.0 us)
Async XLA Ops:
  315.0 8.4 %copy-start.1 = (f32[1,2048]{1,0:T(1,128)S(1)}, f32[1,2048]{1,0:T(1,128)}, u32[]{:S(2)}) copy-start(f32[1,2048]{1,0:T(1,128)} %get-tuple-element.79) | copy-start | bytes 24580
  315.0 8.4 %copy-start.2 = (f32[1,2048]{1,0:T(1,128)S(1)}, f32[1,2048]{1,0:T(1,128)}, u32[]{:S(2)}) copy-start(f32[1,2048]{1,0:T(1,128)} %get-tuple-element.78) | copy-start | bytes 24580
  315.1 8.4 %copy-start.3 = (f32[1,512]{1,0:T(1,128)S(1)}, f32[1,512]{1,0:T(1,128)}, u32[]{:S(2)}) copy-start(f32[1,512]{1,0:T(1,128)} %get-tuple-element.80) | copy-start | bytes 6148
  315.1 8.4 %copy-start.4 = (f32[1,512]{1,0:T(1,128)S(1)}, f32[1,512]{1,0:T(1,128)}, u32[]{:S(2)}) copy-start(f32[1,512]{1,0:T(1,128)} %get-tuple-element.81) | copy-start | bytes 6148
  412.7 7.4 %copy-start = (f32[40,128]{1,0:T(8,128)S(1)}, f32[40,128]{1,0:T(8,128)}, u32[]{:S(2)}) copy-start(f32[40,128]{1,0:T(8,128)} %get-tuple-element.90) | copy-start | bytes 61444

commit v12 on v11

--- a/solution.py
+++ b/solution.py
@@ -531,10 +531,11 @@
             {"tp": lax.rem(self.i + d, self.n)},
         )
 
-    def total(self, columns):
+    def total(self, columns, meanwhile=lambda: None):
         self.mine[...] = jnp.transpose(columns)[:8]
         for d in range(1, self.n):
             self.copy(d).start()
+        meanwhile()
         acc = self.mine[...]
         for d in range(1, self.n):
             self.copy(d).wait_recv()
@@ -895,7 +896,10 @@
                 acc_sq = acc_sq + jnp.sum(part * part, axis=1, keepdims=True)
             return acc_sq
 
-        sums = small.total(lane_pair(squares(qn), squares(kn), rows))
+        def transpose_tokens():
+            tokt[...] = jnp.transpose(tok[...])
+
+        sums = small.total(lane_pair(squares(qn), squares(kn), rows), transpose_tokens)
         scales = lax.rsqrt(sums * (1.0 / width) + norm_eps)
         sc_out[...] = scales
 
@@ -958,7 +962,6 @@
         for t in range(3):
             from_mate(t).wait_recv()
         attend(mx, 1 - core, 0, heads)
-        tokt[...] = jnp.transpose(tok[...])
 
         def half_heads(t, carry):
             low, high = t * heads // 2, (t + 1) * heads // 2

time: 422 us -> 422 us (level)
  no operation moved by 1% of the time
where the time goes in v12:
time: 422 us; the launch traced here: 421 us
  Pallas kernels  416 us (99%)
    pallas_call x3, Pallas kernels, kernel_call(): pl.pallas_call(body, out_shape=[jax.ShapeDtypeStruct(*out) for out in out...  306 us
    pallas_call x1, Pallas kernels, comm_call(): pl.pallas_call(body, out_shape=outs, in_specs=[pl.BlockSpec(memory_space=...  52.9 us
    pallas_call x1, Pallas kernels, front(): pl.pallas_call(body, out_shape=[block((rows, local), bf16), block((count,...  41.1 us
    pallas_call x2, Pallas kernels, row_tiles(): pl.pallas_call(whole, grid=(count,), out_shape=[jax.ShapeDtypeStruct(shap...  15.8 us

profile of v12, /device:TPU:0, one launch (start us, length us, event | category | flops | bytes accessed | tf_op | source)
XLA Modules:
  0.0 421.4 jit_solution(6574689723417239712)
XLA Ops:
  0.7 0.7 select_reduce_fusion
  1.5 0.6 fusion.prow_ref
  2.0 1.8 negate_select_fusion
  3.9 41.1 %front.1 = (bf16[512,512]{1,0:T(8,128)(2,1)}, bf16[2048,512]{1,0:T(8,128)(2,1)}, bf16[2048,512]{1,0:T(8,128)(2,1)}, f32[512,512]{1,0:T(8,128)}, f32[512,512]{1,0...) custom-call(bf16[512,2048]{1,0:T(8,128)(2,1)} %bitcast.18, ...), custom_call_target="tpu_custom_call" | custom-call | tf_op jit(solution)/shard_map/front/pallas_call | solution.py:1026
  44.9 119.8 %middle.1 = (bf16[512,2048]{1,0:T(8,128)(2,1)}, bf16[2048,512]{1,0:T(8,128)(2,1)}, bf16[512,2048]{1,0:T(8,128)(2,1)}, bf16[512,2048]{1,0:T(8,128)(2,1)}, bf16[51...) custom-call(bf16[512,512]{1,0:T(8,128)(2,1)} %get-tuple-element.54.attn_hbm.attn_ref.refs_4_, ...), custom_call_target="tpu_custom_call" | custom-call | tf_op jit(solution)/shard_map/middle/pallas_call | solution.py:1070
  164.8 97.3 %mlp_back.1 = (bf16[512,2048]{1,0:T(8,128)(2,1)}, bf16[512,2048]{1,0:T(8,128)(2,1)}, bf16[512,2048]{1,0:T(8,128)(2,1)}, f32[1,2048]{1,0:T(1,128)}, f32[512,1]{1,...) custom-call(bf16[512,2048]{1,0:T(8,128)(2,1)} %get-tuple-element.57.down_hbm.refs_4_, bf16[512,2048]{1,0:T(8,128)(2,1)} %bitcast.15, ...), custom_call_target="tpu_custom_call" | custom-call | tf_op jit(solution)/shard_map/mlp_back/pallas_call | solution.py:1070
  262.1 52.9 %attention_back.1 = (bf16[512,1536]{1,0:T(8,128)(2,1)}, bf16[2048,512]{1,0:T(8,128)(2,1)}, f32[1,2048]{1,0:T(1,128)}, f32[1,512]{1,0:T(1,128)}, f32[1,512]{1,0:T(1,128)}) custom-call(bf16[512,2048]{1,0:T(8,128)(2,1)} %get-tuple-element.66.back_ref.refs_1_, bf16[512,2048]{1,0:T(8,128)(2,1)} %bitcast.16, bf16[512,2048]{1,0:T(8,128)(2,1)} %get-tuple-element.55.refs_1_.proj_ref, ...), custom_call_target="tpu_custom_call" | custom-call | tf_op jit(solution)/shard_map/attention_back/pallas_call | solution.py:490
  315.0 0.0 copy-start.1
  315.0 0.0 copy-start.2
  315.1 0.0 copy-start.3
  315.1 0.0 copy-start.4
  315.1 8.4 %block_out.1 = (f32[512,2048]{1,0:T(8,128)}, f32[2048,256]{1,0:T(8,128)}, f32[256,2048]{1,0:T(8,128)}) custom-call(bf16[512,2048]{1,0:T(8,128)(2,1)} %bitcast.20, bf16[512,2048]{1,0:T(8,128)(2,1)} %get-tuple-element.55.refs_1_.proj_ref, f32[512,1]{1,0:T(8,128)} %get-tuple-element.56.refs_2_, f32[1,2048]{1,0:T(1,128)} %bitcast.24, ...), custom_call_target="tpu_custom_call" | custom-call | tf_op jit(solution)/shard_map/block_out/pallas_call | solution.py:1464
  323.4 0.0 copy-done.1
  323.5 0.0 copy-done.2
  323.5 0.0 copy-done.3
  323.5 0.0 copy-done.4
  323.5 0.6 pad_maximum_fusion
  324.1 88.6 %last_sums.1 = (bf16[512,2048]{1,0:T(8,128)(2,1)}, f32[256,2048]{1,0:T(8,128)}, f32[256,1536]{1,0:T(8,128)}, f32[512,256]{1,0:T(8,128)}, f32[40,128]{1,0:T(8,128)}) custom-call(bf16[512,1536]{1,0:T(8,128)(2,1)} %get-tuple-element.74.dqkv_ref, bf16[2048,512]{1,0:T(8,128)(2,1)} %wq_ref.1, bf16[2048,512]{1,0:T(8,128)(2,1)} %wk_ref.1, bf16[2048,512]{1,0:T(8,128)(2,1)} %wv_ref.1, ...), custom_call_target="tpu_custom_call" | custom-call | tf_op jit(solution)/shard_map/last_sums/pallas_call | solution.py:1070
  412.7 0.0 copy-start
  412.7 7.4 %input_grad.1 = (f32[512,2048]{1,0:T(8,128)}, f32[256,2048]{1,0:T(8,128)}, f32[512,256]{1,0:T(8,128)}, f32[256,512]{1,0:T(8,128)}, f32[256,512]{1,0:T(8,128)}, /*index=5*/f32[256,512]{1,0:T(8,128)}) custom-call(bf16[512,2048]{1,0:T(8,128)(2,1)} %bitcast.17, bf16[512,2048]{1,0:T(8,128)(2,1)} %get-tuple-element.66.back_ref.refs_1_, ...), custom_call_target="tpu_custom_call" | custom-call | tf_op jit(solution)/shard_map/input_grad/pallas_call | solution.py:1464
  420.1 0.0 copy-done
  420.2 0.6 constant_dynamic-slice_fusion
  420.7 0.7 constant_dynamic-slice_fusion.1
  (6 shorter events, 0.0 us)
Async XLA Ops:
  315.0 8.4 %copy-start.1 = (f32[1,2048]{1,0:T(1,128)S(1)}, f32[1,2048]{1,0:T(1,128)}, u32[]{:S(2)}) copy-start(f32[1,2048]{1,0:T(1,128)} %get-tuple-element.79) | copy-start | bytes 24580
  315.0 8.4 %copy-start.2 = (f32[1,2048]{1,0:T(1,128)S(1)}, f32[1,2048]{1,0:T(1,128)}, u32[]{:S(2)}) copy-start(f32[1,2048]{1,0:T(1,128)} %get-tuple-element.78) | copy-start | bytes 24580
  315.1 8.4 %copy-start.3 = (f32[1,512]{1,0:T(1,128)S(1)}, f32[1,512]{1,0:T(1,128)}, u32[]{:S(2)}) copy-start(f32[1,512]{1,0:T(1,128)} %get-tuple-element.80) | copy-start | bytes 6148
  315.1 8.4 %copy-start.4 = (f32[1,512]{1,0:T(1,128)S(1)}, f32[1,512]{1,0:T(1,128)}, u32[]{:S(2)}) copy-start(f32[1,512]{1,0:T(1,128)} %get-tuple-element.81) | copy-start | bytes 6148
  412.7 7.4 %copy-start = (f32[40,128]{1,0:T(8,128)S(1)}, f32[40,128]{1,0:T(8,128)}, u32[]{:S(2)}) copy-start(f32[40,128]{1,0:T(8,128)} %get-tuple-element.90) | copy-start | bytes 61444
